TPU v7x, 768 devices: a whole 4x8x12 slice. The times are simulated.
768 devices in a mesh: gx: 48 (over x_hi, z, core), gy: 16 (over x_lo, y).
Axes of the slice: x: 4 (x_hi: 2, x_lo: 2; x = x_hi * 2 + x_lo), y: 8, z: 12, core: 2. Of those that a mesh axis runs over, the one named last changes fastest.
Arguments:
- velocity: float32 [3, 768, 256, 128], P(None, 'gx', 'gy'), may hold values from -6 to 6
- stresses: float32 [6, 768, 256, 128], P(None, 'gx', 'gy'), may hold values from -6 to 6
- buoyancy: float32 [768, 256, 128], P('gx', 'gy'), may hold values from 0.3 to 0.6
- lame_first: float32 [768, 256, 128], P('gx', 'gy'), may hold values from 0.05 to 0.15
- rigidity: float32 [768, 256, 128], P('gx', 'gy'), may hold values from 0.04 to 0.12
- histories: bfloat16 [196608, 512], P(('gx', 'gy')), may hold values from -6 to 6
- mechanism: bfloat16 [196608, 6], P(('gx', 'gy')), may hold values from -6 to 6
- resample: bfloat16 [512, 3], replicated, may hold values from -0.25 to 0.25
- owners: int32 [196608, 1], P(('gx', 'gy')), may hold values from 0 to 15; in each aligned block of 256 rows (0 to 255, 256 to 511, ...) at most 64 rows name the same one
- cell_offsets: int32 [196608], P(('gx', 'gy')), may hold values from 0 to 32767
Outputs:
- velocity_out: float32 [3, 768, 256, 128], P(None, 'gx', 'gy')
- stresses_out: float32 [6, 768, 256, 128], P(None, 'gx', 'gy')
Inputs may be any that keep to these rules, and one draw needn't show every extreme that they name: `owners`: among the 256 rows of one device at most 64 name the same owner, a bound that some block reaches of them. `cell_offsets`: cell index x * 16 * 128 + y * 128 + z within the enclosing block.
All inputs are finite; a program needn't handle non-finite values.
Results may differ from a plain program's by a relative error of at most 0.00052.
Values may be sent and summed in bfloat16 or wider, within the bound.
No kernel may reach another device: no remote copies, remote signals or barrier semaphores. Data moves between devices by JAX's collectives and lax.ppermute only.
A program may use at most 32 MiB of HBM per device.

v0:
```python
import jax
import jax.numpy as jnp
from jax import lax
from jax.sharding import PartitionSpec as P

INNER_WEIGHT = 9.0 / 8.0
OUTER_WEIGHT = -1.0 / 24.0


def extended(cells, sides, width):
    for axis, dim in sides:
        count = lax.axis_size(axis)
        ends = count - 1
        head = lax.slice_in_dim(cells, 0, width, axis=dim)
        tail = lax.slice_in_dim(cells, cells.shape[dim] - width, cells.shape[dim], axis=dim)
        cells = jnp.concatenate(
            [
                lax.ppermute(tail, axis, [(i, (i + 1) % count) for i in range(ends)]),
                cells,
                lax.ppermute(head, axis, [((i + 1) % count, i) for i in range(ends)]),
            ],
            axis=dim,
        )
    return cells


def differ(values, dimension, forward):
    if dimension == 2:
        values = jnp.pad(values, ((0, 0), (0, 0), (2, 2)))
    extent = values.shape[dimension] - 4

    def window(start_at):
        return lax.slice_in_dim(values, start_at, start_at + extent, axis=dimension)

    if forward:
        result = INNER_WEIGHT * (window(3) - window(2)) + OUTER_WEIGHT * (window(4) - window(1))
    else:
        result = INNER_WEIGHT * (window(2) - window(1)) + OUTER_WEIGHT * (window(3) - window(0))
    for second in (0, 1):
        if second != dimension:
            result = lax.slice_in_dim(result, 2, result.shape[second] - 2, axis=second)
    return result


def shrink(arrays, margin):
    return arrays[..., margin:-margin, margin:-margin, :]


def advance_velocity(velocity, stresses, buoyancy):
    forces = jnp.stack(
        [
            differ(stresses[0], 0, True)
            + differ(stresses[3], 1, False)
            + differ(stresses[4], 2, False),
            differ(stresses[3], 0, False)
            + differ(stresses[1], 1, True)
            + differ(stresses[5], 2, False),
            differ(stresses[4], 0, False)
            + differ(stresses[5], 1, False)
            + differ(stresses[2], 2, True),
        ]
    )
    return velocity + buoyancy * forces


def advance_stress(stresses, velocity, lame_first, rigidity):
    stretch_one = differ(velocity[0], 0, False)
    stretch_two = differ(velocity[1], 1, False)
    stretch_three = differ(velocity[2], 2, False)
    change = stretch_one + stretch_two + stretch_three
    rates = jnp.stack(
        [
            lame_first * change + 2.0 * rigidity * stretch_one,
            lame_first * change + 2.0 * rigidity * stretch_two,
            lame_first * change + 2.0 * rigidity * stretch_three,
            rigidity * (differ(velocity[0], 1, True) + differ(velocity[1], 0, True)),
            rigidity * (differ(velocity[0], 2, True) + differ(velocity[2], 0, True)),
            rigidity * (differ(velocity[1], 2, True) + differ(velocity[2], 1, True)),
        ]
    )
    return stresses + rates


def local(
    velocity,
    stresses,
    buoyancy,
    lame_first,
    rigidity,
    histories,
    mechanism,
    resample,
    owners,
    cell_offsets,
):
    groups = lax.axis_size("gy")
    src_rows = histories.shape[0]
    capacity = src_rows // 4
    across = velocity.shape[1]
    normal = velocity.shape[2]
    levels = velocity.shape[3]
    steps_count = resample.shape[1]
    owner_column = owners[:, 0]
    targets = jnp.arange(groups, dtype=jnp.int32)
    hits = (owner_column[:, None] == targets[None, :]).astype(jnp.int32)
    earlier = jnp.cumsum(hits, axis=0) - hits
    rank_within = jnp.sum(earlier * hits, axis=1)
    slots = owner_column * capacity + rank_within
    cell_buffer = (
        jnp.zeros((groups * capacity,), jnp.int32)
        .at[slots]
        .set(cell_offsets)
        .reshape(groups, capacity)
    )
    arrived_cells = lax.all_to_all(cell_buffer, "gy", split_axis=0, concat_axis=0, tiled=True)
    amplitude = jnp.dot(histories, resample, preferred_element_type=jnp.float32)
    local_terms = (mechanism.astype(jnp.float32)[:, :, None] * amplitude[:, None, :]).astype(
        jnp.bfloat16
    )
    local_terms = local_terms.reshape(src_rows, -1)
    term_buffer = (
        jnp.zeros((groups * capacity, local_terms.shape[1]), jnp.bfloat16)
        .at[slots]
        .set(local_terms)
    )
    arrived = lax.all_to_all(
        term_buffer.reshape(groups, capacity, -1), "gy", split_axis=0, concat_axis=0, tiled=True
    )
    slot_count = groups * capacity
    flat_terms = arrived.reshape(slot_count, 6, steps_count)
    flat_cells = arrived_cells.reshape(slot_count)
    plane = flat_cells // levels
    height = flat_cells % levels
    pick_plane = (plane[:, None] == jnp.arange(across * normal, dtype=jnp.int32)[None, :]).astype(
        jnp.bfloat16
    )
    pick_level = (height[:, None] == jnp.arange(levels, dtype=jnp.int32)[None, :]).astype(
        jnp.bfloat16
    )
    spread = (flat_terms[:, :, :, None] * pick_level[:, None, None, :]).reshape(slot_count, -1)
    placed = jnp.einsum("rp,rk->pk", pick_plane, spread, preferred_element_type=jnp.float32)
    placed = placed.reshape(across, normal, 6, steps_count, levels).transpose(3, 2, 0, 1, 4)
    wide_buoyancy = shrink(extended(buoyancy, (("gx", 0), ("gy", 1)), 4), 2)
    global_x = lax.axis_index("gx") * across + jnp.arange(across + 4, dtype=jnp.int32) - 2
    global_y = lax.axis_index("gy") * normal + jnp.arange(normal + 4, dtype=jnp.int32) - 2
    inside_x = ((global_x >= 0) & (global_x < across * lax.axis_size("gx"))).astype(jnp.float32)
    inside_y = ((global_y >= 0) & (global_y < normal * groups)).astype(jnp.float32)
    inside = inside_x[:, None, None] * inside_y[None, :, None]
    for step_index in range(steps_count):
        state = extended(jnp.concatenate([velocity, stresses], axis=0), (("gx", 1), ("gy", 2)), 4)
        moved = advance_velocity(shrink(state[:3], 2), state[3:], wide_buoyancy) * inside
        stresses = advance_stress(stresses, moved, lame_first, rigidity)
        velocity = shrink(moved, 2)
        stresses = stresses + placed[step_index]
    return (velocity, stresses)


def solution(mesh):
    in_specs = (
        P(None, "gx", "gy", None),
        P(None, "gx", "gy", None),
        P("gx", "gy", None),
        P("gx", "gy", None),
        P("gx", "gy", None),
        P(("gx", "gy"), None),
        P(("gx", "gy"), None),
        P(),
        P(("gx", "gy"), None),
        P(("gx", "gy")),
    )
    out_specs = (P(None, "gx", "gy", None), P(None, "gx", "gy", None))
    return jax.shard_map(local, mesh=mesh, in_specs=in_specs, out_specs=out_specs, check_vma=False)
```

profile of v0, /device:TPU:6, one launch (start us, length us, event | category | flops | bytes accessed | tf_op | source)
XLA Modules:
  0.0 148.0 jit_solution(7686043967872172244)
XLA Ops:
  3.0 1.9 %collective-permute-start = (f32[9,4,16,128]{3,2,1,0:T(8,128)S(1)}, f32[9,4,16,128]{3,2,1,0:T(8,128)S(1)}, u32[]{:S(2)}, u32[]{:S(2)}) collective-permute-start(f32[9,4,16,128]{3,2,1,0:T(8,128)S(1)} %get-tuple-element.58), channel_id=1, source_target_pairs={{0,16},{16,32},{32,48},{48,64},{64,80},{80,96},{96,112},{112,128},... | collective-permute-start | bytes 884744 | tf_op jit(solution)/shard_map/ppermute | solution.py:18
  4.9 14.9 %collective-permute-start.1 = (f32[9,4,16,128]{3,2,1,0:T(8,128)S(1)}, f32[9,4,16,128]{3,2,1,0:T(8,128)S(1)}, u32[]{:S(2)}, u32[]{:S(2)}) collective-permute-start(f32[9,4,16,128]{3,2,1,0:T(8,128)S(1)} %get-tuple-element.59), channel_id=1, source_target_pairs={{16,0},{32,16},{48,32},{64,48},{80,64},{96,80},{112,96},{128,112},... | collective-permute-start | bytes 884744 | tf_op jit(solution)/shard_map/ppermute | solution.py:20
  19.8 1.9 %collective-permute-start.4 = (f32[4,16,128]{2,1,0:T(8,128)S(1)}, f32[4,16,128]{2,1,0:T(8,128)S(1)}, u32[]{:S(2)}, u32[]{:S(2)}) collective-permute-start(f32[4,16,128]{2,1,0:T(8,128)S(1)} %get-tuple-element.207), channel_id=1, source_target_pairs={{0,16},{16,32},{32,48},{48,64},{64,80},{80,96},{96,112},{112,128},... | collective-permute-start | bytes 98312 | tf_op jit(solution)/shard_map/ppermute | solution.py:18
  21.8 7.3 %collective-permute-start.5 = (f32[4,16,128]{2,1,0:T(8,128)S(1)}, f32[4,16,128]{2,1,0:T(8,128)S(1)}, u32[]{:S(2)}, u32[]{:S(2)}) collective-permute-start(f32[4,16,128]{2,1,0:T(8,128)S(1)} %get-tuple-element.206), channel_id=1, source_target_pairs={{16,0},{32,16},{48,32},{64,48},{80,64},{96,80},{112,96},{128,112},... | collective-permute-start | bytes 98312 | tf_op jit(solution)/shard_map/ppermute | solution.py:20
  32.2 8.6 %all-to-all-start = ((s32[16,1,64]{2,1,0:T(1,128)}), s32[16,1,64]{2,1,0:T(1,128)S(1)}, u32[]{:S(2)}, u32[]{:S(2)}) async-start(s32[16,1,64]{2,1,0:T(1,128)} %all_to_all.9), calls=%async_computation | async-start | bytes 16384 | tf_op jit(solution)/shard_map/all_to_all | solution.py:115
  43.5 4.4 %all-to-all-done = s32[16,1,64]{2,1,0:T(1,128)S(1)} async-done(((s32[16,1,64]{2,1,0:T(1,128)}), s32[16,1,64]{2,1,0:T(1,128)S(1)}, u32[]{:S(2)}, u32[]{:S(2)}) %all-to-all-start) | async-done | bytes 4128 | tf_op jit(solution)/shard_map/all_to_all | solution.py:115
  47.9 4.8 %all-to-all-start.1 = ((bf16[16,2,576]{2,1,0:T(2,128)(2,1)}), bf16[16,2,576]{2,1,0:T(2,128)(2,1)S(1)}, u32[]{:S(2)}, u32[]{:S(2)}) async-start(bf16[16,2,576]{2,1,0:T(2,128)(2,1)} %reshape.423), calls=%async_computation.1 | async-start | bytes 81920 | tf_op jit(solution)/shard_map/all_to_all | solution.py:126
  54.1 3.4 %collective-permute-start.6 = (f32[24,4,128]{2,1,0:T(4,128)S(1)}, f32[24,4,128]{2,1,0:T(4,128)S(1)}, u32[]{:S(2)}, u32[]{:S(2)}) collective-permute-start(f32[24,4,128]{2,1,0:T(4,128)S(1)} %get-tuple-element.204), channel_id=1, source_target_pairs={{0,1},{1,2},{2,3},{3,4},{4,5},{5,6},{6,7},{7,8},{8,9},{9,10},{10,1... | collective-permute-start | bytes 147464 | tf_op jit(solution)/shard_map/ppermute | solution.py:18
  57.5 4.6 %collective-permute-start.7 = (f32[24,4,128]{2,1,0:T(4,128)S(1)}, f32[24,4,128]{2,1,0:T(4,128)S(1)}, u32[]{:S(2)}, u32[]{:S(2)}) collective-permute-start(f32[24,4,128]{2,1,0:T(4,128)S(1)} %get-tuple-element.205), channel_id=1, source_target_pairs={{1,0},{2,1},{3,2},{4,3},{5,4},{6,5},{7,6},{8,7},{9,8},{10,9},{11,1... | collective-permute-start | bytes 147464 | tf_op jit(solution)/shard_map/ppermute | solution.py:20
  62.5 1.9 %collective-permute-start.2 = (f32[9,24,4,128]{3,2,1,0:T(4,128)S(1)}, f32[9,24,4,128]{3,2,1,0:T(4,128)S(1)}, u32[]{:S(2)}, u32[]{:S(2)}) collective-permute-start(f32[9,24,4,128]{3,2,1,0:T(4,128)S(1)} %get-tuple-element.52), channel_id=1, source_target_pairs={{0,1},{1,2},{2,3},{3,4},{4,5},{5,6},{6,7},{7,8},{8,9},{9,10},{10,1... | collective-permute-start | bytes 1327112 | tf_op jit(solution)/shard_map/ppermute | solution.py:18
  64.5 6.0 %collective-permute-start.3 = (f32[9,24,4,128]{3,2,1,0:T(4,128)S(1)}, f32[9,24,4,128]{3,2,1,0:T(4,128)S(1)}, u32[]{:S(2)}, u32[]{:S(2)}) collective-permute-start(f32[9,24,4,128]{3,2,1,0:T(4,128)S(1)} %get-tuple-element.53), channel_id=1, source_target_pairs={{1,0},{2,1},{3,2},{4,3},{5,4},{6,5},{7,6},{8,7},{9,8},{10,9},{11,1... | collective-permute-start | bytes 1327112 | tf_op jit(solution)/shard_map/ppermute | solution.py:20
  72.2 2.7 %collective-permute-done.2 = f32[9,24,4,128]{3,2,1,0:T(4,128)S(1)} collective-permute-done((f32[9,24,4,128]{3,2,1,0:T(4,128)S(1)}, f32[9,24,4,128]{3,2,1,0:T(4,128)S(1)}, u32[]{:S(2)}, u32[]{:S(2)}) %collective-permute-start.2) | collective-permute-done | bytes 442400 | tf_op jit(solution)/shard_map/ppermute | solution.py:18
  81.7 1.9 %collective-permute-start.8 = (f32[9,4,16,128]{3,2,1,0:T(8,128)S(1)}, f32[9,4,16,128]{3,2,1,0:T(8,128)S(1)}, u32[]{:S(2)}, u32[]{:S(2)}) collective-permute-start(f32[9,4,16,128]{3,2,1,0:T(8,128)S(1)} %get-tuple-element.56), channel_id=1, source_target_pairs={{0,16},{16,32},{32,48},{48,64},{64,80},{80,96},{96,112},{112,128},... | collective-permute-start | bytes 884744 | tf_op jit(solution)/shard_map/ppermute | solution.py:18
  83.6 7.3 %collective-permute-start.9 = (f32[9,4,16,128]{3,2,1,0:T(8,128)S(1)}, f32[9,4,16,128]{3,2,1,0:T(8,128)S(1)}, u32[]{:S(2)}, u32[]{:S(2)}) collective-permute-start(f32[9,4,16,128]{3,2,1,0:T(8,128)S(1)} %get-tuple-element.57), channel_id=1, source_target_pairs={{16,0},{32,16},{48,32},{64,48},{80,64},{96,80},{112,96},{128,112},... | collective-permute-start | bytes 884744 | tf_op jit(solution)/shard_map/ppermute | solution.py:20
  90.9 2.5 %collective-permute-done.8 = f32[9,4,16,128]{3,2,1,0:T(8,128)S(1)} collective-permute-done((f32[9,4,16,128]{3,2,1,0:T(8,128)S(1)}, f32[9,4,16,128]{3,2,1,0:T(8,128)S(1)}, u32[]{:S(2)}, u32[]{:S(2)}) %collective-permute-start.8) | collective-permute-done | bytes 294944 | tf_op jit(solution)/shard_map/ppermute | solution.py:18
  95.3 1.9 %collective-permute-start.10 = (f32[9,24,4,128]{3,2,1,0:T(4,128)S(1)}, f32[9,24,4,128]{3,2,1,0:T(4,128)S(1)}, u32[]{:S(2)}, u32[]{:S(2)}) collective-permute-start(f32[9,24,4,128]{3,2,1,0:T(4,128)S(1)} %get-tuple-element.50), channel_id=1, source_target_pairs={{0,1},{1,2},{2,3},{3,4},{4,5},{5,6},{6,7},{7,8},{8,9},{9,10},{10,1... | collective-permute-start | bytes 1327112 | tf_op jit(solution)/shard_map/ppermute | solution.py:18
  97.2 6.7 %collective-permute-start.11 = (f32[9,24,4,128]{3,2,1,0:T(4,128)S(1)}, f32[9,24,4,128]{3,2,1,0:T(4,128)S(1)}, u32[]{:S(2)}, u32[]{:S(2)}) collective-permute-start(f32[9,24,4,128]{3,2,1,0:T(4,128)S(1)} %get-tuple-element.51), channel_id=1, source_target_pairs={{1,0},{2,1},{3,2},{4,3},{5,4},{6,5},{7,6},{8,7},{9,8},{10,9},{11,1... | collective-permute-start | bytes 1327112 | tf_op jit(solution)/shard_map/ppermute | solution.py:20
  103.9 4.2 %collective-permute-done.10 = f32[9,24,4,128]{3,2,1,0:T(4,128)S(1)} collective-permute-done((f32[9,24,4,128]{3,2,1,0:T(4,128)S(1)}, f32[9,24,4,128]{3,2,1,0:T(4,128)S(1)}, u32[]{:S(2)}, u32[]{:S(2)}) %collective-permute-start.10) | collective-permute-done | bytes 442400 | tf_op jit(solution)/shard_map/ppermute | solution.py:18
  114.0 1.9 %collective-permute-start.12 = (f32[9,4,16,128]{3,2,1,0:T(8,128)S(1)}, f32[9,4,16,128]{3,2,1,0:T(8,128)S(1)}, u32[]{:S(2)}, u32[]{:S(2)}) collective-permute-start(f32[9,4,16,128]{3,2,1,0:T(8,128)S(1)} %get-tuple-element.54), channel_id=1, source_target_pairs={{0,16},{16,32},{32,48},{48,64},{64,80},{80,96},{96,112},{112,128},... | collective-permute-start | bytes 884744 | tf_op jit(solution)/shard_map/ppermute | solution.py:18
  116.0 7.3 %collective-permute-start.13 = (f32[9,4,16,128]{3,2,1,0:T(8,128)S(1)}, f32[9,4,16,128]{3,2,1,0:T(8,128)S(1)}, u32[]{:S(2)}, u32[]{:S(2)}) collective-permute-start(f32[9,4,16,128]{3,2,1,0:T(8,128)S(1)} %get-tuple-element.55), channel_id=1, source_target_pairs={{16,0},{32,16},{48,32},{64,48},{80,64},{96,80},{112,96},{128,112},... | collective-permute-start | bytes 884744 | tf_op jit(solution)/shard_map/ppermute | solution.py:20
  123.2 2.5 %collective-permute-done.12 = f32[9,4,16,128]{3,2,1,0:T(8,128)S(1)} collective-permute-done((f32[9,4,16,128]{3,2,1,0:T(8,128)S(1)}, f32[9,4,16,128]{3,2,1,0:T(8,128)S(1)}, u32[]{:S(2)}, u32[]{:S(2)}) %collective-permute-start.12) | collective-permute-done | bytes 294944 | tf_op jit(solution)/shard_map/ppermute | solution.py:18
  127.6 3.5 %collective-permute-start.14 = (f32[9,24,4,128]{3,2,1,0:T(4,128)S(1)}, f32[9,24,4,128]{3,2,1,0:T(4,128)S(1)}, u32[]{:S(2)}, u32[]{:S(2)}) collective-permute-start(f32[9,24,4,128]{3,2,1,0:T(4,128)S(1)} %get-tuple-element.48), channel_id=1, source_target_pairs={{0,1},{1,2},{2,3},{3,4},{4,5},{5,6},{6,7},{7,8},{8,9},{9,10},{10,1... | collective-permute-start | bytes 1327112 | tf_op jit(solution)/shard_map/ppermute | solution.py:18
  131.2 4.9 %collective-permute-start.15 = (f32[9,24,4,128]{3,2,1,0:T(4,128)S(1)}, f32[9,24,4,128]{3,2,1,0:T(4,128)S(1)}, u32[]{:S(2)}, u32[]{:S(2)}) collective-permute-start(f32[9,24,4,128]{3,2,1,0:T(4,128)S(1)} %get-tuple-element.49), channel_id=1, source_target_pairs={{1,0},{2,1},{3,2},{4,3},{5,4},{6,5},{7,6},{8,7},{9,8},{10,9},{11,1... | collective-permute-start | bytes 1327112 | tf_op jit(solution)/shard_map/ppermute | solution.py:20
  136.1 4.3 %collective-permute-done.14 = f32[9,24,4,128]{3,2,1,0:T(4,128)S(1)} collective-permute-done((f32[9,24,4,128]{3,2,1,0:T(4,128)S(1)}, f32[9,24,4,128]{3,2,1,0:T(4,128)S(1)}, u32[]{:S(2)}, u32[]{:S(2)}) %collective-permute-start.14) | collective-permute-done | bytes 442400 | tf_op jit(solution)/shard_map/ppermute | solution.py:18
  (160 shorter events, 35.4 us)
Async XLA Ops:
  0.6 40.3 %copy-start = (bf16[256,512]{1,0:T(8,128)(2,1)S(1)}, bf16[256,512]{1,0:T(8,128)(2,1)}, u32[]{:S(2)}) copy-start(bf16[256,512]{1,0:T(8,128)(2,1)} %param.15) | copy-start | bytes 786436
  0.6 19.2 %copy-start.5 = (f32[16,16,128]{2,1,0:T(8,128)S(1)}, f32[16,16,128]{2,1,0:T(8,128)}, u32[]{:S(2)}) copy-start(f32[16,16,128]{2,1,0:T(8,128)} %param.12) | copy-start | bytes 393220
  0.7 28.4 %copy-start.6 = (s32[256,1]{0,1:T(1,128)S(1)}, s32[256,1]{0,1:T(1,128)}, u32[]{:S(2)}) copy-start(s32[256,1]{0,1:T(1,128)} %param.18) | copy-start | bytes 3076
  0.7 40.1 %copy-start.8 = (bf16[256,6]{0,1:T(8,128)(2,1)S(1)}, bf16[256,6]{0,1:T(8,128)(2,1)}, u32[]{:S(2)}) copy-start(bf16[256,6]{0,1:T(8,128)(2,1)} %param.16) | copy-start | bytes 9220
  0.7 40.2 %copy-start.7 = (bf16[512,3]{0,1:T(4,128)(2,1)S(1)}, bf16[512,3]{0,1:T(4,128)(2,1)}, u32[]{:S(2)}) copy-start(bf16[512,3]{0,1:T(4,128)(2,1)} %param.17) | copy-start | bytes 9220
  3.0 59.3 %collective-permute-start = (f32[9,4,16,128]{3,2,1,0:T(8,128)S(1)}, f32[9,4,16,128]{3,2,1,0:T(8,128)S(1)}, u32[]{:S(2)}, u32[]{:S(2)}) collective-permute-start(f32[9,4,16,128]{3,2,1,0:T(8,128)S(1)} %get-tuple-element.58), channel_id=1, source_target_pairs={{0,16},{16,32},{32,48},{48,64},{64,80},{80,96},{96,112},{112,128},... | collective-permute-start | bytes 884744 | tf_op jit(solution)/shard_map/ppermute | solution.py:18
  4.9 57.4 %collective-permute-start.1 = (f32[9,4,16,128]{3,2,1,0:T(8,128)S(1)}, f32[9,4,16,128]{3,2,1,0:T(8,128)S(1)}, u32[]{:S(2)}, u32[]{:S(2)}) collective-permute-start(f32[9,4,16,128]{3,2,1,0:T(8,128)S(1)} %get-tuple-element.59), channel_id=1, source_target_pairs={{16,0},{32,16},{48,32},{64,48},{80,64},{96,80},{112,96},{128,112},... | collective-permute-start | bytes 884744 | tf_op jit(solution)/shard_map/ppermute | solution.py:20
  19.8 34.1 %collective-permute-start.4 = (f32[4,16,128]{2,1,0:T(8,128)S(1)}, f32[4,16,128]{2,1,0:T(8,128)S(1)}, u32[]{:S(2)}, u32[]{:S(2)}) collective-permute-start(f32[4,16,128]{2,1,0:T(8,128)S(1)} %get-tuple-element.207), channel_id=1, source_target_pairs={{0,16},{16,32},{32,48},{48,64},{64,80},{80,96},{96,112},{112,128},... | collective-permute-start | bytes 98312 | tf_op jit(solution)/shard_map/ppermute | solution.py:18
  21.8 32.3 %collective-permute-start.5 = (f32[4,16,128]{2,1,0:T(8,128)S(1)}, f32[4,16,128]{2,1,0:T(8,128)S(1)}, u32[]{:S(2)}, u32[]{:S(2)}) collective-permute-start(f32[4,16,128]{2,1,0:T(8,128)S(1)} %get-tuple-element.206), channel_id=1, source_target_pairs={{16,0},{32,16},{48,32},{64,48},{80,64},{96,80},{112,96},{128,112},... | collective-permute-start | bytes 98312 | tf_op jit(solution)/shard_map/ppermute | solution.py:20
  32.2 15.6 %all-to-all-start = ((s32[16,1,64]{2,1,0:T(1,128)}), s32[16,1,64]{2,1,0:T(1,128)S(1)}, u32[]{:S(2)}, u32[]{:S(2)}) async-start(s32[16,1,64]{2,1,0:T(1,128)} %all_to_all.9), calls=%async_computation | async-start | bytes 16384 | tf_op jit(solution)/shard_map/all_to_all | solution.py:115
  47.9 14.2 %all-to-all-start.1 = ((bf16[16,2,576]{2,1,0:T(2,128)(2,1)}), bf16[16,2,576]{2,1,0:T(2,128)(2,1)S(1)}, u32[]{:S(2)}, u32[]{:S(2)}) async-start(bf16[16,2,576]{2,1,0:T(2,128)(2,1)} %reshape.423), calls=%async_computation.1 | async-start | bytes 81920 | tf_op jit(solution)/shard_map/all_to_all | solution.py:126
  54.1 18.0 %collective-permute-start.6 = (f32[24,4,128]{2,1,0:T(4,128)S(1)}, f32[24,4,128]{2,1,0:T(4,128)S(1)}, u32[]{:S(2)}, u32[]{:S(2)}) collective-permute-start(f32[24,4,128]{2,1,0:T(4,128)S(1)} %get-tuple-element.204), channel_id=1, source_target_pairs={{0,1},{1,2},{2,3},{3,4},{4,5},{5,6},{6,7},{7,8},{8,9},{9,10},{10,1... | collective-permute-start | bytes 147464 | tf_op jit(solution)/shard_map/ppermute | solution.py:18
  57.5 14.7 %collective-permute-start.7 = (f32[24,4,128]{2,1,0:T(4,128)S(1)}, f32[24,4,128]{2,1,0:T(4,128)S(1)}, u32[]{:S(2)}, u32[]{:S(2)}) collective-permute-start(f32[24,4,128]{2,1,0:T(4,128)S(1)} %get-tuple-element.205), channel_id=1, source_target_pairs={{1,0},{2,1},{3,2},{4,3},{5,4},{6,5},{7,6},{8,7},{9,8},{10,9},{11,1... | collective-permute-start | bytes 147464 | tf_op jit(solution)/shard_map/ppermute | solution.py:20
  62.5 12.3 %collective-permute-start.2 = (f32[9,24,4,128]{3,2,1,0:T(4,128)S(1)}, f32[9,24,4,128]{3,2,1,0:T(4,128)S(1)}, u32[]{:S(2)}, u32[]{:S(2)}) collective-permute-start(f32[9,24,4,128]{3,2,1,0:T(4,128)S(1)} %get-tuple-element.52), channel_id=1, source_target_pairs={{0,1},{1,2},{2,3},{3,4},{4,5},{5,6},{6,7},{7,8},{8,9},{9,10},{10,1... | collective-permute-start | bytes 1327112 | tf_op jit(solution)/shard_map/ppermute | solution.py:18
  64.5 11.8 %collective-permute-start.3 = (f32[9,24,4,128]{3,2,1,0:T(4,128)S(1)}, f32[9,24,4,128]{3,2,1,0:T(4,128)S(1)}, u32[]{:S(2)}, u32[]{:S(2)}) collective-permute-start(f32[9,24,4,128]{3,2,1,0:T(4,128)S(1)} %get-tuple-element.53), channel_id=1, source_target_pairs={{1,0},{2,1},{3,2},{4,3},{5,4},{6,5},{7,6},{8,7},{9,8},{10,9},{11,1... | collective-permute-start | bytes 1327112 | tf_op jit(solution)/shard_map/ppermute | solution.py:20
  81.7 11.7 %collective-permute-start.8 = (f32[9,4,16,128]{3,2,1,0:T(8,128)S(1)}, f32[9,4,16,128]{3,2,1,0:T(8,128)S(1)}, u32[]{:S(2)}, u32[]{:S(2)}) collective-permute-start(f32[9,4,16,128]{3,2,1,0:T(8,128)S(1)} %get-tuple-element.56), channel_id=1, source_target_pairs={{0,16},{16,32},{32,48},{48,64},{64,80},{80,96},{96,112},{112,128},... | collective-permute-start | bytes 884744 | tf_op jit(solution)/shard_map/ppermute | solution.py:18
  83.6 11.5 %collective-permute-start.9 = (f32[9,4,16,128]{3,2,1,0:T(8,128)S(1)}, f32[9,4,16,128]{3,2,1,0:T(8,128)S(1)}, u32[]{:S(2)}, u32[]{:S(2)}) collective-permute-start(f32[9,4,16,128]{3,2,1,0:T(8,128)S(1)} %get-tuple-element.57), channel_id=1, source_target_pairs={{16,0},{32,16},{48,32},{64,48},{80,64},{96,80},{112,96},{128,112},... | collective-permute-start | bytes 884744 | tf_op jit(solution)/shard_map/ppermute | solution.py:20
  95.3 12.8 %collective-permute-start.10 = (f32[9,24,4,128]{3,2,1,0:T(4,128)S(1)}, f32[9,24,4,128]{3,2,1,0:T(4,128)S(1)}, u32[]{:S(2)}, u32[]{:S(2)}) collective-permute-start(f32[9,24,4,128]{3,2,1,0:T(4,128)S(1)} %get-tuple-element.50), channel_id=1, source_target_pairs={{0,1},{1,2},{2,3},{3,4},{4,5},{5,6},{6,7},{7,8},{8,9},{9,10},{10,1... | collective-permute-start | bytes 1327112 | tf_op jit(solution)/shard_map/ppermute | solution.py:18
  97.2 12.3 %collective-permute-start.11 = (f32[9,24,4,128]{3,2,1,0:T(4,128)S(1)}, f32[9,24,4,128]{3,2,1,0:T(4,128)S(1)}, u32[]{:S(2)}, u32[]{:S(2)}) collective-permute-start(f32[9,24,4,128]{3,2,1,0:T(4,128)S(1)} %get-tuple-element.51), channel_id=1, source_target_pairs={{1,0},{2,1},{3,2},{4,3},{5,4},{6,5},{7,6},{8,7},{9,8},{10,9},{11,1... | collective-permute-start | bytes 1327112 | tf_op jit(solution)/shard_map/ppermute | solution.py:20
  114.0 11.7 %collective-permute-start.12 = (f32[9,4,16,128]{3,2,1,0:T(8,128)S(1)}, f32[9,4,16,128]{3,2,1,0:T(8,128)S(1)}, u32[]{:S(2)}, u32[]{:S(2)}) collective-permute-start(f32[9,4,16,128]{3,2,1,0:T(8,128)S(1)} %get-tuple-element.54), channel_id=1, source_target_pairs={{0,16},{16,32},{32,48},{48,64},{64,80},{80,96},{96,112},{112,128},... | collective-permute-start | bytes 884744 | tf_op jit(solution)/shard_map/ppermute | solution.py:18
  116.0 11.5 %collective-permute-start.13 = (f32[9,4,16,128]{3,2,1,0:T(8,128)S(1)}, f32[9,4,16,128]{3,2,1,0:T(8,128)S(1)}, u32[]{:S(2)}, u32[]{:S(2)}) collective-permute-start(f32[9,4,16,128]{3,2,1,0:T(8,128)S(1)} %get-tuple-element.55), channel_id=1, source_target_pairs={{16,0},{32,16},{48,32},{64,48},{80,64},{96,80},{112,96},{128,112},... | collective-permute-start | bytes 884744 | tf_op jit(solution)/shard_map/ppermute | solution.py:20
  127.6 12.8 %collective-permute-start.14 = (f32[9,24,4,128]{3,2,1,0:T(4,128)S(1)}, f32[9,24,4,128]{3,2,1,0:T(4,128)S(1)}, u32[]{:S(2)}, u32[]{:S(2)}) collective-permute-start(f32[9,24,4,128]{3,2,1,0:T(4,128)S(1)} %get-tuple-element.48), channel_id=1, source_target_pairs={{0,1},{1,2},{2,3},{3,4},{4,5},{5,6},{6,7},{7,8},{8,9},{9,10},{10,1... | collective-permute-start | bytes 1327112 | tf_op jit(solution)/shard_map/ppermute | solution.py:18
  131.2 10.7 %collective-permute-start.15 = (f32[9,24,4,128]{3,2,1,0:T(4,128)S(1)}, f32[9,24,4,128]{3,2,1,0:T(4,128)S(1)}, u32[]{:S(2)}, u32[]{:S(2)}) collective-permute-start(f32[9,24,4,128]{3,2,1,0:T(4,128)S(1)} %get-tuple-element.49), channel_id=1, source_target_pairs={{1,0},{2,1},{3,2},{4,3},{5,4},{6,5},{7,6},{8,7},{9,8},{10,9},{11,1... | collective-permute-start | bytes 1327112 | tf_op jit(solution)/shard_map/ppermute | solution.py:20
  146.8 1.3 copy-start.1
  (3 other events, 3.0 us)
where the time goes:
time: 150 us; the launch traced here: 148 us
  starting transfers between devices  90.6 us (60%)
  waiting for transfers between devices  28.4 us (19%)
  local copies, waits for them, and re-layouts  17.3 us (12%)
  other arithmetic  8.59 us (6%)
  matrix products  1.62 us (1%)
  between operations  1.53 us (1%)
    ppermute x8, starting transfers between devices, extended(): lax.ppermute(head, axis, [((i + 1) % count, i) for i in range(ends)])  58.8 us
    ppermute x8, starting transfers between devices, extended(): lax.ppermute(tail, axis, [(i, (i + 1) % count) for i in range(ends)])  18.4 us
    ppermute x8, waiting for transfers between devices, extended(): lax.ppermute(tail, axis, [(i, (i + 1) % count) for i in range(ends)])  16.1 us
    all_to_all x1, starting transfers between devices, local(): lax.all_to_all(cell_buffer, 'gy', split_axis=0, concat_axis=0, tiled=True)  8.58 us
    ppermute x8, waiting for transfers between devices, extended(): lax.ppermute(head, axis, [((i + 1) % count, i) for i in range(ends)])  7.9 us
    slice x34, local copies, waits for them, and re-layouts, window(): return lax.slice_in_dim(values, start_at, start_at + extent, axis=dimension)  6.03 us
    all_to_all x1, starting transfers between devices, local(): lax.all_to_all(term_buffer.reshape(groups, capacity, -1), 'gy', split_axi...  4.78 us
    all_to_all x1, waiting for transfers between devices, local(): lax.all_to_all(cell_buffer, 'gy', split_axis=0, concat_axis=0, tiled=True)  4.39 us
  transfers between devices with their start and end apart: 18, of which 11 were waited for; matrix products, arithmetic and copies ran while one was open for 6% of the time, Pallas kernels for 0%

commit v1 on v0

v1 whole, which is shorter than its diff:
```python
import jax
import jax.numpy as jnp
from jax import lax
from jax.experimental import pallas as pl
from jax.experimental.pallas import tpu as pltpu
from jax.sharding import PartitionSpec as P

INNER = 9.0 / 8.0
OUTER = -1.0 / 24.0
F32, BF16, I32 = jnp.float32, jnp.bfloat16, jnp.int32

N = 16
Z = 128
XO = 11
XE = XO + N + XO
YO = 16
YE = 48
DEPTH = [9] * 6 + [8] * 3 + [8, 6, 6]
CORNER = [8] * 6 + [6] * 3 + [6, 5, 5]
NQ = len(DEPTH)
FACE = [(q, d) for q in range(NQ) for d in range(1, DEPTH[q] + 1)]
FACE_AT = {qd: i for i, qd in enumerate(FACE)}
LOW_AT = {q: len(FACE) + q for q in range(NQ)}
NFACE = len(FACE) + NQ
CORN = [(q, d) for q in range(NQ) for d in range(1, CORNER[q] + 1)]
CORN_AT = {qd: NFACE + i for i, qd in enumerate(CORN)}
NCORN = len(CORN)
SLOTS = 64


def vmem():
    return pl.BlockSpec(memory_space=pltpu.VMEM)


def part(refs, q):
    v, s, b, l, m = refs
    if q < 6:
        return s.at[q]
    if q < 9:
        return v.at[q - 6]
    return (b, l, m)[q - 9]


def split(x):
    hi = x.astype(BF16)
    return hi, (x - hi.astype(F32)).astype(BF16)


def pack_y(v, s, b, l, m, out_a, out_b):
    odd = lax.rem(lax.axis_index("gy"), 2)
    refs = (v, s, b, l, m)
    for out, high in ((out_a, odd == 0), (out_b, odd == 1)):
        for q in range(NQ):
            src = part(refs, q)
            for d in range(1, DEPTH[q] + 1):
                y = jnp.where(high, N - d, d - 1)
                rows = src[pl.ds(y, N, stride=N), :]
                if d == 1:
                    hi, lo = split(rows)
                    out[FACE_AT[q, d]] = hi
                    out[LOW_AT[q]] = lo
                else:
                    out[FACE_AT[q, d]] = rows.astype(BF16)


def route(groups, hist, mech, res, owners, cells, out, vals):
    rows = hist.shape[0]
    nt = (((1,), (1,)), ((), ()))
    amp = lax.dot_general(res[...], hist[...], nt, preferred_element_type=F32)
    mechf = mech[...].astype(F32)
    vals[...] = jnp.zeros_like(vals)
    vals[0:6] = mechf * amp[0:1]
    vals[6:12] = mechf * amp[1:2]
    vals[16:22] = mechf * amp[2:3]
    cell = cells[...]
    vals[12:13] = (cell // Z).astype(F32)
    vals[13:14] = (cell % Z).astype(F32)
    v = vals[...].astype(BF16)
    own = owners[...]
    hits = (lax.broadcasted_iota(I32, (groups, rows), 0) == own).astype(F32)
    r0 = lax.broadcasted_iota(I32, (rows, rows), 0)
    r1 = lax.broadcasted_iota(I32, (rows, rows), 1)
    before = (r0 < r1).astype(F32).astype(BF16)
    earlier = jnp.dot(hits.astype(BF16), before, preferred_element_type=F32)
    rank = jnp.sum(hits * earlier, axis=0, keepdims=True)
    slot = own * SLOTS + rank.astype(I32)
    total = groups * SLOTS
    pick = (lax.broadcasted_iota(I32, (total, rows), 0) == slot).astype(F32).astype(BF16)
    sent = lax.dot_general(v, pick, nt, preferred_element_type=F32)
    turned = pltpu.roll(sent, SLOTS, 1)
    left = lax.broadcasted_iota(I32, (16, 2 * SLOTS), 1) < SLOTS
    zero = jnp.zeros((16, 2 * SLOTS), F32)

    def plain(j, h):
        return sent[16 * h : 16 * h + 16, 128 * j : 128 * j + 128]

    def shifted(j, h):
        j = j % (groups // 2)
        return turned[16 * h : 16 * h + 16, 128 * j : 128 * j + 128]

    for o in range(groups):
        j = o // 2
        if o % 2 == 0:
            sides = jnp.where(left, shifted(j, 0) if j else zero, plain(j, 0))
            mine = jnp.where(left, plain(j, 0), shifted(j, 1))
        else:
            last = o == groups - 1
            sides = jnp.where(left, plain(j, 0), zero if last else shifted(j + 1, 0))
            mine = jnp.where(left, shifted(j + 1, 0), plain(j, 1))
        out[o, 0:16, :] = sides.astype(BF16)
        out[o, 16:32, :] = mine.astype(BF16)


def pack_x(ya, yb, v, s, b, l, m, lists, out_a, out_b):
    odd_x = lax.rem(lax.axis_index("gx"), 2)
    odd_y = lax.rem(lax.axis_index("gy"), 2)
    refs = (v, s, b, l, m)
    for out, high in ((out_a, odd_x == 0), (out_b, odd_x == 1)):
        for q in range(NQ):
            src = part(refs, q)
            for d in range(1, DEPTH[q] + 1):
                x = jnp.where(high, N - d, d - 1)
                rows = src[pl.ds(pl.multiple_of(x * N, N), N), :]
                if d == 1:
                    hi, lo = split(rows)
                    out[FACE_AT[q, d]] = hi
                    out[LOW_AT[q]] = lo
                else:
                    out[FACE_AT[q, d]] = rows.astype(BF16)
        groups = lists.shape[0]
        for g in range(groups):
            for h in range(2):
                out[NFACE + NCORN + 2 * g + h] = lists[g, 16 * h : 16 * h + 16, :]

    def corners(low, top, out, high):
        for q, d in CORN:
            i = FACE_AT[q, d]
            a = low[i].astype(F32)
            c = top[i].astype(F32)
            k = 8 if high else 0
            both = jnp.concatenate([a[k : k + 8], c[k : k + 8]], axis=0)
            out[CORN_AT[q, d]] = both.astype(BF16)

    for px in range(2):
        for py in range(2):

            @pl.when((odd_x == px) & (odd_y == py))
            def _():
                low, top = (yb, ya) if py == 0 else (ya, yb)
                corners(low, top, out_a, px == 0)
                corners(low, top, out_b, px == 1)


def lanes(blocks):
    return jnp.concatenate(blocks, axis=1)


def own_lists(get, groups):
    left = lax.broadcasted_iota(I32, (16, 128), 1) < SLOTS
    first, last = [], []
    for i in range(groups // 2):
        a, b = get(2 * i), get(2 * i + 1)
        first.append(jnp.where(left, a, pltpu.roll(b, SLOTS, 1)))
        last.append(jnp.where(left, pltpu.roll(a, SLOTS, 1), b))
    return lanes(first), lanes(last)


def one_hot(code, count):
    width = code.shape[1]
    return (lax.broadcasted_iota(I32, (count, width), 0) == code).astype(F32).astype(BF16)


NT = (((1,), (1,)), ((), ()))


def place(planes, levels, values, row):
    a = planes * values[row : row + 1, :]
    return lax.dot_general(a, levels, NT, preferred_element_type=F32)


def sided(groups, sides):
    plane = sides[12:13, :].astype(I32)
    level = sides[13:14, :].astype(I32)
    upper = lax.rem(lax.broadcasted_iota(I32, plane.shape, 1), 128) >= SLOTS
    x, y = plane // N, plane % N
    row = jnp.where(upper, y, y - 8)
    row = jnp.where(upper, jnp.where(y <= 5, row, -9999), jnp.where(y >= 10, row, -9999))
    levels = one_hot(jnp.where(upper, level + Z, level), 2 * Z)
    return x, row, levels


def place_own(lists, out_own, out_side):
    groups = lists.shape[0]
    first, last = own_lists(lambda g: lists[g, 16:32, :].astype(F32), groups)
    planes = one_hot(first[12:13, :].astype(I32), N * N)
    levels = one_hot(first[13:14, :].astype(I32), Z)
    first, last = first.astype(BF16), last.astype(BF16)
    for t in range(3):
        for c in range(6):
            vals, row = (first, 6 * t + c) if t < 2 else (last, c)
            out_own[6 * t + c] = place(planes, levels, vals, row)
    sides = lanes([lists[g, 0:16, :].astype(F32) for g in range(groups)])
    x, row, levels = sided(groups, sides)
    planes = one_hot(x * 8 + row, 8 * N)
    sides = sides.astype(BF16)
    for k in range(12):
        out_side[k] = place(planes, levels, sides, k)


def roll_z(f, k, lane):
    moved = pltpu.roll(f, (-k) % Z, f.ndim - 1)
    keep = (lane < Z - k) if k > 0 else (lane >= -k)
    return jnp.where(keep, moved, 0.0)


def advance(xa, xb, ya, yb, v, s, b, l, m, own, side, vout, sout, ev, es, eb, el, em):
    odd_x = lax.rem(lax.axis_index("gx"), 2)
    odd_y = lax.rem(lax.axis_index("gy"), 2)
    refs = (v, s, b, l, m)
    ext = (ev, es, eb, el, em)

    def at(x, y):
        return x * YE + y

    for q in range(NQ):
        src, dst = part(refs, q), part(ext, q)
        for x in range(N):
            dst[at(XO + x, YO) : at(XO + x, YO) + N, :] = src[N * x : N * x + N, :]

    def layer(msg, q, d):
        rows = msg[FACE_AT[q, d]].astype(F32)
        if d == 1:
            rows = rows + msg[LOW_AT[q]].astype(F32)
        return rows

    def put_y(low, top):
        for q in range(NQ):
            dst = part(ext, q)
            for d in range(1, DEPTH[q] + 1):
                dst[pl.ds(at(XO, YO - d), N, stride=YE), :] = layer(low, q, d)
                dst[pl.ds(at(XO, YO + N - 1 + d), N, stride=YE), :] = layer(top, q, d)

    def put_x(low, top):
        groups = (low.shape[0] - NFACE - NCORN) // 2
        for q in range(NQ):
            dst = part(ext, q)
            for d in range(1, DEPTH[q] + 1):
                for msg, x in ((low, XO - d), (top, XO + N - 1 + d)):
                    dst[at(x, YO) : at(x, YO) + N, :] = layer(msg, q, d)
            for d in range(1, CORNER[q] + 1):
                for msg, x in ((low, XO - 8), (top, XO + N)):
                    both = msg[CORN_AT[q, d]].astype(F32)
                    dst[pl.ds(at(x, YO - d), 8, stride=YE), :] = both[0:8]
                    dst[pl.ds(at(x, YO + N - 1 + d), 8, stride=YE), :] = both[8:16]
        return groups

    for odd, put, one, two in ((odd_y, put_y, ya, yb), (odd_x, put_x, xa, xb)):

        @pl.when(odd == 0)
        def _():
            put(two, one)

        @pl.when(odd == 1)
        def _():
            put(one, two)

    def velocity_at(x, y0, n):
        base = x * YE
        lane = lax.broadcasted_iota(I32, (n, Z), 1)

        def st(c, dx=0, dy=0):
            return es[c, pl.ds(base + (dx * YE + y0 + dy), n), :]

        def dif(g, fwd):
            k = 0 if fwd else -1
            return INNER * (g(1 + k) - g(k)) + OUTER * (g(2 + k) - g(k - 1))

        def along_z(f):
            return lambda k: f if k == 0 else roll_z(f, k, lane)

        buoy = eb[pl.ds(base + y0, n), :]
        fx = dif(lambda k: st(0, dx=k), True) + dif(lambda k: st(3, dy=k), False)
        fx = fx + dif(along_z(st(4)), False)
        fy = dif(lambda k: st(3, dx=k), False) + dif(lambda k: st(1, dy=k), True)
        fy = fy + dif(along_z(st(5)), False)
        fz = dif(lambda k: st(4, dx=k), False) + dif(lambda k: st(5, dy=k), False)
        fz = fz + dif(along_z(st(2)), True)
        for c, f in enumerate((fx, fy, fz)):
            here = pl.ds(base + y0, n)
            ev[c, here, :] = ev[c, here, :] + buoy * f

    def stress_at(x, y0, n):
        base = x * YE
        lane = lax.broadcasted_iota(I32, (n, Z), 1)

        def ve(c, dx=0, dy=0):
            return ev[c, pl.ds(base + (dx * YE + y0 + dy), n), :]

        def dif(g, fwd):
            k = 0 if fwd else -1
            return INNER * (g(1 + k) - g(k)) + OUTER * (g(2 + k) - g(k - 1))

        def along_z(f):
            return lambda k: f if k == 0 else roll_z(f, k, lane)

        here = pl.ds(base + y0, n)
        lam, rig = el[here, :], em[here, :]
        d1 = dif(lambda k: ve(0, dx=k), False)
        d2 = dif(lambda k: ve(1, dy=k), False)
        d3 = dif(along_z(ve(2)), False)
        e = lam * (d1 + d2 + d3)
        two = 2.0 * rig
        rates = (
            e + two * d1,
            e + two * d2,
            e + two * d3,
            rig * (dif(lambda k: ve(0, dy=k), True) + dif(lambda k: ve(1, dx=k), True)),
            rig * (dif(along_z(ve(0)), True) + dif(lambda k: ve(2, dx=k), True)),
            rig * (dif(along_z(ve(1)), True) + dif(lambda k: ve(2, dy=k), True)),
        )
        for c, r in enumerate(rates):
            es[c, here, :] = es[c, here, :] + r

    def sweep(fn, reach, y0, n):
        def step(x, carry):
            fn(x, y0, n)
            return carry

        lax.fori_loop(XO - reach, XO + N + reach, step, 0)

    def add(c, x, y, rows):
        here = slice(at(x, y), at(x, y) + rows.shape[0])
        es[c, here, :] = es[c, here, :] + rows

    def add_own(t):
        for c in range(6):
            for x in range(N):
                add(c, XO + x, YO, own[6 * t + c, N * x : N * x + N, :])

    def add_side(t):
        for c in range(6):
            for x in range(N):
                rows = slice(8 * x, 8 * x + 8)
                add(c, XO + x, YO - 8, side[6 * t + c, rows, 0:Z])
                add(c, XO + x, YO + N, side[6 * t + c, rows, Z : 2 * Z])

    def add_beyond(t, far):
        groups = (xa.shape[0] - NFACE - NCORN) // 2
        base = NFACE + NCORN

        def one(msg, up):
            first, _ = own_lists(lambda g: msg[base + 2 * g + 1].astype(F32), groups)
            plane = first[12:13, :].astype(I32)
            levels = one_hot(first[13:14, :].astype(I32), Z)
            x, y = plane // N, plane % N
            i = x if up else x - (N - far)
            planes = one_hot(jnp.where(i >= 0, i * N + y, -1), far * N)
            first = first.astype(BF16)
            x0 = XO + N if up else XO - far
            for c in range(6):
                got = place(planes, levels, first, 6 * t + c)
                for k in range(far):
                    add(c, x0 + k, YO, got[N * k : N * k + N])
            near = 5 if t == 0 else 2
            sides = lanes([msg[base + 2 * g].astype(F32) for g in range(groups)])
            x, row, levels = sided(groups, sides)
            i = x if up else x - (N - near)
            planes = one_hot(jnp.where(i >= 0, i * 8 + row, -1), 8 * near)
            sides = sides.astype(BF16)
            x0 = XO + N if up else XO - near
            for c in range(6):
                got = place(planes, levels, sides, 6 * t + c)
                for k in range(near):
                    add(c, x0 + k, YO - 8, got[8 * k : 8 * k + 8, 0:Z])
                    add(c, x0 + k, YO + N, got[8 * k : 8 * k + 8, Z : 2 * Z])

        @pl.when(odd_x == 0)
        def _():
            one(xb, False)
            one(xa, True)

        @pl.when(odd_x == 1)
        def _():
            one(xa, False)
            one(xb, True)

    sweep(velocity_at, 8, 8, 32)
    sweep(stress_at, 6, 8, 32)
    add_own(0)
    add_side(0)
    add_beyond(0, 6)
    sweep(velocity_at, 5, 8, 32)
    sweep(stress_at, 3, 8, 32)
    add_own(1)
    add_side(1)
    add_beyond(1, 3)
    sweep(velocity_at, 2, 8, 32)
    sweep(stress_at, 0, 16, 16)
    for x in range(N):
        here = slice(at(XO + x, YO), at(XO + x, YO) + N)
        rows = slice(N * x, N * x + N)
        for c in range(3):
            vout[c, rows, :] = ev[c, here, :]
        for c in range(6):
            sout[c, rows, :] = es[c, here, :] + own[12 + c, rows, :]


def swaps(count, first):
    pairs = []
    for i in range(first, count - 1, 2):
        pairs += [(i, i + 1), (i + 1, i)]
    return pairs


def swap_both(a, b, axis):
    count = lax.axis_size(axis)
    return (
        lax.ppermute(a, axis, swaps(count, 0)),
        lax.ppermute(b, axis, swaps(count, 1)),
    )


def call(kernel, outs, args, scratch=(), flops=1_000_000):
    return pl.pallas_call(
        kernel,
        out_shape=[jax.ShapeDtypeStruct(s, t) for s, t in outs],
        in_specs=[vmem()] * len(args),
        out_specs=[vmem()] * len(outs),
        scratch_shapes=list(scratch),
        compiler_params=pltpu.CompilerParams(vmem_limit_bytes=56 * 1024 * 1024),
        cost_estimate=pl.CostEstimate(flops=flops, bytes_accessed=1_000_000, transcendentals=0),
    )(*args)


def local(velocity, stresses, buoyancy, lame, rigidity, hist, mech, res, owners, cells):
    groups = lax.axis_size("gy")
    v = velocity.reshape(3, N * N, Z)
    s = stresses.reshape(6, N * N, Z)
    b, l, m = (a.reshape(N * N, Z) for a in (buoyancy, lame, rigidity))
    state = (v, s, b, l, m)
    face = ((NFACE, N, Z), BF16)
    ya, yb = call(pack_y, [face, face], state)
    ya, yb = swap_both(ya, yb, "gy")
    rows = hist.shape[0]
    (sent,) = call(
        lambda *refs: route(groups, *refs),
        [((groups, 32, 128), BF16)],
        (hist, mech.T, res.T, owners.reshape(1, rows), cells.reshape(1, rows)),
        [pltpu.VMEM((32, rows), F32)],
    )
    lists = lax.all_to_all(sent, "gy", split_axis=0, concat_axis=0, tiled=True)
    whole = ((NFACE + NCORN + 2 * groups, N, Z), BF16)
    xa, xb = call(pack_x, [whole, whole], (ya, yb) + state + (lists,))
    xa, xb = swap_both(xa, xb, "gx")
    own, side = call(
        place_own,
        [((18, N * N, Z), F32), ((12, 8 * N, 2 * Z), F32)],
        (lists,),
        flops=10_000_000_000,
    )
    block = pltpu.VMEM((XE * YE, Z), F32)
    vout, sout = call(
        advance,
        [(v.shape, F32), (s.shape, F32)],
        (xa, xb, ya, yb) + state + (own, side),
        [pltpu.VMEM((3, XE * YE, Z), F32), pltpu.VMEM((6, XE * YE, Z), F32), block, block, block],
    )
    return vout.reshape(velocity.shape), sout.reshape(stresses.shape)


def solution(mesh):
    in_specs = (
        P(None, "gx", "gy", None),
        P(None, "gx", "gy", None),
        P("gx", "gy", None),
        P("gx", "gy", None),
        P("gx", "gy", None),
        P(("gx", "gy"), None),
        P(("gx", "gy"), None),
        P(),
        P(("gx", "gy"), None),
        P(("gx", "gy")),
    )
    out_specs = (P(None, "gx", "gy", None), P(None, "gx", "gy", None))
    return jax.shard_map(local, mesh=mesh, in_specs=in_specs, out_specs=out_specs, check_vma=False)
```

time: 150 us -> 93.4 us (0.62); the launches traced: 148 us -> 93 us
  starting transfers between devices: 90.6 us -> 26.3 us
  Pallas kernels: 0 us -> 48.5 us
  waiting for transfers between devices: 28.4 us -> 2.66 us
  local copies, waits for them, and re-layouts: 17.3 us -> 2.48 us
  blocking collectives: 0 us -> 12.4 us
  other arithmetic: 8.59 us -> 0 us
  matrix products: 1.62 us -> 0 us
    ppermute x16 -> x4, starting transfers between devices: 77.2 us -> 26.3 us  [the longest x2 20.9 us: swap_both(): lax.ppermute(b, axis, swaps(count, 1))]
    pallas_call x0 -> x5, Pallas kernels: none -> 48.5 us  [call(): pl.pallas_call(kernel, out_shape=[jax.ShapeDtypeStruct(s, t) for s, t in...]
    ppermute x16 -> x4, waiting for transfers between devices: 24 us -> 2.66 us  [the longest x2 2.65 us: swap_both(): lax.ppermute(b, axis, swaps(count, 1))]
    all_to_all x2 -> x0, starting transfers between devices: 13.4 us -> none  [the longest x1 8.58 us: local(): lax.all_to_all(cell_buffer, 'gy', split_axis=0, concat_axis=0, tiled=True)]
    all_to_all x0 -> x1, blocking collectives: none -> 12.4 us  [local(): lists = lax.all_to_all(sent, 'gy', split_axis=0, concat_axis=0, tiled=True)]
    slice x42 -> x0, local copies, waits for them, and re-layouts: 7.24 us -> none  [the longest x34 6.03 us: window(): return lax.slice_in_dim(values, start_at, start_at + extent, axis=dimension)]
    all_to_all x2 -> x0, waiting for transfers between devices: 4.39 us -> none  [the longest x1 4.39 us: local(): lax.all_to_all(cell_buffer, 'gy', split_axis=0, concat_axis=0, tiled=True)]
    another operation x14 -> x0, other arithmetic: 2.95 us -> none  [the longest x9 1.96 us: advance_velocity(): jnp.stack([differ(stresses[0], 0, True) + differ(stresses[3], 1, False) +...]
  transfers between devices with their start and end apart: 18 -> 4, of which waited for: 11 -> 1; matrix products, arithmetic and copies ran while one was open for 6% -> 0% of each run, Pallas kernels for 0% -> 12%
where the time goes in v1:
time: 93.4 us; the launch traced here: 93 us
  Pallas kernels  48.5 us (52%)
  starting transfers between devices  26.3 us (28%)
  blocking collectives  12.4 us (13%)
  waiting for transfers between devices  2.66 us (3%)
  local copies, waits for them, and re-layouts  2.48 us (3%)
    pallas_call x5, Pallas kernels, call(): pl.pallas_call(kernel, out_shape=[jax.ShapeDtypeStruct(s, t) for s, t in...  48.5 us
    ppermute x2, starting transfers between devices, swap_both(): lax.ppermute(b, axis, swaps(count, 1))  20.9 us
    all_to_all x1, blocking collectives, local(): lists = lax.all_to_all(sent, 'gy', split_axis=0, concat_axis=0, tiled=True)  12.4 us
    ppermute x2, starting transfers between devices, swap_both(): lax.ppermute(a, axis, swaps(count, 0))  5.38 us
    ppermute x2, waiting for transfers between devices, swap_both(): lax.ppermute(b, axis, swaps(count, 1))  2.65 us
    unnamed x8, local copies, waits for them, and re-layouts  2.48 us
  transfers between devices with their start and end apart: 4, of which 1 were waited for; matrix products, arithmetic and copies ran while one was open for 0% of the time, Pallas kernels for 12%

profile of v1, /device:TPU:6, one launch (start us, length us, event | category | flops | bytes accessed | tf_op | source)
XLA Modules:
  0.0 93.0 jit_solution(1476971943833855929)
XLA Ops:
  0.6 3.1 %shard_map.113 = (bf16[110,16,128]{2,1,0:T(8,128)(2,1)}, bf16[110,16,128]{2,1,0:T(8,128)(2,1)}) custom-call(f32[3,256,128]{2,1,0:T(8,128)} %bitcast.14, f32[6,256,128]{2,1,0:T(8,128)} %bitcast.11, f32[256,128]{1,0:T(8,128)} %bitcast.17, f32[256,128]{1,0:T(8,128)} %bitcast.20, f32[256,128]{1,0:T(8,128)} %bitcast.23), custom_call_target="tpu_custom_call" | custom-call | flops 1000000 | bytes 1000000 | tf_op jit(solution)/shard_map/pallas_call | solution.py:424
  3.7 3.5 %collective-permute-start = (bf16[110,16,128]{2,1,0:T(8,128)(2,1)}, bf16[110,16,128]{2,1,0:T(8,128)(2,1)S(1)}, u32[]{:S(2)}, u32[]{:S(2)}) collective-permute-start(bf16[110,16,128]{2,1,0:T(8,128)(2,1)} %get-tuple-element.10), channel_id=1, source_target_pairs={{0,1},{1,0},{2,3},{3,2},{4,5},{5,4},{6,7},{7,6},{8,9},{9,8},{10,11... | collective-permute-start | bytes 1351688 | tf_op jit(solution)/shard_map/ppermute | solution.py:418
  7.2 5.4 %collective-permute-start.1 = (bf16[110,16,128]{2,1,0:T(8,128)(2,1)}, bf16[110,16,128]{2,1,0:T(8,128)(2,1)S(1)}, u32[]{:S(2)}, u32[]{:S(2)}) collective-permute-start(bf16[110,16,128]{2,1,0:T(8,128)(2,1)} %get-tuple-element.11), channel_id=1, source_target_pairs={{1,2},{2,1},{3,4},{4,3},{5,6},{6,5},{7,8},{8,7},{9,10},{10,9},{11,... | collective-permute-start | bytes 1351688 | tf_op jit(solution)/shard_map/ppermute | solution.py:419
  12.6 2.2 %shard_map.114 = bf16[16,32,128]{2,1,0:T(8,128)(2,1)} custom-call(bf16[256,512]{1,0:T(8,128)(2,1)} %refs_0_.1, bf16[6,256]{1,0:T(8,128)(2,1)} %bitcast.26, bf16[3,512]{1,0:T(4,128)(2,1)} %bitcast.27, s32[1,256]{1,0:T(1,128)} %bitcast.28, s32[1,256]{1,0:T(1,128)} %bitcast.29), custom_call_target="tpu_custom_call" | custom-call | flops 1000000 | bytes 1000000 | tf_op jit(solution)/shard_map/pallas_call | solution.py:424
  14.9 12.4 %all_to_all.5.lists = bf16[16,32,128]{2,1,0:T(8,128)(2,1)} all-to-all(bf16[16,32,128]{2,1,0:T(8,128)(2,1)} %shard_map.114), channel_id=1, replica_groups=mesh['gx'=48,'gy'=16] {'gy'}, dimensions={0} | all-to-all | bytes 262144 | tf_op jit(solution)/shard_map/all_to_all | solution.py:451
  27.2 0.0 collective-permute-done.ya
  27.2 0.0 copy-start
  27.2 0.0 collective-permute-done.1.yb
  27.3 0.8 copy-done
  28.0 0.0 copy-start.1
  28.0 0.8 copy-done.1
  28.8 3.1 %shard_map.115 = (bf16[224,16,128]{2,1,0:T(8,128)(2,1)}, bf16[224,16,128]{2,1,0:T(8,128)(2,1)}) custom-call(bf16[110,16,128]{2,1,0:T(8,128)(2,1)} %copy-done, bf16[110,16,128]{2,1,0:T(8,128)(2,1)} %copy-done.1, f32[3,256,128]{2,1,0:T(8,128)} %bitcast.15, f32[6,256,128]{2,1,0:T(8,128)} %bitcast.12, f32[256,128]{1,0:T(8,128)} %bitcast.18, ...), custom_call_target="tpu_custom_call" | custom-call | flops 1000000 | bytes 1000000 | tf_op jit(solution)/shard_map/pallas_call | solution.py:424
  31.9 1.9 %collective-permute-start.2 = (bf16[224,16,128]{2,1,0:T(8,128)(2,1)}, bf16[224,16,128]{2,1,0:T(8,128)(2,1)S(1)}, u32[]{:S(2)}, u32[]{:S(2)}) collective-permute-start(bf16[224,16,128]{2,1,0:T(8,128)(2,1)} %get-tuple-element.12), channel_id=1, source_target_pairs={{0,16},{16,0},{32,48},{48,32},{64,80},{80,64},{96,112},{112,96},{1... | collective-permute-start | bytes 2752520 | tf_op jit(solution)/shard_map/ppermute | solution.py:418
  33.9 15.5 %collective-permute-start.3 = (bf16[224,16,128]{2,1,0:T(8,128)(2,1)}, bf16[224,16,128]{2,1,0:T(8,128)(2,1)S(1)}, u32[]{:S(2)}, u32[]{:S(2)}) collective-permute-start(bf16[224,16,128]{2,1,0:T(8,128)(2,1)} %get-tuple-element.13), channel_id=1, source_target_pairs={{16,32},{32,16},{48,64},{64,48},{80,96},{96,80},{112,128},{128,112... | collective-permute-start | bytes 2752520 | tf_op jit(solution)/shard_map/ppermute | solution.py:419
  49.4 8.6 %shard_map.116 = (f32[18,256,128]{2,1,0:T(8,128)}, f32[12,128,256]{2,1,0:T(8,128)}) custom-call(bf16[16,32,128]{2,1,0:T(8,128)(2,1)} %all_to_all.5.lists), custom_call_target="tpu_custom_call" | custom-call | flops 10000000000 | bytes 1000000 | tf_op jit(solution)/shard_map/pallas_call | solution.py:424
  58.0 0.0 collective-permute-done.2.xa
  58.0 0.0 copy-start.2
  58.0 2.6 %collective-permute-done.3.xb = bf16[224,16,128]{2,1,0:T(8,128)(2,1)S(1)} collective-permute-done((bf16[224,16,128]{2,1,0:T(8,128)(2,1)}, bf16[224,16,128]{2,1,0:T(8,128)(2,1)S(1)}, u32[]{:S(2)}, u32[]{:S(2)}) %collective-permute-start.3) | collective-permute-done | bytes 917536 | tf_op jit(solution)/shard_map/ppermute | solution.py:419
  60.7 0.0 copy-start.3
  60.7 0.0 copy-done.2
  60.7 0.9 %copy-done.3 = bf16[224,16,128]{2,1,0:T(8,128)(2,1)} copy-done((bf16[224,16,128]{2,1,0:T(8,128)(2,1)}, bf16[224,16,128]{2,1,0:T(8,128)(2,1)S(1)}, u32[]{:S(2)}) %copy-start.3) | copy-done | bytes 917528
  61.6 31.4 %shard_map.117 = (f32[3,256,128]{2,1,0:T(8,128)}, f32[6,256,128]{2,1,0:T(8,128)}) custom-call(bf16[224,16,128]{2,1,0:T(8,128)(2,1)} %copy-done.2, bf16[224,16,128]{2,1,0:T(8,128)(2,1)} %copy-done.3, bf16[110,16,128]{2,1,0:T(8,128)(2,1)} %copy-done, bf16[110,16,128]{2,1,0:T(8,128)(2,1)} %copy-done.1, f32[3,256,128]{2,1,0:T(8,128)} %bitcast.16, ...), custom_call_target="tpu_custom_call" | custom-call | flops 1000000 | bytes 1000000 | tf_op jit(solution)/shard_map/pallas_call | solution.py:424
Async XLA Ops:
  3.7 23.5 %collective-permute-start = (bf16[110,16,128]{2,1,0:T(8,128)(2,1)}, bf16[110,16,128]{2,1,0:T(8,128)(2,1)S(1)}, u32[]{:S(2)}, u32[]{:S(2)}) collective-permute-start(bf16[110,16,128]{2,1,0:T(8,128)(2,1)} %get-tuple-element.10), channel_id=1, source_target_pairs={{0,1},{1,0},{2,3},{3,2},{4,5},{5,4},{6,7},{7,6},{8,9},{9,8},{10,11... | collective-permute-start | bytes 1351688 | tf_op jit(solution)/shard_map/ppermute | solution.py:418
  7.2 20.1 %collective-permute-start.1 = (bf16[110,16,128]{2,1,0:T(8,128)(2,1)}, bf16[110,16,128]{2,1,0:T(8,128)(2,1)S(1)}, u32[]{:S(2)}, u32[]{:S(2)}) collective-permute-start(bf16[110,16,128]{2,1,0:T(8,128)(2,1)} %get-tuple-element.11), channel_id=1, source_target_pairs={{1,2},{2,1},{3,4},{4,3},{5,6},{6,5},{7,8},{8,7},{9,10},{10,9},{11,... | collective-permute-start | bytes 1351688 | tf_op jit(solution)/shard_map/ppermute | solution.py:419
  27.2 0.8 copy-start
  28.0 0.8 copy-start.1
  31.9 26.1 %collective-permute-start.2 = (bf16[224,16,128]{2,1,0:T(8,128)(2,1)}, bf16[224,16,128]{2,1,0:T(8,128)(2,1)S(1)}, u32[]{:S(2)}, u32[]{:S(2)}) collective-permute-start(bf16[224,16,128]{2,1,0:T(8,128)(2,1)} %get-tuple-element.12), channel_id=1, source_target_pairs={{0,16},{16,0},{32,48},{48,32},{64,80},{80,64},{96,112},{112,96},{1... | collective-permute-start | bytes 2752520 | tf_op jit(solution)/shard_map/ppermute | solution.py:418
  33.9 26.8 %collective-permute-start.3 = (bf16[224,16,128]{2,1,0:T(8,128)(2,1)}, bf16[224,16,128]{2,1,0:T(8,128)(2,1)S(1)}, u32[]{:S(2)}, u32[]{:S(2)}) collective-permute-start(bf16[224,16,128]{2,1,0:T(8,128)(2,1)} %get-tuple-element.13), channel_id=1, source_target_pairs={{16,32},{32,16},{48,64},{64,48},{80,96},{96,80},{112,128},{128,112... | collective-permute-start | bytes 2752520 | tf_op jit(solution)/shard_map/ppermute | solution.py:419
  58.0 2.7 %copy-start.2 = (bf16[224,16,128]{2,1,0:T(8,128)(2,1)}, bf16[224,16,128]{2,1,0:T(8,128)(2,1)S(1)}, u32[]{:S(2)}) copy-start(bf16[224,16,128]{2,1,0:T(8,128)(2,1)S(1)} %collective-permute-done.2.xa) | copy-start | bytes 2752516
  60.7 0.9 %copy-start.3 = (bf16[224,16,128]{2,1,0:T(8,128)(2,1)}, bf16[224,16,128]{2,1,0:T(8,128)(2,1)S(1)}, u32[]{:S(2)}) copy-start(bf16[224,16,128]{2,1,0:T(8,128)(2,1)S(1)} %collective-permute-done.3.xb) | copy-start | bytes 2752516

commit v2 on v1

--- a/solution.py
+++ b/solution.py
@@ -26,6 +26,11 @@
 CORN_AT = {qd: NFACE + i for i, qd in enumerate(CORN)}
 NCORN = len(CORN)
 SLOTS = 64
+UNROLL = 4
+FIRST = 61
+SECOND = 61
+FAR = (6, 3)
+NEAR = (5, 2)
 
 
 def vmem():
@@ -46,7 +51,17 @@
     return hi, (x - hi.astype(F32)).astype(BF16)
 
 
-def pack_y(v, s, b, l, m, out_a, out_b):
+def fetch(pairs, sems):
+    copies = [pltpu.make_async_copy(a, b, sems.at[i]) for i, (a, b) in enumerate(pairs)]
+    for copy in copies:
+        copy.start()
+    return copies
+
+
+def pack_y(v_in, s_in, b_in, l_in, m_in, out_a, out_b, v, s, b, l, m, sems):
+    copies = fetch([(s_in, s), (v_in, v), (b_in, b), (l_in, l), (m_in, m)], sems)
+    for copy in copies:
+        copy.wait()
     odd = lax.rem(lax.axis_index("gy"), 2)
     refs = (v, s, b, l, m)
     for out, high in ((out_a, odd == 0), (out_b, odd == 1)):
@@ -63,7 +78,11 @@
                     out[FACE_AT[q, d]] = rows.astype(BF16)
 
 
-def route(groups, hist, mech, res, owners, cells, out, vals):
+def route(groups, *refs):
+    given, out, held, vals, sems = refs[:5], refs[5], refs[6:11], refs[11], refs[12]
+    for copy in fetch(list(zip(given, held)), sems):
+        copy.wait()
+    hist, mech, res, owners, cells = held
     rows = hist.shape[0]
     nt = (((1,), (1,)), ((), ()))
     amp = lax.dot_general(res[...], hist[...], nt, preferred_element_type=F32)
@@ -111,10 +130,10 @@
         out[o, 16:32, :] = mine.astype(BF16)
 
 
-def pack_x(ya, yb, v, s, b, l, m, lists, out_a, out_b):
+def pack_x(ya, yb, v, s, mats, lists, out_a, out_b):
     odd_x = lax.rem(lax.axis_index("gx"), 2)
     odd_y = lax.rem(lax.axis_index("gy"), 2)
-    refs = (v, s, b, l, m)
+    refs = (v, s, mats.at[0], mats.at[1], mats.at[2])
     for out, high in ((out_a, odd_x == 0), (out_b, odd_x == 1)):
         for q in range(NQ):
             src = part(refs, q)
@@ -173,9 +192,9 @@
 NT = (((1,), (1,)), ((), ()))
 
 
-def place(planes, levels, values, row):
-    a = planes * values[row : row + 1, :]
-    return lax.dot_general(a, levels, NT, preferred_element_type=F32)
+def place(parts, values, levels):
+    a = [p * values[r + c : r + c + 1, :] for p, r in parts for c in range(6)]
+    return lax.dot_general(jnp.concatenate(a, axis=0), levels, NT, preferred_element_type=F32)
 
 
 def sided(groups, sides):
@@ -196,15 +215,18 @@
     levels = one_hot(first[13:14, :].astype(I32), Z)
     first, last = first.astype(BF16), last.astype(BF16)
     for t in range(3):
+        vals, row = (first, 6 * t) if t < 2 else (last, 0)
+        spread = [levels * vals[row + c : row + c + 1, :] for c in range(6)]
+        got = lax.dot_general(planes, jnp.concatenate(spread, axis=0), NT, preferred_element_type=F32)
         for c in range(6):
-            vals, row = (first, 6 * t + c) if t < 2 else (last, c)
-            out_own[6 * t + c] = place(planes, levels, vals, row)
+            out_own[6 * t + c] = got[:, Z * c : Z * c + Z]
     sides = lanes([lists[g, 0:16, :].astype(F32) for g in range(groups)])
     x, row, levels = sided(groups, sides)
     planes = one_hot(x * 8 + row, 8 * N)
     sides = sides.astype(BF16)
+    got = place(((planes, 0), (planes, 6)), sides, levels)
     for k in range(12):
-        out_side[k] = place(planes, levels, sides, k)
+        out_side[k] = got[8 * N * k : 8 * N * k + 8 * N]
 
 
 def roll_z(f, k, lane):
@@ -213,10 +235,10 @@
     return jnp.where(keep, moved, 0.0)
 
 
-def advance(xa, xb, ya, yb, v, s, b, l, m, own, side, vout, sout, ev, es, eb, el, em):
+def advance(xa, xb, ya, yb, v, s, mats, own, side, vout, sout, ev, es, eb, el, em, beyond, corner):
     odd_x = lax.rem(lax.axis_index("gx"), 2)
     odd_y = lax.rem(lax.axis_index("gy"), 2)
-    refs = (v, s, b, l, m)
+    refs = (v, s, mats.at[0], mats.at[1], mats.at[2])
     ext = (ev, es, eb, el, em)
 
     def at(x, y):
@@ -264,59 +286,54 @@
         def _():
             put(one, two)
 
+    def total(terms):
+        near = far = None
+        for g, fwd in terms:
+            k = 0 if fwd else -1
+            p, q = g(1 + k) - g(k), g(2 + k) - g(k - 1)
+            near, far = (p, q) if near is None else (near + p, far + q)
+        return INNER * near + OUTER * far
+
+    def reader(ref, x, y0, n):
+        base = pl.multiple_of(x * YE, 8)
+
+        def along_x(c):
+            return lambda k: ref[c, pl.ds(base + (k * YE + y0), n), :]
+
+        def along_y(c):
+            return lambda k: ref[c, pl.ds(base + (y0 + k), n), :]
+
+        def along_z(c):
+            f = ref[c, pl.ds(base + y0, n), :]
+            lane = lax.broadcasted_iota(I32, (n, Z), 1)
+            return lambda k: f if k == 0 else roll_z(f, k, lane)
+
+        return along_x, along_y, along_z, pl.ds(base + y0, n)
+
     def velocity_at(x, y0, n):
-        base = x * YE
-        lane = lax.broadcasted_iota(I32, (n, Z), 1)
-
-        def st(c, dx=0, dy=0):
-            return es[c, pl.ds(base + (dx * YE + y0 + dy), n), :]
-
-        def dif(g, fwd):
-            k = 0 if fwd else -1
-            return INNER * (g(1 + k) - g(k)) + OUTER * (g(2 + k) - g(k - 1))
-
-        def along_z(f):
-            return lambda k: f if k == 0 else roll_z(f, k, lane)
-
-        buoy = eb[pl.ds(base + y0, n), :]
-        fx = dif(lambda k: st(0, dx=k), True) + dif(lambda k: st(3, dy=k), False)
-        fx = fx + dif(along_z(st(4)), False)
-        fy = dif(lambda k: st(3, dx=k), False) + dif(lambda k: st(1, dy=k), True)
-        fy = fy + dif(along_z(st(5)), False)
-        fz = dif(lambda k: st(4, dx=k), False) + dif(lambda k: st(5, dy=k), False)
-        fz = fz + dif(along_z(st(2)), True)
-        for c, f in enumerate((fx, fy, fz)):
-            here = pl.ds(base + y0, n)
+        ax, ay, az, here = reader(es, x, y0, n)
+        buoy = eb[here, :]
+        forces = (
+            total(((ax(0), True), (ay(3), False), (az(4), False))),
+            total(((ax(3), False), (ay(1), True), (az(5), False))),
+            total(((ax(4), False), (ay(5), False), (az(2), True))),
+        )
+        for c, f in enumerate(forces):
             ev[c, here, :] = ev[c, here, :] + buoy * f
 
     def stress_at(x, y0, n):
-        base = x * YE
-        lane = lax.broadcasted_iota(I32, (n, Z), 1)
-
-        def ve(c, dx=0, dy=0):
-            return ev[c, pl.ds(base + (dx * YE + y0 + dy), n), :]
-
-        def dif(g, fwd):
-            k = 0 if fwd else -1
-            return INNER * (g(1 + k) - g(k)) + OUTER * (g(2 + k) - g(k - 1))
-
-        def along_z(f):
-            return lambda k: f if k == 0 else roll_z(f, k, lane)
-
-        here = pl.ds(base + y0, n)
+        ax, ay, az, here = reader(ev, x, y0, n)
         lam, rig = el[here, :], em[here, :]
-        d1 = dif(lambda k: ve(0, dx=k), False)
-        d2 = dif(lambda k: ve(1, dy=k), False)
-        d3 = dif(along_z(ve(2)), False)
+        d1, d2, d3 = total(((ax(0), False),)), total(((ay(1), False),)), total(((az(2), False),))
         e = lam * (d1 + d2 + d3)
         two = 2.0 * rig
         rates = (
             e + two * d1,
             e + two * d2,
             e + two * d3,
-            rig * (dif(lambda k: ve(0, dy=k), True) + dif(lambda k: ve(1, dx=k), True)),
-            rig * (dif(along_z(ve(0)), True) + dif(lambda k: ve(2, dx=k), True)),
-            rig * (dif(along_z(ve(1)), True) + dif(lambda k: ve(2, dy=k), True)),
+            rig * total(((ay(0), True), (ax(1), True))),
+            rig * total(((az(0), True), (ax(2), True))),
+            rig * total(((az(1), True), (ay(2), True))),
         )
         for c, r in enumerate(rates):
             es[c, here, :] = es[c, here, :] + r
@@ -326,7 +343,7 @@
             fn(x, y0, n)
             return carry
 
-        lax.fori_loop(XO - reach, XO + N + reach, step, 0)
+        lax.fori_loop(XO - reach, XO + N + reach, step, 0, unroll=UNROLL)
 
     def add(c, x, y, rows):
         here = slice(at(x, y), at(x, y) + rows.shape[0])
@@ -344,57 +361,69 @@
                 add(c, XO + x, YO - 8, side[6 * t + c, rows, 0:Z])
                 add(c, XO + x, YO + N, side[6 * t + c, rows, Z : 2 * Z])
 
-    def add_beyond(t, far):
+    def place_beyond():
         groups = (xa.shape[0] - NFACE - NCORN) // 2
         base = NFACE + NCORN
 
-        def one(msg, up):
+        def one(msg, up, k):
             first, _ = own_lists(lambda g: msg[base + 2 * g + 1].astype(F32), groups)
             plane = first[12:13, :].astype(I32)
             levels = one_hot(first[13:14, :].astype(I32), Z)
             x, y = plane // N, plane % N
-            i = x if up else x - (N - far)
-            planes = one_hot(jnp.where(i >= 0, i * N + y, -1), far * N)
-            first = first.astype(BF16)
-            x0 = XO + N if up else XO - far
-            for c in range(6):
-                got = place(planes, levels, first, 6 * t + c)
-                for k in range(far):
-                    add(c, x0 + k, YO, got[N * k : N * k + N])
-            near = 5 if t == 0 else 2
+
+            def faces(far):
+                i = x if up else x - (N - far)
+                return one_hot(jnp.where(i >= 0, i * N + y, -1), far * N)
+
+            parts = ((faces(FAR[0]), 0), (faces(FAR[1]), 6))
+            beyond[k] = place(parts, first.astype(BF16), levels)
             sides = lanes([msg[base + 2 * g].astype(F32) for g in range(groups)])
-            x, row, levels = sided(groups, sides)
-            i = x if up else x - (N - near)
-            planes = one_hot(jnp.where(i >= 0, i * 8 + row, -1), 8 * near)
-            sides = sides.astype(BF16)
-            x0 = XO + N if up else XO - near
-            for c in range(6):
-                got = place(planes, levels, sides, 6 * t + c)
-                for k in range(near):
-                    add(c, x0 + k, YO - 8, got[8 * k : 8 * k + 8, 0:Z])
-                    add(c, x0 + k, YO + N, got[8 * k : 8 * k + 8, Z : 2 * Z])
+            sx, row, levels = sided(groups, sides)
+
+            def edges(near):
+                i = sx if up else sx - (N - near)
+                return one_hot(jnp.where(i >= 0, i * 8 + row, -1), 8 * near)
+
+            parts = ((edges(NEAR[0]), 0), (edges(NEAR[1]), 6))
+            corner[k] = place(parts, sides.astype(BF16), levels)
 
         @pl.when(odd_x == 0)
         def _():
-            one(xb, False)
-            one(xa, True)
+            one(xb, False, 0)
+            one(xa, True, 1)
 
         @pl.when(odd_x == 1)
         def _():
-            one(xa, False)
-            one(xb, True)
-
+            one(xa, False, 0)
+            one(xb, True, 1)
+
+    def add_beyond(t):
+        far, near = FAR[t], NEAR[t]
+        f0, n0 = (0, 0) if t == 0 else (6 * N * FAR[0], 6 * 8 * NEAR[0])
+        for k in range(2):
+            for c in range(6):
+                x0 = XO + N if k else XO - far
+                for i in range(far):
+                    r = f0 + N * (c * far + i)
+                    add(c, x0 + i, YO, beyond[k, r : r + N, :])
+                x0 = XO + N if k else XO - near
+                for i in range(near):
+                    r = n0 + 8 * (c * near + i)
+                    add(c, x0 + i, YO - 8, corner[k, r : r + 8, 0:Z])
+                    add(c, x0 + i, YO + N, corner[k, r : r + 8, Z : 2 * Z])
+
+    place_beyond()
     sweep(velocity_at, 8, 8, 32)
     sweep(stress_at, 6, 8, 32)
     add_own(0)
     add_side(0)
-    add_beyond(0, 6)
+    add_beyond(0)
     sweep(velocity_at, 5, 8, 32)
-    sweep(stress_at, 3, 8, 32)
+    sweep(stress_at, 3, 13, 24)
     add_own(1)
     add_side(1)
-    add_beyond(1, 3)
-    sweep(velocity_at, 2, 8, 32)
+    add_beyond(1)
+    sweep(velocity_at, 2, 14, 24)
     sweep(stress_at, 0, 16, 16)
     for x in range(N):
         here = slice(at(XO + x, YO), at(XO + x, YO) + N)
@@ -405,6 +434,13 @@
             sout[c, rows, :] = es[c, here, :] + own[12 + c, rows, :]
 
 
+SCRATCH = [pltpu.VMEM((n, XE * YE, Z), F32) for n in (3, 6)] + [pltpu.VMEM((XE * YE, Z), F32)] * 3
+SCRATCH += [
+    pltpu.VMEM((2, 6 * N * (FAR[0] + FAR[1]), Z), F32),
+    pltpu.VMEM((2, 6 * 8 * (NEAR[0] + NEAR[1]), 2 * Z), F32),
+]
+
+
 def swaps(count, first):
     pairs = []
     for i in range(first, count - 1, 2):
@@ -420,14 +456,17 @@
     )
 
 
-def call(kernel, outs, args, scratch=(), flops=1_000_000):
+def call(kernel, outs, args, scratch=(), flops=1_000_000, mib=8, here=True):
+    if not here:
+        held = [pltpu.VMEM(a.shape, a.dtype) for a in args]
+        scratch = held + list(scratch) + [pltpu.SemaphoreType.DMA((len(args),))]
     return pl.pallas_call(
         kernel,
         out_shape=[jax.ShapeDtypeStruct(s, t) for s, t in outs],
-        in_specs=[vmem()] * len(args),
+        in_specs=[vmem() if here else pl.BlockSpec(memory_space=pltpu.HBM)] * len(args),
         out_specs=[vmem()] * len(outs),
         scratch_shapes=list(scratch),
-        compiler_params=pltpu.CompilerParams(vmem_limit_bytes=56 * 1024 * 1024),
+        compiler_params=pltpu.CompilerParams(vmem_limit_bytes=mib * 1024 * 1024),
         cost_estimate=pl.CostEstimate(flops=flops, bytes_accessed=1_000_000, transcendentals=0),
     )(*args)
 
@@ -438,8 +477,10 @@
     s = stresses.reshape(6, N * N, Z)
     b, l, m = (a.reshape(N * N, Z) for a in (buoyancy, lame, rigidity))
     state = (v, s, b, l, m)
+    mats = jnp.stack([b, l, m])
+    later = (v, s, mats)
     face = ((NFACE, N, Z), BF16)
-    ya, yb = call(pack_y, [face, face], state)
+    ya, yb = call(pack_y, [face, face], state, here=False, mib=FIRST)
     ya, yb = swap_both(ya, yb, "gy")
     rows = hist.shape[0]
     (sent,) = call(
@@ -447,23 +488,26 @@
         [((groups, 32, 128), BF16)],
         (hist, mech.T, res.T, owners.reshape(1, rows), cells.reshape(1, rows)),
         [pltpu.VMEM((32, rows), F32)],
+        here=False,
+        mib=SECOND,
     )
     lists = lax.all_to_all(sent, "gy", split_axis=0, concat_axis=0, tiled=True)
     whole = ((NFACE + NCORN + 2 * groups, N, Z), BF16)
-    xa, xb = call(pack_x, [whole, whole], (ya, yb) + state + (lists,))
+    xa, xb = call(pack_x, [whole, whole], (ya, yb) + later + (lists,))
     xa, xb = swap_both(xa, xb, "gx")
     own, side = call(
         place_own,
         [((18, N * N, Z), F32), ((12, 8 * N, 2 * Z), F32)],
         (lists,),
         flops=10_000_000_000,
+        mib=24,
     )
-    block = pltpu.VMEM((XE * YE, Z), F32)
     vout, sout = call(
         advance,
         [(v.shape, F32), (s.shape, F32)],
-        (xa, xb, ya, yb) + state + (own, side),
-        [pltpu.VMEM((3, XE * YE, Z), F32), pltpu.VMEM((6, XE * YE, Z), F32), block, block, block],
+        (xa, xb, ya, yb) + later + (own, side),
+        SCRATCH,
+        mib=32,
     )
     return vout.reshape(velocity.shape), sout.reshape(stresses.shape)
 

time: 93.4 us -> 68.7 us (0.74)
  Pallas kernels: 48.5 us -> 21.1 us
  blocking collectives: 12.4 us -> 0 us
  waiting for transfers between devices: 2.66 us -> 14.4 us
  starting transfers between devices: 26.3 us -> 31.1 us
  local copies, waits for them, and re-layouts: 2.48 us -> 0.01 us
  other arithmetic: 0 us -> 1.06 us
    pallas_call x5, Pallas kernels: 48.5 us -> 21.1 us  [call(): pl.pallas_call(kernel, out_shape=[jax.ShapeDtypeStruct(s, t) for s, t in...]
    all_to_all x1 -> x0, blocking collectives: 12.4 us -> none  [local(): lists = lax.all_to_all(sent, 'gy', split_axis=0, concat_axis=0, tiled=True)]
    all_to_all x0 -> x1, waiting for transfers between devices: none -> 6.49 us  [local(): lists = lax.all_to_all(sent, 'gy', split_axis=0, concat_axis=0, tiled=True)]
    ppermute x2, waiting for transfers between devices: 2.65 us -> 7.89 us  [swap_both(): lax.ppermute(b, axis, swaps(count, 1))]
    all_to_all x0 -> x1, starting transfers between devices: none -> 4.75 us  [local(): lists = lax.all_to_all(sent, 'gy', split_axis=0, concat_axis=0, tiled=True)]
    unnamed x8 -> x4, local copies, waits for them, and re-layouts: 2.48 us -> 0.01 us
    another operation x0 -> x1, other arithmetic: none -> 1.06 us  [local(): mats = jnp.stack([b, l, m])]
  transfers between devices with their start and end apart: 4 -> 5, of which waited for: 1 -> 2; matrix products, arithmetic and copies ran while one was open for 0% -> 2% of each run, Pallas kernels for 12% -> 8%
where the time goes in v2:
time: 68.7 us; the launch traced here: 68.4 us
  starting transfers between devices  31.1 us (45%)
  Pallas kernels  21.1 us (31%)
  waiting for transfers between devices  14.4 us (21%)
  other arithmetic  1.06 us (2%)
  between operations  0.73 us (1%)
    pallas_call x5, Pallas kernels, call(): pl.pallas_call(kernel, out_shape=[jax.ShapeDtypeStruct(s, t) for s, t in...  21.1 us
    ppermute x2, starting transfers between devices, swap_both(): lax.ppermute(b, axis, swaps(count, 1))  20.9 us
    ppermute x2, waiting for transfers between devices, swap_both(): lax.ppermute(b, axis, swaps(count, 1))  7.89 us
    all_to_all x1, waiting for transfers between devices, local(): lists = lax.all_to_all(sent, 'gy', split_axis=0, concat_axis=0, tiled=True)  6.49 us
    ppermute x2, starting transfers between devices, swap_both(): lax.ppermute(a, axis, swaps(count, 0))  5.4 us
    all_to_all x1, starting transfers between devices, local(): lists = lax.all_to_all(sent, 'gy', split_axis=0, concat_axis=0, tiled=True)  4.75 us
  transfers between devices with their start and end apart: 5, of which 2 were waited for; matrix products, arithmetic and copies ran while one was open for 2% of the time, Pallas kernels for 8%

profile of v2, /device:TPU:6, one launch (start us, length us, event | category | flops | bytes accessed | tf_op | source)
XLA Modules:
  0.0 68.4 jit_solution(1929554287655647366)
XLA Ops:
  0.6 0.0 copy-start
  0.6 0.0 copy-start.1
  0.6 3.2 %shard_map.113 = (bf16[110,16,128]{2,1,0:T(8,128)(2,1)}, bf16[110,16,128]{2,1,0:T(8,128)(2,1)}) custom-call(f32[3,256,128]{2,1,0:T(8,128)} %bitcast.17, f32[6,256,128]{2,1,0:T(8,128)} %bitcast.14, f32[256,128]{1,0:T(8,128)} %bitcast.20, f32[256,128]{1,0:T(8,128)} %bitcast.22, f32[256,128]{1,0:T(8,128)} %bitcast.24), custom_call_target="tpu_custom_call" | custom-call | flops 1000000 | bytes 1000000 | tf_op jit(solution)/shard_map/pallas_call | solution.py:463
  3.9 3.5 %collective-permute-start = (bf16[110,16,128]{2,1,0:T(8,128)(2,1)}, bf16[110,16,128]{2,1,0:T(8,128)(2,1)S(1)}, u32[]{:S(2)}, u32[]{:S(2)}) collective-permute-start(bf16[110,16,128]{2,1,0:T(8,128)(2,1)} %get-tuple-element.10), channel_id=1, source_target_pairs={{0,1},{1,0},{2,3},{3,2},{4,5},{5,4},{6,7},{7,6},{8,9},{9,8},{10,11... | collective-permute-start | bytes 1351688 | tf_op jit(solution)/shard_map/ppermute | solution.py:454
  7.4 5.4 %collective-permute-start.1 = (bf16[110,16,128]{2,1,0:T(8,128)(2,1)}, bf16[110,16,128]{2,1,0:T(8,128)(2,1)S(1)}, u32[]{:S(2)}, u32[]{:S(2)}) collective-permute-start(bf16[110,16,128]{2,1,0:T(8,128)(2,1)} %get-tuple-element.11), channel_id=1, source_target_pairs={{1,2},{2,1},{3,4},{4,3},{5,6},{6,5},{7,8},{8,7},{9,10},{10,9},{11,... | collective-permute-start | bytes 1351688 | tf_op jit(solution)/shard_map/ppermute | solution.py:455
  12.8 2.3 %shard_map.114 = bf16[16,32,128]{2,1,0:T(8,128)(2,1)} custom-call(bf16[256,512]{1,0:T(8,128)(2,1)} %refs_0_.1, bf16[6,256]{1,0:T(8,128)(2,1)} %bitcast.26, bf16[3,512]{1,0:T(4,128)(2,1)} %bitcast.27, s32[1,256]{1,0:T(1,128)} %bitcast.28, s32[1,256]{1,0:T(1,128)} %bitcast.29), custom_call_target="tpu_custom_call" | custom-call | flops 1000000 | bytes 1000000 | tf_op jit(solution)/shard_map/pallas_call | solution.py:463
  15.1 4.7 %all-to-all-start = ((bf16[16,32,128]{2,1,0:T(8,128)(2,1)}), bf16[16,32,128]{2,1,0:T(8,128)(2,1)S(1)}, u32[]{:S(2)}, u32[]{:S(2)}) async-start(bf16[16,32,128]{2,1,0:T(8,128)(2,1)} %shard_map.114), calls=%async_computation | async-start | bytes 262144 | tf_op jit(solution)/shard_map/all_to_all | solution.py:494
  19.8 1.1 %pad_maximum_fusion.mats = f32[3,256,128]{2,1,0:T(8,128)S(1)} fusion(f32[1,256,128]{2,1,0:T(8,128)} %bitcast.25, f32[1,256,128]{2,1,0:T(8,128)} %bitcast.23, f32[1,256,128]{2,1,0:T(8,128)} %bitcast.21), kind=kLoop, calls=%fused_computation | loop fusion | flops 196608 | bytes 786432 | tf_op jit(solution)/shard_map/stack | solution.py:480
  20.9 6.5 %all-to-all-done.lists = bf16[16,32,128]{2,1,0:T(8,128)(2,1)S(1)} async-done(((bf16[16,32,128]{2,1,0:T(8,128)(2,1)}), bf16[16,32,128]{2,1,0:T(8,128)(2,1)S(1)}, u32[]{:S(2)}, u32[]{:S(2)}) %all-to-all-start) | async-done | bytes 131104 | tf_op jit(solution)/shard_map/all_to_all | solution.py:494
  27.4 0.0 collective-permute-done.ya
  27.4 0.0 collective-permute-done.1.yb
  27.4 0.0 copy-done
  27.4 0.0 copy-done.1
  27.4 0.3 shard_map.115
  27.7 1.9 %collective-permute-start.2 = (bf16[224,16,128]{2,1,0:T(8,128)(2,1)S(1)}, bf16[224,16,128]{2,1,0:T(8,128)(2,1)S(1)}, u32[]{:S(2)}, u32[]{:S(2)}) collective-permute-start(bf16[224,16,128]{2,1,0:T(8,128)(2,1)S(1)} %get-tuple-element.12), channel_id=1, source_target_pairs={{0,16},{16,0},{32,48},{48,32},{64,80},{80,64},{96,112},{112,96},{1... | collective-permute-start | bytes 2752520 | tf_op jit(solution)/shard_map/ppermute | solution.py:454
  29.6 15.5 %collective-permute-start.3 = (bf16[224,16,128]{2,1,0:T(8,128)(2,1)S(1)}, bf16[224,16,128]{2,1,0:T(8,128)(2,1)S(1)}, u32[]{:S(2)}, u32[]{:S(2)}) collective-permute-start(bf16[224,16,128]{2,1,0:T(8,128)(2,1)S(1)} %get-tuple-element.13), channel_id=1, source_target_pairs={{16,32},{32,16},{48,64},{64,48},{80,96},{96,80},{112,128},{128,112... | collective-permute-start | bytes 2752520 | tf_op jit(solution)/shard_map/ppermute | solution.py:455
  45.1 3.2 %shard_map.116 = (f32[18,256,128]{2,1,0:T(8,128)S(1)}, f32[12,128,256]{2,1,0:T(8,128)S(1)}) custom-call(bf16[16,32,128]{2,1,0:T(8,128)(2,1)S(1)} %all-to-all-done.lists), custom_call_target="tpu_custom_call" | custom-call | flops 10000000000 | bytes 1000000 | tf_op jit(solution)/shard_map/pallas_call | solution.py:463
  48.3 0.0 collective-permute-done.2.xa
  48.3 7.9 %collective-permute-done.3.xb = bf16[224,16,128]{2,1,0:T(8,128)(2,1)S(1)} collective-permute-done((bf16[224,16,128]{2,1,0:T(8,128)(2,1)S(1)}, bf16[224,16,128]{2,1,0:T(8,128)(2,1)S(1)}, u32[]{:S(2)}, u32[]{:S(2)}) %collective-permute-start.3) | collective-permute-done | bytes 917536 | tf_op jit(solution)/shard_map/ppermute | solution.py:455
  56.2 12.2 %shard_map.117 = (f32[3,256,128]{2,1,0:T(8,128)}, f32[6,256,128]{2,1,0:T(8,128)}) custom-call(bf16[224,16,128]{2,1,0:T(8,128)(2,1)S(1)} %collective-permute-done.2.xa, bf16[224,16,128]{2,1,0:T(8,128)(2,1)S(1)} %collective-permute-done.3.xb, bf16[110,16,128]{2,1,0:T(8,128)(2,1)S(1)} %collective-permute-done.ya, ...), custom_call_target="tpu_custom_call" | custom-call | flops 1000000 | bytes 1000000 | tf_op jit(solution)/shard_map/pallas_call | solution.py:463
Async XLA Ops:
  0.6 26.7 %copy-start = (f32[6,16,16,128]{3,2,1,0:T(8,128)S(1)}, f32[6,16,16,128]{3,2,1,0:T(8,128)}, u32[]{:S(2)}) copy-start(f32[6,16,16,128]{3,2,1,0:T(8,128)} %param.11) | copy-start | bytes 2359300
  0.6 26.7 %copy-start.1 = (f32[3,16,16,128]{3,2,1,0:T(8,128)S(1)}, f32[3,16,16,128]{3,2,1,0:T(8,128)}, u32[]{:S(2)}) copy-start(f32[3,16,16,128]{3,2,1,0:T(8,128)} %param.10) | copy-start | bytes 1179652
  3.9 23.5 %collective-permute-start = (bf16[110,16,128]{2,1,0:T(8,128)(2,1)}, bf16[110,16,128]{2,1,0:T(8,128)(2,1)S(1)}, u32[]{:S(2)}, u32[]{:S(2)}) collective-permute-start(bf16[110,16,128]{2,1,0:T(8,128)(2,1)} %get-tuple-element.10), channel_id=1, source_target_pairs={{0,1},{1,0},{2,3},{3,2},{4,5},{5,4},{6,7},{7,6},{8,9},{9,8},{10,11... | collective-permute-start | bytes 1351688 | tf_op jit(solution)/shard_map/ppermute | solution.py:454
  7.4 20.0 %collective-permute-start.1 = (bf16[110,16,128]{2,1,0:T(8,128)(2,1)}, bf16[110,16,128]{2,1,0:T(8,128)(2,1)S(1)}, u32[]{:S(2)}, u32[]{:S(2)}) collective-permute-start(bf16[110,16,128]{2,1,0:T(8,128)(2,1)} %get-tuple-element.11), channel_id=1, source_target_pairs={{1,2},{2,1},{3,4},{4,3},{5,6},{6,5},{7,8},{8,7},{9,10},{10,9},{11,... | collective-permute-start | bytes 1351688 | tf_op jit(solution)/shard_map/ppermute | solution.py:455
  15.1 12.3 %all-to-all-start = ((bf16[16,32,128]{2,1,0:T(8,128)(2,1)}), bf16[16,32,128]{2,1,0:T(8,128)(2,1)S(1)}, u32[]{:S(2)}, u32[]{:S(2)}) async-start(bf16[16,32,128]{2,1,0:T(8,128)(2,1)} %shard_map.114), calls=%async_computation | async-start | bytes 262144 | tf_op jit(solution)/shard_map/all_to_all | solution.py:494
  27.7 20.6 %collective-permute-start.2 = (bf16[224,16,128]{2,1,0:T(8,128)(2,1)S(1)}, bf16[224,16,128]{2,1,0:T(8,128)(2,1)S(1)}, u32[]{:S(2)}, u32[]{:S(2)}) collective-permute-start(bf16[224,16,128]{2,1,0:T(8,128)(2,1)S(1)} %get-tuple-element.12), channel_id=1, source_target_pairs={{0,16},{16,0},{32,48},{48,32},{64,80},{80,64},{96,112},{112,96},{1... | collective-permute-start | bytes 2752520 | tf_op jit(solution)/shard_map/ppermute | solution.py:454
  29.6 26.6 %collective-permute-start.3 = (bf16[224,16,128]{2,1,0:T(8,128)(2,1)S(1)}, bf16[224,16,128]{2,1,0:T(8,128)(2,1)S(1)}, u32[]{:S(2)}, u32[]{:S(2)}) collective-permute-start(bf16[224,16,128]{2,1,0:T(8,128)(2,1)S(1)} %get-tuple-element.13), channel_id=1, source_target_pairs={{16,32},{32,16},{48,64},{64,48},{80,96},{96,80},{112,128},{128,112... | collective-permute-start | bytes 2752520 | tf_op jit(solution)/shard_map/ppermute | solution.py:455

commit v3 on v2

--- a/solution.py
+++ b/solution.py
@@ -12,9 +12,9 @@
 N = 16
 Z = 128
 XO = 11
-XE = XO + N + XO
+XE = XO + N + 10
 YO = 16
-YE = 48
+YE = 40
 DEPTH = [9] * 6 + [8] * 3 + [8, 6, 6]
 CORNER = [8] * 6 + [6] * 3 + [6, 5, 5]
 NQ = len(DEPTH)
@@ -22,13 +22,16 @@
 FACE_AT = {qd: i for i, qd in enumerate(FACE)}
 LOW_AT = {q: len(FACE) + q for q in range(NQ)}
 NFACE = len(FACE) + NQ
-CORN = [(q, d) for q in range(NQ) for d in range(1, CORNER[q] + 1)]
-CORN_AT = {qd: NFACE + i for i, qd in enumerate(CORN)}
+PACKED = {
+    8: ((1, 0, 0), (2, 0, 0), (3, 7, 2), (4, 6, 3), (5, 8, 2)),
+    6: ((1, 6, 2), (2, 0, 0), (3, 4, 3), (5, 0, 0)),
+    5: ((1, 3, 3), (2, 4, 2), (5, 0, 0)),
+}
+CORN = [(q,) + unit for q in range(NQ) for unit in PACKED[CORNER[q]]]
 NCORN = len(CORN)
 SLOTS = 64
-UNROLL = 4
+UNROLL = {8: 8, 6: 7, 5: 13, 3: 11, 2: 10, 0: 8}
 FIRST = 61
-SECOND = 61
 FAR = (6, 3)
 NEAR = (5, 2)
 
@@ -58,10 +61,18 @@
     return copies
 
 
-def pack_y(v_in, s_in, b_in, l_in, m_in, out_a, out_b, v, s, b, l, m, sems):
-    copies = fetch([(s_in, s), (v_in, v), (b_in, b), (l_in, l), (m_in, m)], sems)
-    for copy in copies:
+def opening(groups, *refs):
+    given, (out_a, out_b, sent), held, vals, sems = refs[:10], refs[10:13], refs[13:23], refs[23], refs[24]
+    copies = fetch(list(zip(given, held)), sems)
+    for copy in copies[5:]:
         copy.wait()
+    route(groups, *held[5:], sent, vals)
+    for copy in copies[:5]:
+        copy.wait()
+    pack_y(*held[:5], out_a, out_b)
+
+
+def pack_y(v, s, b, l, m, out_a, out_b):
     odd = lax.rem(lax.axis_index("gy"), 2)
     refs = (v, s, b, l, m)
     for out, high in ((out_a, odd == 0), (out_b, odd == 1)):
@@ -78,11 +89,7 @@
                     out[FACE_AT[q, d]] = rows.astype(BF16)
 
 
-def route(groups, *refs):
-    given, out, held, vals, sems = refs[:5], refs[5], refs[6:11], refs[11], refs[12]
-    for copy in fetch(list(zip(given, held)), sems):
-        copy.wait()
-    hist, mech, res, owners, cells = held
+def route(groups, hist, mech, res, owners, cells, out, vals):
     rows = hist.shape[0]
     nt = (((1,), (1,)), ((), ()))
     amp = lax.dot_general(res[...], hist[...], nt, preferred_element_type=F32)
@@ -130,11 +137,10 @@
         out[o, 16:32, :] = mine.astype(BF16)
 
 
-def pack_x(ya, yb, v, s, mats, lists, out_a, out_b):
-    odd_x = lax.rem(lax.axis_index("gx"), 2)
-    odd_y = lax.rem(lax.axis_index("gy"), 2)
+def pack_x(v, s, mats, out_a, out_b):
+    odd = lax.rem(lax.axis_index("gx"), 2)
     refs = (v, s, mats.at[0], mats.at[1], mats.at[2])
-    for out, high in ((out_a, odd_x == 0), (out_b, odd_x == 1)):
+    for out, high in ((out_a, odd == 0), (out_b, odd == 1)):
         for q in range(NQ):
             src = part(refs, q)
             for d in range(1, DEPTH[q] + 1):
@@ -146,19 +152,32 @@
                     out[LOW_AT[q]] = lo
                 else:
                     out[FACE_AT[q, d]] = rows.astype(BF16)
-        groups = lists.shape[0]
+
+
+def pack_corners(ya, yb, lists, out_a, out_b):
+    odd_x = lax.rem(lax.axis_index("gx"), 2)
+    odd_y = lax.rem(lax.axis_index("gy"), 2)
+    groups = lists.shape[0]
+    for out in (out_a, out_b):
         for g in range(groups):
             for h in range(2):
-                out[NFACE + NCORN + 2 * g + h] = lists[g, 16 * h : 16 * h + 16, :]
+                out[NCORN + 2 * g + h] = lists[g, 16 * h : 16 * h + 16, :]
 
     def corners(low, top, out, high):
-        for q, d in CORN:
-            i = FACE_AT[q, d]
-            a = low[i].astype(F32)
-            c = top[i].astype(F32)
-            k = 8 if high else 0
-            both = jnp.concatenate([a[k : k + 8], c[k : k + 8]], axis=0)
-            out[CORN_AT[q, d]] = both.astype(BF16)
+        row = lax.broadcasted_iota(I32, (8, Z), 0)
+        k = 8 if high else 0
+        for i, (q, d, far, m) in enumerate(CORN):
+            halves = []
+            for msg in (low, top):
+                a = msg[FACE_AT[q, d]].astype(F32)[k : k + 8]
+                if far:
+                    c = msg[FACE_AT[q, far]].astype(F32)[k : k + 8]
+                    if high:
+                        a = jnp.where(row < m, pltpu.roll(c, m, 0), a)
+                    else:
+                        a = jnp.where(row >= 8 - m, pltpu.roll(c, 8 - m, 0), a)
+                halves.append(a)
+            out[i] = jnp.concatenate(halves, axis=0).astype(BF16)
 
     for px in range(2):
         for py in range(2):
@@ -235,7 +254,7 @@
     return jnp.where(keep, moved, 0.0)
 
 
-def advance(xa, xb, ya, yb, v, s, mats, own, side, vout, sout, ev, es, eb, el, em, beyond, corner):
+def advance(xa, xb, ca, cb, ya, yb, v, s, mats, own, side, vout, sout, ev, es, eb, el, em, beyond, corner):
     odd_x = lax.rem(lax.axis_index("gx"), 2)
     odd_y = lax.rem(lax.axis_index("gy"), 2)
     refs = (v, s, mats.at[0], mats.at[1], mats.at[2])
@@ -263,20 +282,29 @@
                 dst[pl.ds(at(XO, YO + N - 1 + d), N, stride=YE), :] = layer(top, q, d)
 
     def put_x(low, top):
-        groups = (low.shape[0] - NFACE - NCORN) // 2
         for q in range(NQ):
             dst = part(ext, q)
             for d in range(1, DEPTH[q] + 1):
                 for msg, x in ((low, XO - d), (top, XO + N - 1 + d)):
                     dst[at(x, YO) : at(x, YO) + N, :] = layer(msg, q, d)
-            for d in range(1, CORNER[q] + 1):
-                for msg, x in ((low, XO - 8), (top, XO + N)):
-                    both = msg[CORN_AT[q, d]].astype(F32)
-                    dst[pl.ds(at(x, YO - d), 8, stride=YE), :] = both[0:8]
-                    dst[pl.ds(at(x, YO + N - 1 + d), 8, stride=YE), :] = both[8:16]
-        return groups
-
-    for odd, put, one, two in ((odd_y, put_y, ya, yb), (odd_x, put_x, xa, xb)):
+
+    def put_corners(low, top):
+        for i, (q, d, far, m) in enumerate(CORN):
+            dst = part(ext, q)
+            for msg, x, back in ((low, XO - 8, 8 - m), (top, XO + N, m)):
+                both = msg[i].astype(F32)
+                for h in range(2):
+                    rows = both[8 * h : 8 * h + 8]
+
+                    def put(depth, rows):
+                        y = YO + N - 1 + depth if h else YO - depth
+                        dst[pl.ds(at(x, y), 8, stride=YE), :] = rows
+
+                    put(d, rows)
+                    if far:
+                        put(far, pltpu.roll(rows, back, 0))
+
+    for odd, put, one, two in ((odd_y, put_y, ya, yb), (odd_x, put_x, xa, xb), (odd_x, put_corners, ca, cb)):
 
         @pl.when(odd == 0)
         def _():
@@ -343,7 +371,7 @@
             fn(x, y0, n)
             return carry
 
-        lax.fori_loop(XO - reach, XO + N + reach, step, 0, unroll=UNROLL)
+        lax.fori_loop(XO - reach, XO + N + reach, step, 0, unroll=UNROLL[reach])
 
     def add(c, x, y, rows):
         here = slice(at(x, y), at(x, y) + rows.shape[0])
@@ -362,8 +390,8 @@
                 add(c, XO + x, YO + N, side[6 * t + c, rows, Z : 2 * Z])
 
     def place_beyond():
-        groups = (xa.shape[0] - NFACE - NCORN) // 2
-        base = NFACE + NCORN
+        groups = (ca.shape[0] - NCORN) // 2
+        base = NCORN
 
         def one(msg, up, k):
             first, _ = own_lists(lambda g: msg[base + 2 * g + 1].astype(F32), groups)
@@ -389,13 +417,13 @@
 
         @pl.when(odd_x == 0)
         def _():
-            one(xb, False, 0)
-            one(xa, True, 1)
+            one(cb, False, 0)
+            one(ca, True, 1)
 
         @pl.when(odd_x == 1)
         def _():
-            one(xa, False, 0)
-            one(xb, True, 1)
+            one(ca, False, 0)
+            one(cb, True, 1)
 
     def add_beyond(t):
         far, near = FAR[t], NEAR[t]
@@ -480,21 +508,22 @@
     mats = jnp.stack([b, l, m])
     later = (v, s, mats)
     face = ((NFACE, N, Z), BF16)
-    ya, yb = call(pack_y, [face, face], state, here=False, mib=FIRST)
-    ya, yb = swap_both(ya, yb, "gy")
     rows = hist.shape[0]
-    (sent,) = call(
-        lambda *refs: route(groups, *refs),
-        [((groups, 32, 128), BF16)],
-        (hist, mech.T, res.T, owners.reshape(1, rows), cells.reshape(1, rows)),
+    ya, yb, sent = call(
+        lambda *refs: opening(groups, *refs),
+        [face, face, ((groups, 32, 128), BF16)],
+        state + (hist, mech.T, res.T, owners.reshape(1, rows), cells.reshape(1, rows)),
         [pltpu.VMEM((32, rows), F32)],
         here=False,
-        mib=SECOND,
+        mib=FIRST,
     )
+    ya, yb = swap_both(ya, yb, "gy")
     lists = lax.all_to_all(sent, "gy", split_axis=0, concat_axis=0, tiled=True)
-    whole = ((NFACE + NCORN + 2 * groups, N, Z), BF16)
-    xa, xb = call(pack_x, [whole, whole], (ya, yb) + later + (lists,))
+    xa, xb = call(pack_x, [face, face], later)
     xa, xb = swap_both(xa, xb, "gx")
+    rest = ((NCORN + 2 * groups, N, Z), BF16)
+    ca, cb = call(pack_corners, [rest, rest], (ya, yb, lists))
+    ca, cb = swap_both(ca, cb, "gx")
     own, side = call(
         place_own,
         [((18, N * N, Z), F32), ((12, 8 * N, 2 * Z), F32)],
@@ -505,9 +534,9 @@
     vout, sout = call(
         advance,
         [(v.shape, F32), (s.shape, F32)],
-        (xa, xb, ya, yb) + later + (own, side),
+        (xa, xb, ca, cb, ya, yb) + later + (own, side),
         SCRATCH,
-        mib=32,
+        mib=24,
     )
     return vout.reshape(velocity.shape), sout.reshape(stresses.shape)
 

time: 68.7 us -> 64.2 us (0.934)
  waiting for transfers between devices: 14.4 us -> 3.88 us
  starting transfers between devices: 31.1 us -> 38.1 us
  Pallas kernels: 21.1 us -> 19.9 us
    all_to_all x1, waiting for transfers between devices: 6.49 us -> 0.01 us  [local(): lists = lax.all_to_all(sent, 'gy', split_axis=0, concat_axis=0, tiled=True)]
    ppermute x2 -> x3, starting transfers between devices: 20.9 us -> 26.1 us  [swap_both(): lax.ppermute(b, axis, swaps(count, 1))]
    ppermute x2 -> x3, waiting for transfers between devices: 7.89 us -> 3.87 us  [swap_both(): lax.ppermute(b, axis, swaps(count, 1))]
    ppermute x2 -> x3, starting transfers between devices: 5.4 us -> 7.31 us  [swap_both(): lax.ppermute(a, axis, swaps(count, 0))]
    pallas_call x5, Pallas kernels: 21.1 us -> 19.9 us  [call(): pl.pallas_call(kernel, out_shape=[jax.ShapeDtypeStruct(s, t) for s, t in...]
  transfers between devices with their start and end apart: 5 -> 7, of which waited for: 2 -> 1; matrix products, arithmetic and copies ran while one was open for 2% -> 2% of each run, Pallas kernels for 8% -> 7%
where the time goes in v3:
time: 64.2 us; the launch traced here: 63.8 us
  starting transfers between devices  38.1 us (59%)
  Pallas kernels  19.9 us (31%)
  waiting for transfers between devices  3.88 us (6%)
  other arithmetic  1.06 us (2%)
  between operations  0.79 us (1%)
    ppermute x3, starting transfers between devices, swap_both(): lax.ppermute(b, axis, swaps(count, 1))  26.1 us
    pallas_call x5, Pallas kernels, call(): pl.pallas_call(kernel, out_shape=[jax.ShapeDtypeStruct(s, t) for s, t in...  19.9 us
    ppermute x3, starting transfers between devices, swap_both(): lax.ppermute(a, axis, swaps(count, 0))  7.31 us
    all_to_all x1, starting transfers between devices, local(): lists = lax.all_to_all(sent, 'gy', split_axis=0, concat_axis=0, tiled=True)  4.75 us
    ppermute x3, waiting for transfers between devices, swap_both(): lax.ppermute(b, axis, swaps(count, 1))  3.87 us
  transfers between devices with their start and end apart: 7, of which 1 were waited for; matrix products, arithmetic and copies ran while one was open for 2% of the time, Pallas kernels for 7%

profile of v3, /device:TPU:6, one launch (start us, length us, event | category | flops | bytes accessed | tf_op | source)
XLA Modules:
  0.0 63.8 jit_solution(18130805450428890010)
XLA Ops:
  0.6 0.0 copy-start
  0.6 0.0 copy-start.1
  0.7 4.0 %shard_map.114 = (bf16[110,16,128]{2,1,0:T(8,128)(2,1)}, bf16[110,16,128]{2,1,0:T(8,128)(2,1)}, bf16[16,32,128]{2,1,0:T(8,128)(2,1)}) custom-call(f32[3,256,128]{2,1,0:T(8,128)} %bitcast.17, f32[6,256,128]{2,1,0:T(8,128)} %bitcast.14, f32[256,128]{1,0:T(8,128)} %bitcast.24, f32[256,128]{1,0:T(8,128)} %bitcast.22, f32[256,128]{1,0:T(8,128)} %bitcast.20, ...), custom_call_target="tpu_custom_call" | custom-call | flops 1000000 | bytes 1000000 | tf_op jit(solution)/shard_map/pallas_call | solution.py:491
  4.7 3.5 %collective-permute-start.2 = (bf16[110,16,128]{2,1,0:T(8,128)(2,1)}, bf16[110,16,128]{2,1,0:T(8,128)(2,1)S(1)}, u32[]{:S(2)}, u32[]{:S(2)}) collective-permute-start(bf16[110,16,128]{2,1,0:T(8,128)(2,1)} %get-tuple-element.15), channel_id=1, source_target_pairs={{0,1},{1,0},{2,3},{3,2},{4,5},{5,4},{6,7},{7,6},{8,9},{9,8},{10,11... | collective-permute-start | bytes 1351688 | tf_op jit(solution)/shard_map/ppermute | solution.py:482
  8.2 5.4 %collective-permute-start.3 = (bf16[110,16,128]{2,1,0:T(8,128)(2,1)}, bf16[110,16,128]{2,1,0:T(8,128)(2,1)S(1)}, u32[]{:S(2)}, u32[]{:S(2)}) collective-permute-start(bf16[110,16,128]{2,1,0:T(8,128)(2,1)} %get-tuple-element.16), channel_id=1, source_target_pairs={{1,2},{2,1},{3,4},{4,3},{5,6},{6,5},{7,8},{8,7},{9,10},{10,9},{11,... | collective-permute-start | bytes 1351688 | tf_op jit(solution)/shard_map/ppermute | solution.py:483
  13.6 4.7 %all-to-all-start = ((bf16[16,32,128]{2,1,0:T(8,128)(2,1)}), bf16[16,32,128]{2,1,0:T(8,128)(2,1)S(1)}, u32[]{:S(2)}, u32[]{:S(2)}) async-start(bf16[16,32,128]{2,1,0:T(8,128)(2,1)} %get-tuple-element.17), calls=%async_computation | async-start | bytes 262144 | tf_op jit(solution)/shard_map/all_to_all | solution.py:521
  18.3 1.1 %pad_maximum_fusion.mats = f32[3,256,128]{2,1,0:T(8,128)S(1)} fusion(f32[1,256,128]{2,1,0:T(8,128)} %bitcast.21, f32[1,256,128]{2,1,0:T(8,128)} %bitcast.23, f32[1,256,128]{2,1,0:T(8,128)} %bitcast.25), kind=kLoop, calls=%fused_computation | loop fusion | flops 196608 | bytes 786432 | tf_op jit(solution)/shard_map/stack | solution.py:508
  19.4 0.0 copy-done
  19.4 0.0 copy-done.1
  19.4 1.0 %shard_map.113 = (bf16[110,16,128]{2,1,0:T(8,128)(2,1)}, bf16[110,16,128]{2,1,0:T(8,128)(2,1)}) custom-call(f32[3,256,128]{2,1,0:T(8,128)S(1)} %bitcast.18, f32[6,256,128]{2,1,0:T(8,128)S(1)} %bitcast.15, f32[3,256,128]{2,1,0:T(8,128)S(1)} %pad_maximum_fusion.mats), custom_call_target="tpu_custom_call" | custom-call | flops 1000000 | bytes 1000000 | tf_op jit(solution)/shard_map/pallas_call | solution.py:491
  20.5 1.9 %collective-permute-start = (bf16[110,16,128]{2,1,0:T(8,128)(2,1)}, bf16[110,16,128]{2,1,0:T(8,128)(2,1)S(1)}, u32[]{:S(2)}, u32[]{:S(2)}) collective-permute-start(bf16[110,16,128]{2,1,0:T(8,128)(2,1)} %get-tuple-element.13), channel_id=1, source_target_pairs={{0,16},{16,0},{32,48},{48,32},{64,80},{80,64},{96,112},{112,96},{1... | collective-permute-start | bytes 1351688 | tf_op jit(solution)/shard_map/ppermute | solution.py:482
  22.4 15.5 %collective-permute-start.1 = (bf16[110,16,128]{2,1,0:T(8,128)(2,1)}, bf16[110,16,128]{2,1,0:T(8,128)(2,1)}, u32[]{:S(2)}, u32[]{:S(2)}) collective-permute-start(bf16[110,16,128]{2,1,0:T(8,128)(2,1)} %get-tuple-element.14), channel_id=1, source_target_pairs={{16,32},{32,16},{48,64},{64,48},{80,96},{96,80},{112,128},{128,112... | collective-permute-start | bytes 1351688 | tf_op jit(solution)/shard_map/ppermute | solution.py:483
  37.9 0.0 all-to-all-done.lists
  37.9 0.0 collective-permute-done.2.ya
  37.9 0.0 collective-permute-done.3.yb
  37.9 0.1 shard_map.115
  38.1 1.9 %collective-permute-start.4 = (bf16[84,16,128]{2,1,0:T(8,128)(2,1)S(1)}, bf16[84,16,128]{2,1,0:T(8,128)(2,1)S(1)}, u32[]{:S(2)}, u32[]{:S(2)}) collective-permute-start(bf16[84,16,128]{2,1,0:T(8,128)(2,1)S(1)} %get-tuple-element.18), channel_id=1, source_target_pairs={{0,16},{16,0},{32,48},{48,32},{64,80},{80,64},{96,112},{112,96},{1... | collective-permute-start | bytes 1032200 | tf_op jit(solution)/shard_map/ppermute | solution.py:482
  40.0 5.1 %collective-permute-start.5 = (bf16[84,16,128]{2,1,0:T(8,128)(2,1)S(1)}, bf16[84,16,128]{2,1,0:T(8,128)(2,1)S(1)}, u32[]{:S(2)}, u32[]{:S(2)}) collective-permute-start(bf16[84,16,128]{2,1,0:T(8,128)(2,1)S(1)} %get-tuple-element.19), channel_id=1, source_target_pairs={{16,32},{32,16},{48,64},{64,48},{80,96},{96,80},{112,128},{128,112... | collective-permute-start | bytes 1032200 | tf_op jit(solution)/shard_map/ppermute | solution.py:483
  45.2 3.2 %shard_map.116 = (f32[18,256,128]{2,1,0:T(8,128)S(1)}, f32[12,128,256]{2,1,0:T(8,128)S(1)}) custom-call(bf16[16,32,128]{2,1,0:T(8,128)(2,1)S(1)} %all-to-all-done.lists), custom_call_target="tpu_custom_call" | custom-call | flops 10000000000 | bytes 1000000 | tf_op jit(solution)/shard_map/pallas_call | solution.py:491
  48.3 0.0 collective-permute-done.xa
  48.3 0.0 collective-permute-done.1.xb
  48.3 0.0 collective-permute-done.4.ca
  48.3 3.9 %collective-permute-done.5.cb = bf16[84,16,128]{2,1,0:T(8,128)(2,1)S(1)} collective-permute-done((bf16[84,16,128]{2,1,0:T(8,128)(2,1)S(1)}, bf16[84,16,128]{2,1,0:T(8,128)(2,1)S(1)}, u32[]{:S(2)}, u32[]{:S(2)}) %collective-permute-start.5) | collective-permute-done | bytes 344096 | tf_op jit(solution)/shard_map/ppermute | solution.py:483
  52.2 11.5 %shard_map.117 = (f32[3,256,128]{2,1,0:T(8,128)}, f32[6,256,128]{2,1,0:T(8,128)}) custom-call(bf16[110,16,128]{2,1,0:T(8,128)(2,1)S(1)} %collective-permute-done.xa, bf16[110,16,128]{2,1,0:T(8,128)(2,1)} %collective-permute-done.1.xb, bf16[84,16,128]{2,1,0:T(8,128)(2,1)S(1)} %collective-permute-done.4.ca, ...), custom_call_target="tpu_custom_call" | custom-call | flops 1000000 | bytes 1000000 | tf_op jit(solution)/shard_map/pallas_call | solution.py:491
Async XLA Ops:
  0.6 18.8 %copy-start = (f32[6,16,16,128]{3,2,1,0:T(8,128)S(1)}, f32[6,16,16,128]{3,2,1,0:T(8,128)}, u32[]{:S(2)}) copy-start(f32[6,16,16,128]{3,2,1,0:T(8,128)} %param.11) | copy-start | bytes 2359300
  0.6 18.8 %copy-start.1 = (f32[3,16,16,128]{3,2,1,0:T(8,128)S(1)}, f32[3,16,16,128]{3,2,1,0:T(8,128)}, u32[]{:S(2)}) copy-start(f32[3,16,16,128]{3,2,1,0:T(8,128)} %param.10) | copy-start | bytes 1179652
  4.7 33.3 %collective-permute-start.2 = (bf16[110,16,128]{2,1,0:T(8,128)(2,1)}, bf16[110,16,128]{2,1,0:T(8,128)(2,1)S(1)}, u32[]{:S(2)}, u32[]{:S(2)}) collective-permute-start(bf16[110,16,128]{2,1,0:T(8,128)(2,1)} %get-tuple-element.15), channel_id=1, source_target_pairs={{0,1},{1,0},{2,3},{3,2},{4,5},{5,4},{6,7},{7,6},{8,9},{9,8},{10,11... | collective-permute-start | bytes 1351688 | tf_op jit(solution)/shard_map/ppermute | solution.py:482
  8.2 29.8 %collective-permute-start.3 = (bf16[110,16,128]{2,1,0:T(8,128)(2,1)}, bf16[110,16,128]{2,1,0:T(8,128)(2,1)S(1)}, u32[]{:S(2)}, u32[]{:S(2)}) collective-permute-start(bf16[110,16,128]{2,1,0:T(8,128)(2,1)} %get-tuple-element.16), channel_id=1, source_target_pairs={{1,2},{2,1},{3,4},{4,3},{5,6},{6,5},{7,8},{8,7},{9,10},{10,9},{11,... | collective-permute-start | bytes 1351688 | tf_op jit(solution)/shard_map/ppermute | solution.py:483
  13.6 24.3 %all-to-all-start = ((bf16[16,32,128]{2,1,0:T(8,128)(2,1)}), bf16[16,32,128]{2,1,0:T(8,128)(2,1)S(1)}, u32[]{:S(2)}, u32[]{:S(2)}) async-start(bf16[16,32,128]{2,1,0:T(8,128)(2,1)} %get-tuple-element.17), calls=%async_computation | async-start | bytes 262144 | tf_op jit(solution)/shard_map/all_to_all | solution.py:521
  20.5 27.9 %collective-permute-start = (bf16[110,16,128]{2,1,0:T(8,128)(2,1)}, bf16[110,16,128]{2,1,0:T(8,128)(2,1)S(1)}, u32[]{:S(2)}, u32[]{:S(2)}) collective-permute-start(bf16[110,16,128]{2,1,0:T(8,128)(2,1)} %get-tuple-element.13), channel_id=1, source_target_pairs={{0,16},{16,0},{32,48},{48,32},{64,80},{80,64},{96,112},{112,96},{1... | collective-permute-start | bytes 1351688 | tf_op jit(solution)/shard_map/ppermute | solution.py:482
  22.4 26.0 %collective-permute-start.1 = (bf16[110,16,128]{2,1,0:T(8,128)(2,1)}, bf16[110,16,128]{2,1,0:T(8,128)(2,1)}, u32[]{:S(2)}, u32[]{:S(2)}) collective-permute-start(bf16[110,16,128]{2,1,0:T(8,128)(2,1)} %get-tuple-element.14), channel_id=1, source_target_pairs={{16,32},{32,16},{48,64},{64,48},{80,96},{96,80},{112,128},{128,112... | collective-permute-start | bytes 1351688 | tf_op jit(solution)/shard_map/ppermute | solution.py:483
  38.1 10.2 %collective-permute-start.4 = (bf16[84,16,128]{2,1,0:T(8,128)(2,1)S(1)}, bf16[84,16,128]{2,1,0:T(8,128)(2,1)S(1)}, u32[]{:S(2)}, u32[]{:S(2)}) collective-permute-start(bf16[84,16,128]{2,1,0:T(8,128)(2,1)S(1)} %get-tuple-element.18), channel_id=1, source_target_pairs={{0,16},{16,0},{32,48},{48,32},{64,80},{80,64},{96,112},{112,96},{1... | collective-permute-start | bytes 1032200 | tf_op jit(solution)/shard_map/ppermute | solution.py:482
  40.0 12.2 %collective-permute-start.5 = (bf16[84,16,128]{2,1,0:T(8,128)(2,1)S(1)}, bf16[84,16,128]{2,1,0:T(8,128)(2,1)S(1)}, u32[]{:S(2)}, u32[]{:S(2)}) collective-permute-start(bf16[84,16,128]{2,1,0:T(8,128)(2,1)S(1)} %get-tuple-element.19), channel_id=1, source_target_pairs={{16,32},{32,16},{48,64},{64,48},{80,96},{96,80},{112,128},{128,112... | collective-permute-start | bytes 1032200 | tf_op jit(solution)/shard_map/ppermute | solution.py:483

commit v4 on v3

--- a/solution.py
+++ b/solution.py
@@ -30,8 +30,6 @@
 CORN = [(q,) + unit for q in range(NQ) for unit in PACKED[CORNER[q]]]
 NCORN = len(CORN)
 SLOTS = 64
-UNROLL = {8: 8, 6: 7, 5: 13, 3: 11, 2: 10, 0: 8}
-FIRST = 61
 FAR = (6, 3)
 NEAR = (5, 2)
 
@@ -62,7 +60,7 @@
 
 
 def opening(groups, *refs):
-    given, (out_a, out_b, sent), held, vals, sems = refs[:10], refs[10:13], refs[13:23], refs[23], refs[24]
+    given, (out_a, out_b, sent, mats), held, vals, sems = refs[:10], refs[10:14], refs[14:24], refs[24], refs[25]
     copies = fetch(list(zip(given, held)), sems)
     for copy in copies[5:]:
         copy.wait()
@@ -70,6 +68,8 @@
     for copy in copies[:5]:
         copy.wait()
     pack_y(*held[:5], out_a, out_b)
+    for i in range(3):
+        mats[i] = held[2 + i][...]
 
 
 def pack_y(v, s, b, l, m, out_a, out_b):
@@ -158,10 +158,13 @@
     odd_x = lax.rem(lax.axis_index("gx"), 2)
     odd_y = lax.rem(lax.axis_index("gy"), 2)
     groups = lists.shape[0]
+    first, _ = own_lists(lambda g: lists[g, 16:32, :].astype(F32), groups)
+    first = first.astype(BF16)
     for out in (out_a, out_b):
         for g in range(groups):
-            for h in range(2):
-                out[NCORN + 2 * g + h] = lists[g, 16 * h : 16 * h + 16, :]
+            out[NCORN + g] = lists[g, 0:16, :]
+        for g in range(groups // 2):
+            out[NCORN + groups + g] = first[:, 128 * g : 128 * g + 128]
 
     def corners(low, top, out, high):
         row = lax.broadcasted_iota(I32, (8, Z), 0)
@@ -323,7 +326,7 @@
         return INNER * near + OUTER * far
 
     def reader(ref, x, y0, n):
-        base = pl.multiple_of(x * YE, 8)
+        base = x * YE if isinstance(x, int) else pl.multiple_of(x * YE, 8)
 
         def along_x(c):
             return lambda k: ref[c, pl.ds(base + (k * YE + y0), n), :]
@@ -366,12 +369,15 @@
         for c, r in enumerate(rates):
             es[c, here, :] = es[c, here, :] + r
 
-    def sweep(fn, reach, y0, n):
+    def sweep(fn, wide, y0, n, sides, unroll):
         def step(x, carry):
             fn(x, y0, n)
             return carry
 
-        lax.fori_loop(XO - reach, XO + N + reach, step, 0, unroll=UNROLL[reach])
+        lax.fori_loop(XO - wide, XO + N + wide, step, 0, unroll=unroll)
+        for depth, rows in sides:
+            for x in (XO - depth, XO + N - 1 + depth):
+                fn(x, YO + (N - rows) // 2, rows)
 
     def add(c, x, y, rows):
         here = slice(at(x, y), at(x, y) + rows.shape[0])
@@ -390,11 +396,11 @@
                 add(c, XO + x, YO + N, side[6 * t + c, rows, Z : 2 * Z])
 
     def place_beyond():
-        groups = (ca.shape[0] - NCORN) // 2
+        groups = (ca.shape[0] - NCORN) * 2 // 3
         base = NCORN
 
         def one(msg, up, k):
-            first, _ = own_lists(lambda g: msg[base + 2 * g + 1].astype(F32), groups)
+            first = lanes([msg[base + groups + g].astype(F32) for g in range(groups // 2)])
             plane = first[12:13, :].astype(I32)
             levels = one_hot(first[13:14, :].astype(I32), Z)
             x, y = plane // N, plane % N
@@ -405,7 +411,7 @@
 
             parts = ((faces(FAR[0]), 0), (faces(FAR[1]), 6))
             beyond[k] = place(parts, first.astype(BF16), levels)
-            sides = lanes([msg[base + 2 * g].astype(F32) for g in range(groups)])
+            sides = lanes([msg[base + g].astype(F32) for g in range(groups)])
             sx, row, levels = sided(groups, sides)
 
             def edges(near):
@@ -441,18 +447,18 @@
                     add(c, x0 + i, YO + N, corner[k, r : r + 8, Z : 2 * Z])
 
     place_beyond()
-    sweep(velocity_at, 8, 8, 32)
-    sweep(stress_at, 6, 8, 32)
+    sweep(velocity_at, 4, 8, 32, ((5, 24), (6, 24), (7, 16), (8, 16)), 8)
+    sweep(stress_at, 2, 8, 32, ((3, 24), (4, 24), (5, 24), (6, 16)), 10)
     add_own(0)
     add_side(0)
     add_beyond(0)
-    sweep(velocity_at, 5, 8, 32)
-    sweep(stress_at, 3, 13, 24)
+    sweep(velocity_at, 0, 8, 32, ((1, 24), (2, 24), (3, 24), (4, 16), (5, 16)), 8)
+    sweep(stress_at, 2, 12, 24, ((3, 16),), 10)
     add_own(1)
     add_side(1)
     add_beyond(1)
-    sweep(velocity_at, 2, 14, 24)
-    sweep(stress_at, 0, 16, 16)
+    sweep(velocity_at, 0, 12, 24, ((1, 16), (2, 16)), 8)
+    sweep(stress_at, 0, 16, 16, (), 8)
     for x in range(N):
         here = slice(at(XO + x, YO), at(XO + x, YO) + N)
         rows = slice(N * x, N * x + N)
@@ -484,13 +490,14 @@
     )
 
 
-def call(kernel, outs, args, scratch=(), flops=1_000_000, mib=8, here=True):
+def call(kernel, outs, args, scratch=(), flops=1_000_000, mib=8, here=True, keep=True):
     if not here:
         held = [pltpu.VMEM(a.shape, a.dtype) for a in args]
+        args = [pltpu.with_memory_space_constraint(a, pltpu.HBM) for a in args]
         scratch = held + list(scratch) + [pltpu.SemaphoreType.DMA((len(args),))]
     return pl.pallas_call(
         kernel,
-        out_shape=[jax.ShapeDtypeStruct(s, t) for s, t in outs],
+        out_shape=[(pltpu.VMEM if keep else jax.ShapeDtypeStruct)(s, t) for s, t in outs],
         in_specs=[vmem() if here else pl.BlockSpec(memory_space=pltpu.HBM)] * len(args),
         out_specs=[vmem()] * len(outs),
         scratch_shapes=list(scratch),
@@ -505,23 +512,21 @@
     s = stresses.reshape(6, N * N, Z)
     b, l, m = (a.reshape(N * N, Z) for a in (buoyancy, lame, rigidity))
     state = (v, s, b, l, m)
-    mats = jnp.stack([b, l, m])
-    later = (v, s, mats)
     face = ((NFACE, N, Z), BF16)
     rows = hist.shape[0]
-    ya, yb, sent = call(
+    ya, yb, sent, mats = call(
         lambda *refs: opening(groups, *refs),
-        [face, face, ((groups, 32, 128), BF16)],
+        [face, face, ((groups, 32, 128), BF16), ((3, N * N, Z), F32)],
         state + (hist, mech.T, res.T, owners.reshape(1, rows), cells.reshape(1, rows)),
         [pltpu.VMEM((32, rows), F32)],
         here=False,
-        mib=FIRST,
     )
+    later = (v, s, mats)
     ya, yb = swap_both(ya, yb, "gy")
     lists = lax.all_to_all(sent, "gy", split_axis=0, concat_axis=0, tiled=True)
     xa, xb = call(pack_x, [face, face], later)
     xa, xb = swap_both(xa, xb, "gx")
-    rest = ((NCORN + 2 * groups, N, Z), BF16)
+    rest = ((NCORN + groups + groups // 2, N, Z), BF16)
     ca, cb = call(pack_corners, [rest, rest], (ya, yb, lists))
     ca, cb = swap_both(ca, cb, "gx")
     own, side = call(
@@ -536,6 +541,7 @@
         [(v.shape, F32), (s.shape, F32)],
         (xa, xb, ca, cb, ya, yb) + later + (own, side),
         SCRATCH,
+        keep=False,
         mib=24,
     )
     return vout.reshape(velocity.shape), sout.reshape(stresses.shape)

time: 64.2 us -> 61.3 us (0.955)
  waiting for transfers between devices: 3.88 us -> 2.48 us
  Pallas kernels: 19.9 us -> 18.5 us
  starting transfers between devices: 38.1 us -> 39.2 us
  other arithmetic: 1.06 us -> 0 us
    pallas_call x5, Pallas kernels: 19.9 us -> 18.5 us  [call(): pl.pallas_call(kernel, out_shape=[(pltpu.VMEM if keep else jax.ShapeDtype...]
    ppermute x3, waiting for transfers between devices: 3.87 us -> 2.47 us  [swap_both(): lax.ppermute(b, axis, swaps(count, 1))]
    another operation x1 -> x0, other arithmetic: 1.06 us -> none  [local(): mats = jnp.stack([b, l, m])]
    ppermute x3, starting transfers between devices: 26.1 us -> 27.1 us  [swap_both(): lax.ppermute(b, axis, swaps(count, 1))]
  transfers between devices with their start and end apart: 7 -> 7, of which waited for: 1 -> 1; matrix products, arithmetic and copies ran while one was open for 2% -> 0% of each run, Pallas kernels for 7% -> 7%
where the time goes in v4:
time: 61.3 us; the launch traced here: 60.9 us
  starting transfers between devices  39.2 us (64%)
  Pallas kernels  18.5 us (30%)
  waiting for transfers between devices  2.48 us (4%)
  between operations  0.78 us (1%)
    ppermute x3, starting transfers between devices, swap_both(): lax.ppermute(b, axis, swaps(count, 1))  27.1 us
    pallas_call x5, Pallas kernels, call(): pl.pallas_call(kernel, out_shape=[(pltpu.VMEM if keep else jax.ShapeDtype...  18.5 us
    ppermute x3, starting transfers between devices, swap_both(): lax.ppermute(a, axis, swaps(count, 0))  7.31 us
    all_to_all x1, starting transfers between devices, local(): lists = lax.all_to_all(sent, 'gy', split_axis=0, concat_axis=0, tiled=True)  4.74 us
    ppermute x3, waiting for transfers between devices, swap_both(): lax.ppermute(b, axis, swaps(count, 1))  2.47 us
  transfers between devices with their start and end apart: 7, of which 1 were waited for; matrix products, arithmetic and copies ran while one was open for 0% of the time, Pallas kernels for 7%

profile of v4, /device:TPU:6, one launch (start us, length us, event | category | flops | bytes accessed | tf_op | source)
XLA Modules:
  0.0 60.9 jit_solution(8686707368882596951)
XLA Ops:
  0.6 0.0 copy-start
  0.6 0.0 copy-start.1
  0.7 4.0 %shard_map.113 = (bf16[110,16,128]{2,1,0:T(8,128)(2,1)}, bf16[110,16,128]{2,1,0:T(8,128)(2,1)}, bf16[16,32,128]{2,1,0:T(8,128)(2,1)}, f32[3,256,128]{2,1,0:T(8,128)S(1)}) custom-call(f32[3,256,128]{2,1,0:T(8,128)} %bitcast.14, f32[6,256,128]{2,1,0:T(8,128)} %bitcast.11, f32[256,128]{1,0:T(8,128)} %bitcast.17, f32[256,128]{1,0:T(8,128)} %bitcast.18, ...), custom_call_target="tpu_custom_call" | custom-call | flops 1000000 | bytes 1000000 | tf_op jit(solution)/shard_map/pallas_call | solution.py:498
  4.6 3.5 %collective-permute-start.2 = (bf16[110,16,128]{2,1,0:T(8,128)(2,1)}, bf16[110,16,128]{2,1,0:T(8,128)(2,1)S(1)}, u32[]{:S(2)}, u32[]{:S(2)}) collective-permute-start(bf16[110,16,128]{2,1,0:T(8,128)(2,1)} %get-tuple-element.17), channel_id=1, source_target_pairs={{0,1},{1,0},{2,3},{3,2},{4,5},{5,4},{6,7},{7,6},{8,9},{9,8},{10,11... | collective-permute-start | bytes 1351688 | tf_op jit(solution)/shard_map/ppermute | solution.py:488
  8.1 5.4 %collective-permute-start.3 = (bf16[110,16,128]{2,1,0:T(8,128)(2,1)}, bf16[110,16,128]{2,1,0:T(8,128)(2,1)S(1)}, u32[]{:S(2)}, u32[]{:S(2)}) collective-permute-start(bf16[110,16,128]{2,1,0:T(8,128)(2,1)} %get-tuple-element.18), channel_id=1, source_target_pairs={{1,2},{2,1},{3,4},{4,3},{5,6},{6,5},{7,8},{8,7},{9,10},{10,9},{11,... | collective-permute-start | bytes 1351688 | tf_op jit(solution)/shard_map/ppermute | solution.py:489
  13.6 4.7 %all-to-all-start = ((bf16[16,32,128]{2,1,0:T(8,128)(2,1)}), bf16[16,32,128]{2,1,0:T(8,128)(2,1)S(1)}, u32[]{:S(2)}, u32[]{:S(2)}) async-start(bf16[16,32,128]{2,1,0:T(8,128)(2,1)} %get-tuple-element.19), calls=%async_computation | async-start | bytes 262144 | tf_op jit(solution)/shard_map/all_to_all | solution.py:526
  18.3 0.0 copy-done
  18.3 0.0 copy-done.1
  18.3 1.1 %shard_map.114 = (bf16[110,16,128]{2,1,0:T(8,128)(2,1)}, bf16[110,16,128]{2,1,0:T(8,128)(2,1)}) custom-call(f32[3,256,128]{2,1,0:T(8,128)S(1)} %bitcast.15, f32[6,256,128]{2,1,0:T(8,128)S(1)} %bitcast.12, f32[3,256,128]{2,1,0:T(8,128)S(1)} %get-tuple-element.14.mats), custom_call_target="tpu_custom_call" | custom-call | flops 1000000 | bytes 1000000 | tf_op jit(solution)/shard_map/pallas_call | solution.py:498
  19.4 1.9 %collective-permute-start = (bf16[110,16,128]{2,1,0:T(8,128)(2,1)}, bf16[110,16,128]{2,1,0:T(8,128)(2,1)S(1)}, u32[]{:S(2)}, u32[]{:S(2)}) collective-permute-start(bf16[110,16,128]{2,1,0:T(8,128)(2,1)} %get-tuple-element.15), channel_id=1, source_target_pairs={{0,16},{16,0},{32,48},{48,32},{64,80},{80,64},{96,112},{112,96},{1... | collective-permute-start | bytes 1351688 | tf_op jit(solution)/shard_map/ppermute | solution.py:488
  21.3 15.5 %collective-permute-start.1 = (bf16[110,16,128]{2,1,0:T(8,128)(2,1)}, bf16[110,16,128]{2,1,0:T(8,128)(2,1)S(1)}, u32[]{:S(2)}, u32[]{:S(2)}) collective-permute-start(bf16[110,16,128]{2,1,0:T(8,128)(2,1)} %get-tuple-element.16), channel_id=1, source_target_pairs={{16,32},{32,16},{48,64},{64,48},{80,96},{96,80},{112,128},{128,112... | collective-permute-start | bytes 1351688 | tf_op jit(solution)/shard_map/ppermute | solution.py:489
  36.8 0.0 all-to-all-done.lists
  36.9 0.0 collective-permute-done.2.ya
  36.9 0.0 collective-permute-done.3.yb
  36.9 0.2 shard_map.115
  37.1 1.9 %collective-permute-start.4 = (bf16[76,16,128]{2,1,0:T(8,128)(2,1)S(1)}, bf16[76,16,128]{2,1,0:T(8,128)(2,1)S(1)}, u32[]{:S(2)}, u32[]{:S(2)}) collective-permute-start(bf16[76,16,128]{2,1,0:T(8,128)(2,1)S(1)} %get-tuple-element.20), channel_id=1, source_target_pairs={{0,16},{16,0},{32,48},{48,32},{64,80},{80,64},{96,112},{112,96},{1... | collective-permute-start | bytes 933896 | tf_op jit(solution)/shard_map/ppermute | solution.py:488
  39.0 6.2 %collective-permute-start.5 = (bf16[76,16,128]{2,1,0:T(8,128)(2,1)S(1)}, bf16[76,16,128]{2,1,0:T(8,128)(2,1)S(1)}, u32[]{:S(2)}, u32[]{:S(2)}) collective-permute-start(bf16[76,16,128]{2,1,0:T(8,128)(2,1)S(1)} %get-tuple-element.21), channel_id=1, source_target_pairs={{16,32},{32,16},{48,64},{64,48},{80,96},{96,80},{112,128},{128,112... | collective-permute-start | bytes 933896 | tf_op jit(solution)/shard_map/ppermute | solution.py:489
  45.2 3.2 %shard_map.116 = (f32[18,256,128]{2,1,0:T(8,128)S(1)}, f32[12,128,256]{2,1,0:T(8,128)S(1)}) custom-call(bf16[16,32,128]{2,1,0:T(8,128)(2,1)S(1)} %all-to-all-done.lists), custom_call_target="tpu_custom_call" | custom-call | flops 10000000000 | bytes 1000000 | tf_op jit(solution)/shard_map/pallas_call | solution.py:498
  48.3 0.0 collective-permute-done.xa
  48.3 0.0 collective-permute-done.1.xb
  48.3 0.0 collective-permute-done.4.ca
  48.4 2.5 %collective-permute-done.5.cb = bf16[76,16,128]{2,1,0:T(8,128)(2,1)S(1)} collective-permute-done((bf16[76,16,128]{2,1,0:T(8,128)(2,1)S(1)}, bf16[76,16,128]{2,1,0:T(8,128)(2,1)S(1)}, u32[]{:S(2)}, u32[]{:S(2)}) %collective-permute-start.5) | collective-permute-done | bytes 311328 | tf_op jit(solution)/shard_map/ppermute | solution.py:489
  50.8 10.1 %shard_map.117 = (f32[3,256,128]{2,1,0:T(8,128)}, f32[6,256,128]{2,1,0:T(8,128)}) custom-call(bf16[110,16,128]{2,1,0:T(8,128)(2,1)S(1)} %collective-permute-done.xa, bf16[110,16,128]{2,1,0:T(8,128)(2,1)S(1)} %collective-permute-done.1.xb, bf16[76,16,128]{2,1,0:T(8,128)(2,1)S(1)} %collective-permute-done.4.ca, ...), custom_call_target="tpu_custom_call" | custom-call | flops 1000000 | bytes 1000000 | tf_op jit(solution)/shard_map/pallas_call | solution.py:498
Async XLA Ops:
  0.6 17.7 %copy-start = (f32[6,16,16,128]{3,2,1,0:T(8,128)S(1)}, f32[6,16,16,128]{3,2,1,0:T(8,128)}, u32[]{:S(2)}) copy-start(f32[6,16,16,128]{3,2,1,0:T(8,128)} %param.11) | copy-start | bytes 2359300
  0.6 17.7 %copy-start.1 = (f32[3,16,16,128]{3,2,1,0:T(8,128)S(1)}, f32[3,16,16,128]{3,2,1,0:T(8,128)}, u32[]{:S(2)}) copy-start(f32[3,16,16,128]{3,2,1,0:T(8,128)} %param.10) | copy-start | bytes 1179652
  4.6 32.2 %collective-permute-start.2 = (bf16[110,16,128]{2,1,0:T(8,128)(2,1)}, bf16[110,16,128]{2,1,0:T(8,128)(2,1)S(1)}, u32[]{:S(2)}, u32[]{:S(2)}) collective-permute-start(bf16[110,16,128]{2,1,0:T(8,128)(2,1)} %get-tuple-element.17), channel_id=1, source_target_pairs={{0,1},{1,0},{2,3},{3,2},{4,5},{5,4},{6,7},{7,6},{8,9},{9,8},{10,11... | collective-permute-start | bytes 1351688 | tf_op jit(solution)/shard_map/ppermute | solution.py:488
  8.1 28.7 %collective-permute-start.3 = (bf16[110,16,128]{2,1,0:T(8,128)(2,1)}, bf16[110,16,128]{2,1,0:T(8,128)(2,1)S(1)}, u32[]{:S(2)}, u32[]{:S(2)}) collective-permute-start(bf16[110,16,128]{2,1,0:T(8,128)(2,1)} %get-tuple-element.18), channel_id=1, source_target_pairs={{1,2},{2,1},{3,4},{4,3},{5,6},{6,5},{7,8},{8,7},{9,10},{10,9},{11,... | collective-permute-start | bytes 1351688 | tf_op jit(solution)/shard_map/ppermute | solution.py:489
  13.6 23.3 %all-to-all-start = ((bf16[16,32,128]{2,1,0:T(8,128)(2,1)}), bf16[16,32,128]{2,1,0:T(8,128)(2,1)S(1)}, u32[]{:S(2)}, u32[]{:S(2)}) async-start(bf16[16,32,128]{2,1,0:T(8,128)(2,1)} %get-tuple-element.19), calls=%async_computation | async-start | bytes 262144 | tf_op jit(solution)/shard_map/all_to_all | solution.py:526
  19.4 28.9 %collective-permute-start = (bf16[110,16,128]{2,1,0:T(8,128)(2,1)}, bf16[110,16,128]{2,1,0:T(8,128)(2,1)S(1)}, u32[]{:S(2)}, u32[]{:S(2)}) collective-permute-start(bf16[110,16,128]{2,1,0:T(8,128)(2,1)} %get-tuple-element.15), channel_id=1, source_target_pairs={{0,16},{16,0},{32,48},{48,32},{64,80},{80,64},{96,112},{112,96},{1... | collective-permute-start | bytes 1351688 | tf_op jit(solution)/shard_map/ppermute | solution.py:488
  21.3 27.0 %collective-permute-start.1 = (bf16[110,16,128]{2,1,0:T(8,128)(2,1)}, bf16[110,16,128]{2,1,0:T(8,128)(2,1)S(1)}, u32[]{:S(2)}, u32[]{:S(2)}) collective-permute-start(bf16[110,16,128]{2,1,0:T(8,128)(2,1)} %get-tuple-element.16), channel_id=1, source_target_pairs={{16,32},{32,16},{48,64},{64,48},{80,96},{96,80},{112,128},{128,112... | collective-permute-start | bytes 1351688 | tf_op jit(solution)/shard_map/ppermute | solution.py:489
  37.1 11.3 %collective-permute-start.4 = (bf16[76,16,128]{2,1,0:T(8,128)(2,1)S(1)}, bf16[76,16,128]{2,1,0:T(8,128)(2,1)S(1)}, u32[]{:S(2)}, u32[]{:S(2)}) collective-permute-start(bf16[76,16,128]{2,1,0:T(8,128)(2,1)S(1)} %get-tuple-element.20), channel_id=1, source_target_pairs={{0,16},{16,0},{32,48},{48,32},{64,80},{80,64},{96,112},{112,96},{1... | collective-permute-start | bytes 933896 | tf_op jit(solution)/shard_map/ppermute | solution.py:488
  39.0 11.8 %collective-permute-start.5 = (bf16[76,16,128]{2,1,0:T(8,128)(2,1)S(1)}, bf16[76,16,128]{2,1,0:T(8,128)(2,1)S(1)}, u32[]{:S(2)}, u32[]{:S(2)}) collective-permute-start(bf16[76,16,128]{2,1,0:T(8,128)(2,1)S(1)} %get-tuple-element.21), channel_id=1, source_target_pairs={{16,32},{32,16},{48,64},{64,48},{80,96},{96,80},{112,128},{128,112... | collective-permute-start | bytes 933896 | tf_op jit(solution)/shard_map/ppermute | solution.py:489

commit v5 on v4

--- a/solution.py
+++ b/solution.py
@@ -30,6 +30,7 @@
 CORN = [(q,) + unit for q in range(NQ) for unit in PACKED[CORNER[q]]]
 NCORN = len(CORN)
 SLOTS = 64
+LIMIT = (24, 24)
 FAR = (6, 3)
 NEAR = (5, 2)
 
@@ -257,66 +258,7 @@
     return jnp.where(keep, moved, 0.0)
 
 
-def advance(xa, xb, ca, cb, ya, yb, v, s, mats, own, side, vout, sout, ev, es, eb, el, em, beyond, corner):
-    odd_x = lax.rem(lax.axis_index("gx"), 2)
-    odd_y = lax.rem(lax.axis_index("gy"), 2)
-    refs = (v, s, mats.at[0], mats.at[1], mats.at[2])
-    ext = (ev, es, eb, el, em)
-
-    def at(x, y):
-        return x * YE + y
-
-    for q in range(NQ):
-        src, dst = part(refs, q), part(ext, q)
-        for x in range(N):
-            dst[at(XO + x, YO) : at(XO + x, YO) + N, :] = src[N * x : N * x + N, :]
-
-    def layer(msg, q, d):
-        rows = msg[FACE_AT[q, d]].astype(F32)
-        if d == 1:
-            rows = rows + msg[LOW_AT[q]].astype(F32)
-        return rows
-
-    def put_y(low, top):
-        for q in range(NQ):
-            dst = part(ext, q)
-            for d in range(1, DEPTH[q] + 1):
-                dst[pl.ds(at(XO, YO - d), N, stride=YE), :] = layer(low, q, d)
-                dst[pl.ds(at(XO, YO + N - 1 + d), N, stride=YE), :] = layer(top, q, d)
-
-    def put_x(low, top):
-        for q in range(NQ):
-            dst = part(ext, q)
-            for d in range(1, DEPTH[q] + 1):
-                for msg, x in ((low, XO - d), (top, XO + N - 1 + d)):
-                    dst[at(x, YO) : at(x, YO) + N, :] = layer(msg, q, d)
-
-    def put_corners(low, top):
-        for i, (q, d, far, m) in enumerate(CORN):
-            dst = part(ext, q)
-            for msg, x, back in ((low, XO - 8, 8 - m), (top, XO + N, m)):
-                both = msg[i].astype(F32)
-                for h in range(2):
-                    rows = both[8 * h : 8 * h + 8]
-
-                    def put(depth, rows):
-                        y = YO + N - 1 + depth if h else YO - depth
-                        dst[pl.ds(at(x, y), 8, stride=YE), :] = rows
-
-                    put(d, rows)
-                    if far:
-                        put(far, pltpu.roll(rows, back, 0))
-
-    for odd, put, one, two in ((odd_y, put_y, ya, yb), (odd_x, put_x, xa, xb), (odd_x, put_corners, ca, cb)):
-
-        @pl.when(odd == 0)
-        def _():
-            put(two, one)
-
-        @pl.when(odd == 1)
-        def _():
-            put(one, two)
-
+def stencil(ev, es, eb, el, em):
     def total(terms):
         near = far = None
         for g, fwd in terms:
@@ -369,15 +311,95 @@
         for c, r in enumerate(rates):
             es[c, here, :] = es[c, here, :] + r
 
-    def sweep(fn, wide, y0, n, sides, unroll):
+    def sweep(fn, first, last, y0, n, unroll):
         def step(x, carry):
             fn(x, y0, n)
             return carry
 
-        lax.fori_loop(XO - wide, XO + N + wide, step, 0, unroll=unroll)
+        lax.fori_loop(XO + first, XO + last + 1, step, 0, unroll=unroll)
+
+    def strips(fn, sides):
         for depth, rows in sides:
             for x in (XO - depth, XO + N - 1 + depth):
                 fn(x, YO + (N - rows) // 2, rows)
+
+    return velocity_at, stress_at, sweep, strips
+
+
+def at(x, y):
+    return x * YE + y
+
+
+def layer(msg, q, d):
+    rows = msg[FACE_AT[q, d]].astype(F32)
+    if d == 1:
+        rows = rows + msg[LOW_AT[q]].astype(F32)
+    return rows
+
+
+def by_parity(odd, put, one, two):
+    @pl.when(odd == 0)
+    def _():
+        put(two, one)
+
+    @pl.when(odd == 1)
+    def _():
+        put(one, two)
+
+
+def prepare(lists, ya, yb, v, s, mats, out_own, out_side, ev, es, eb, el, em):
+    refs = (v, s, mats.at[0], mats.at[1], mats.at[2])
+    ext = (ev, es, eb, el, em)
+    for q in range(NQ):
+        src, dst = part(refs, q), part(ext, q)
+        for x in range(N):
+            dst[at(XO + x, YO) : at(XO + x, YO) + N, :] = src[N * x : N * x + N, :]
+
+    def put_y(low, top):
+        for q in range(NQ):
+            dst = part(ext, q)
+            for d in range(1, DEPTH[q] + 1):
+                dst[pl.ds(at(XO, YO - d), N, stride=YE), :] = layer(low, q, d)
+                dst[pl.ds(at(XO, YO + N - 1 + d), N, stride=YE), :] = layer(top, q, d)
+
+    by_parity(lax.rem(lax.axis_index("gy"), 2), put_y, ya, yb)
+    place_own(lists, out_own, out_side)
+    velocity_at, stress_at, sweep, _ = stencil(*ext)
+    sweep(velocity_at, 2, N - 3, 8, 32, 6)
+    sweep(stress_at, 4, N - 5, 8, 32, 8)
+
+
+def advance(xa, xb, ca, cb, own, side, *refs):
+    vout, sout, ev, es, eb, el, em, beyond, corner = refs[5:]
+    odd_x = lax.rem(lax.axis_index("gx"), 2)
+    ext = (ev, es, eb, el, em)
+
+    def put_x(low, top):
+        for q in range(NQ):
+            dst = part(ext, q)
+            for d in range(1, DEPTH[q] + 1):
+                for msg, x in ((low, XO - d), (top, XO + N - 1 + d)):
+                    dst[at(x, YO) : at(x, YO) + N, :] = layer(msg, q, d)
+
+    def put_corners(low, top):
+        for i, (q, d, far, m) in enumerate(CORN):
+            dst = part(ext, q)
+            for msg, x, back in ((low, XO - 8, 8 - m), (top, XO + N, m)):
+                both = msg[i].astype(F32)
+                for h in range(2):
+                    rows = both[8 * h : 8 * h + 8]
+
+                    def put(depth, rows):
+                        y = YO + N - 1 + depth if h else YO - depth
+                        dst[pl.ds(at(x, y), 8, stride=YE), :] = rows
+
+                    put(d, rows)
+                    if far:
+                        put(far, pltpu.roll(rows, back, 0))
+
+    by_parity(odd_x, put_x, xa, xb)
+    by_parity(odd_x, put_corners, ca, cb)
+    velocity_at, stress_at, sweep, strips = stencil(*ext)
 
     def add(c, x, y, rows):
         here = slice(at(x, y), at(x, y) + rows.shape[0])
@@ -447,18 +469,25 @@
                     add(c, x0 + i, YO + N, corner[k, r : r + 8, Z : 2 * Z])
 
     place_beyond()
-    sweep(velocity_at, 4, 8, 32, ((5, 24), (6, 24), (7, 16), (8, 16)), 8)
-    sweep(stress_at, 2, 8, 32, ((3, 24), (4, 24), (5, 24), (6, 16)), 10)
+    sweep(velocity_at, -4, 1, 8, 32, 6)
+    sweep(velocity_at, N - 2, N + 3, 8, 32, 6)
+    strips(velocity_at, ((5, 24), (6, 24), (7, 16), (8, 16)))
+    sweep(stress_at, -2, 3, 8, 32, 6)
+    sweep(stress_at, N - 4, N + 1, 8, 32, 6)
+    strips(stress_at, ((3, 24), (4, 24), (5, 24), (6, 16)))
     add_own(0)
     add_side(0)
     add_beyond(0)
-    sweep(velocity_at, 0, 8, 32, ((1, 24), (2, 24), (3, 24), (4, 16), (5, 16)), 8)
-    sweep(stress_at, 2, 12, 24, ((3, 16),), 10)
+    sweep(velocity_at, 0, N - 1, 8, 32, 8)
+    strips(velocity_at, ((1, 24), (2, 24), (3, 24), (4, 16), (5, 16)))
+    sweep(stress_at, -2, N + 1, 12, 24, 10)
+    strips(stress_at, ((3, 16),))
     add_own(1)
     add_side(1)
     add_beyond(1)
-    sweep(velocity_at, 0, 12, 24, ((1, 16), (2, 16)), 8)
-    sweep(stress_at, 0, 16, 16, (), 8)
+    sweep(velocity_at, 0, N - 1, 12, 24, 8)
+    strips(velocity_at, ((1, 16), (2, 16)))
+    sweep(stress_at, 0, N - 1, 16, 16, 8)
     for x in range(N):
         here = slice(at(XO + x, YO), at(XO + x, YO) + N)
         rows = slice(N * x, N * x + N)
@@ -468,8 +497,8 @@
             sout[c, rows, :] = es[c, here, :] + own[12 + c, rows, :]
 
 
-SCRATCH = [pltpu.VMEM((n, XE * YE, Z), F32) for n in (3, 6)] + [pltpu.VMEM((XE * YE, Z), F32)] * 3
-SCRATCH += [
+EXT = [((n, XE * YE, Z), F32) for n in (3, 6)] + [((XE * YE, Z), F32)] * 3
+SCRATCH = [
     pltpu.VMEM((2, 6 * N * (FAR[0] + FAR[1]), Z), F32),
     pltpu.VMEM((2, 6 * 8 * (NEAR[0] + NEAR[1]), 2 * Z), F32),
 ]
@@ -490,7 +519,7 @@
     )
 
 
-def call(kernel, outs, args, scratch=(), flops=1_000_000, mib=8, here=True, keep=True):
+def call(kernel, outs, args, scratch=(), flops=1_000_000, mib=8, here=True, keep=True, aliases=None):
     if not here:
         held = [pltpu.VMEM(a.shape, a.dtype) for a in args]
         args = [pltpu.with_memory_space_constraint(a, pltpu.HBM) for a in args]
@@ -501,6 +530,7 @@
         in_specs=[vmem() if here else pl.BlockSpec(memory_space=pltpu.HBM)] * len(args),
         out_specs=[vmem()] * len(outs),
         scratch_shapes=list(scratch),
+        input_output_aliases=aliases or {},
         compiler_params=pltpu.CompilerParams(vmem_limit_bytes=mib * 1024 * 1024),
         cost_estimate=pl.CostEstimate(flops=flops, bytes_accessed=1_000_000, transcendentals=0),
     )(*args)
@@ -529,20 +559,21 @@
     rest = ((NCORN + groups + groups // 2, N, Z), BF16)
     ca, cb = call(pack_corners, [rest, rest], (ya, yb, lists))
     ca, cb = swap_both(ca, cb, "gx")
-    own, side = call(
-        place_own,
-        [((18, N * N, Z), F32), ((12, 8 * N, 2 * Z), F32)],
-        (lists,),
+    own, side, *ext = call(
+        prepare,
+        [((18, N * N, Z), F32), ((12, 8 * N, 2 * Z), F32)] + EXT,
+        (lists, ya, yb) + later,
         flops=10_000_000_000,
-        mib=24,
+        mib=LIMIT[0],
     )
-    vout, sout = call(
+    vout, sout, *_ = call(
         advance,
-        [(v.shape, F32), (s.shape, F32)],
-        (xa, xb, ca, cb, ya, yb) + later + (own, side),
+        [(v.shape, F32), (s.shape, F32)] + EXT,
+        (xa, xb, ca, cb, own, side) + tuple(ext),
         SCRATCH,
         keep=False,
-        mib=24,
+        mib=LIMIT[1],
+        aliases={6 + i: 2 + i for i in range(5)},
     )
     return vout.reshape(velocity.shape), sout.reshape(stresses.shape)
 

time: 61.3 us -> 59.7 us (0.974)
  waiting for transfers between devices: 2.48 us -> 1.12 us
    ppermute x3, waiting for transfers between devices: 2.47 us -> 1.11 us  [swap_both(): lax.ppermute(b, axis, swaps(count, 1))]
  transfers between devices with their start and end apart: 7 -> 7, of which waited for: 1 -> 1; matrix products, arithmetic and copies ran while one was open for 0% -> 0% of each run, Pallas kernels for 7% -> 10%
where the time goes in v5:
time: 59.7 us; the launch traced here: 59.3 us
  starting transfers between devices  39.2 us (66%)
  Pallas kernels  18.2 us (30%)
  waiting for transfers between devices  1.12 us (2%)
  between operations  0.78 us (1%)
    ppermute x3, starting transfers between devices, swap_both(): lax.ppermute(b, axis, swaps(count, 1))  27.1 us
    pallas_call x5, Pallas kernels, call(): pl.pallas_call(kernel, out_shape=[(pltpu.VMEM if keep else jax.ShapeDtype...  18.2 us
    ppermute x3, starting transfers between devices, swap_both(): lax.ppermute(a, axis, swaps(count, 0))  7.31 us
    all_to_all x1, starting transfers between devices, local(): lists = lax.all_to_all(sent, 'gy', split_axis=0, concat_axis=0, tiled=True)  4.74 us
  transfers between devices with their start and end apart: 7, of which 1 were waited for; matrix products, arithmetic and copies ran while one was open for 0% of the time, Pallas kernels for 10%

profile of v5, /device:TPU:6, one launch (start us, length us, event | category | flops | bytes accessed | tf_op | source)
XLA Modules:
  0.0 59.3 jit_solution(3493544916409343754)
XLA Ops:
  0.6 0.0 copy-start
  0.6 0.0 copy-start.1
  0.7 4.0 %shard_map.113 = (bf16[110,16,128]{2,1,0:T(8,128)(2,1)}, bf16[110,16,128]{2,1,0:T(8,128)(2,1)}, bf16[16,32,128]{2,1,0:T(8,128)(2,1)}, f32[3,256,128]{2,1,0:T(8,128)S(1)}) custom-call(f32[3,256,128]{2,1,0:T(8,128)} %bitcast.14, f32[6,256,128]{2,1,0:T(8,128)} %bitcast.11, f32[256,128]{1,0:T(8,128)} %bitcast.17, f32[256,128]{1,0:T(8,128)} %bitcast.18, ...), custom_call_target="tpu_custom_call" | custom-call | flops 1000000 | bytes 1000000 | tf_op jit(solution)/shard_map/pallas_call | solution.py:527
  4.6 3.5 %collective-permute-start.2 = (bf16[110,16,128]{2,1,0:T(8,128)(2,1)}, bf16[110,16,128]{2,1,0:T(8,128)(2,1)S(1)}, u32[]{:S(2)}, u32[]{:S(2)}) collective-permute-start(bf16[110,16,128]{2,1,0:T(8,128)(2,1)} %get-tuple-element.22), channel_id=1, source_target_pairs={{0,1},{1,0},{2,3},{3,2},{4,5},{5,4},{6,7},{7,6},{8,9},{9,8},{10,11... | collective-permute-start | bytes 1351688 | tf_op jit(solution)/shard_map/ppermute | solution.py:517
  8.1 5.4 %collective-permute-start.3 = (bf16[110,16,128]{2,1,0:T(8,128)(2,1)}, bf16[110,16,128]{2,1,0:T(8,128)(2,1)S(1)}, u32[]{:S(2)}, u32[]{:S(2)}) collective-permute-start(bf16[110,16,128]{2,1,0:T(8,128)(2,1)} %get-tuple-element.23), channel_id=1, source_target_pairs={{1,2},{2,1},{3,4},{4,3},{5,6},{6,5},{7,8},{8,7},{9,10},{10,9},{11,... | collective-permute-start | bytes 1351688 | tf_op jit(solution)/shard_map/ppermute | solution.py:518
  13.6 4.7 %all-to-all-start = ((bf16[16,32,128]{2,1,0:T(8,128)(2,1)}), bf16[16,32,128]{2,1,0:T(8,128)(2,1)S(1)}, u32[]{:S(2)}, u32[]{:S(2)}) async-start(bf16[16,32,128]{2,1,0:T(8,128)(2,1)} %get-tuple-element.24), calls=%async_computation | async-start | bytes 262144 | tf_op jit(solution)/shard_map/all_to_all | solution.py:556
  18.3 0.0 copy-done
  18.3 0.0 copy-done.1
  18.3 1.1 %shard_map.114 = (bf16[110,16,128]{2,1,0:T(8,128)(2,1)}, bf16[110,16,128]{2,1,0:T(8,128)(2,1)}) custom-call(f32[3,256,128]{2,1,0:T(8,128)S(1)} %bitcast.15, f32[6,256,128]{2,1,0:T(8,128)S(1)} %bitcast.12, f32[3,256,128]{2,1,0:T(8,128)S(1)} %get-tuple-element.19.mats), custom_call_target="tpu_custom_call" | custom-call | flops 1000000 | bytes 1000000 | tf_op jit(solution)/shard_map/pallas_call | solution.py:527
  19.4 1.9 %collective-permute-start = (bf16[110,16,128]{2,1,0:T(8,128)(2,1)}, bf16[110,16,128]{2,1,0:T(8,128)(2,1)S(1)}, u32[]{:S(2)}, u32[]{:S(2)}) collective-permute-start(bf16[110,16,128]{2,1,0:T(8,128)(2,1)} %get-tuple-element.20), channel_id=1, source_target_pairs={{0,16},{16,0},{32,48},{48,32},{64,80},{80,64},{96,112},{112,96},{1... | collective-permute-start | bytes 1351688 | tf_op jit(solution)/shard_map/ppermute | solution.py:517
  21.3 15.5 %collective-permute-start.1 = (bf16[110,16,128]{2,1,0:T(8,128)(2,1)}, bf16[110,16,128]{2,1,0:T(8,128)(2,1)S(1)}, u32[]{:S(2)}, u32[]{:S(2)}) collective-permute-start(bf16[110,16,128]{2,1,0:T(8,128)(2,1)} %get-tuple-element.21), channel_id=1, source_target_pairs={{16,32},{32,16},{48,64},{64,48},{80,96},{96,80},{112,128},{128,112... | collective-permute-start | bytes 1351688 | tf_op jit(solution)/shard_map/ppermute | solution.py:518
  36.8 0.0 all-to-all-done.lists
  36.9 0.0 collective-permute-done.2.ya
  36.9 0.0 collective-permute-done.3.yb
  36.9 0.2 shard_map.115
  37.1 1.9 %collective-permute-start.4 = (bf16[76,16,128]{2,1,0:T(8,128)(2,1)S(1)}, bf16[76,16,128]{2,1,0:T(8,128)(2,1)S(1)}, u32[]{:S(2)}, u32[]{:S(2)}) collective-permute-start(bf16[76,16,128]{2,1,0:T(8,128)(2,1)S(1)} %get-tuple-element.25), channel_id=1, source_target_pairs={{0,16},{16,0},{32,48},{48,32},{64,80},{80,64},{96,112},{112,96},{1... | collective-permute-start | bytes 933896 | tf_op jit(solution)/shard_map/ppermute | solution.py:517
  39.0 6.2 %collective-permute-start.5 = (bf16[76,16,128]{2,1,0:T(8,128)(2,1)S(1)}, bf16[76,16,128]{2,1,0:T(8,128)(2,1)S(1)}, u32[]{:S(2)}, u32[]{:S(2)}) collective-permute-start(bf16[76,16,128]{2,1,0:T(8,128)(2,1)S(1)} %get-tuple-element.26), channel_id=1, source_target_pairs={{16,32},{32,16},{48,64},{64,48},{80,96},{96,80},{112,128},{128,112... | collective-permute-start | bytes 933896 | tf_op jit(solution)/shard_map/ppermute | solution.py:518
  45.2 4.5 %shard_map.116 = (f32[18,256,128]{2,1,0:T(8,128)S(1)}, f32[12,128,256]{2,1,0:T(8,128)S(1)}, f32[3,1480,128]{2,1,0:T(8,128)S(1)}, f32[6,1480,128]{2,1,0:T(8,128)S...) custom-call(bf16[16,32,128]{2,1,0:T(8,128)(2,1)S(1)} %all-to-all-done.lists, ...), custom_call_target="tpu_custom_call" | custom-call | flops 10000000000 | bytes 1000000 | tf_op jit(solution)/shard_map/pallas_call | solution.py:527
  49.7 0.0 collective-permute-done.xa
  49.7 0.0 collective-permute-done.1.xb
  49.7 0.0 collective-permute-done.4.ca
  49.7 1.1 %collective-permute-done.5.cb = bf16[76,16,128]{2,1,0:T(8,128)(2,1)S(1)} collective-permute-done((bf16[76,16,128]{2,1,0:T(8,128)(2,1)S(1)}, bf16[76,16,128]{2,1,0:T(8,128)(2,1)S(1)}, u32[]{:S(2)}, u32[]{:S(2)}) %collective-permute-start.5) | collective-permute-done | bytes 311328 | tf_op jit(solution)/shard_map/ppermute | solution.py:518
  50.8 8.5 %shard_map.117 = (f32[3,256,128]{2,1,0:T(8,128)}, f32[6,256,128]{2,1,0:T(8,128)}, f32[3,1480,128]{2,1,0:T(8,128)S(1)}, f32[6,1480,128]{2,1,0:T(8,128)S(1)}, f32[...) custom-call(bf16[110,16,128]{2,1,0:T(8,128)(2,1)S(1)} %collective-pe, ...), custom_call_target="tpu_custom_call", output_to_operand_aliasing={{2}: (6, {}), {3}: (7, {}), {4}: (8, {}), {5}: (9, {}), {6}... | custom-call | flops 1000000 | bytes 1000000 | tf_op jit(solution)/shard_map/pallas_call | solution.py:527
Async XLA Ops:
  0.6 17.7 %copy-start = (f32[6,16,16,128]{3,2,1,0:T(8,128)S(1)}, f32[6,16,16,128]{3,2,1,0:T(8,128)}, u32[]{:S(2)}) copy-start(f32[6,16,16,128]{3,2,1,0:T(8,128)} %param.11) | copy-start | bytes 2359300
  0.6 17.7 %copy-start.1 = (f32[3,16,16,128]{3,2,1,0:T(8,128)S(1)}, f32[3,16,16,128]{3,2,1,0:T(8,128)}, u32[]{:S(2)}) copy-start(f32[3,16,16,128]{3,2,1,0:T(8,128)} %param.10) | copy-start | bytes 1179652
  4.6 32.2 %collective-permute-start.2 = (bf16[110,16,128]{2,1,0:T(8,128)(2,1)}, bf16[110,16,128]{2,1,0:T(8,128)(2,1)S(1)}, u32[]{:S(2)}, u32[]{:S(2)}) collective-permute-start(bf16[110,16,128]{2,1,0:T(8,128)(2,1)} %get-tuple-element.22), channel_id=1, source_target_pairs={{0,1},{1,0},{2,3},{3,2},{4,5},{5,4},{6,7},{7,6},{8,9},{9,8},{10,11... | collective-permute-start | bytes 1351688 | tf_op jit(solution)/shard_map/ppermute | solution.py:517
  8.1 28.7 %collective-permute-start.3 = (bf16[110,16,128]{2,1,0:T(8,128)(2,1)}, bf16[110,16,128]{2,1,0:T(8,128)(2,1)S(1)}, u32[]{:S(2)}, u32[]{:S(2)}) collective-permute-start(bf16[110,16,128]{2,1,0:T(8,128)(2,1)} %get-tuple-element.23), channel_id=1, source_target_pairs={{1,2},{2,1},{3,4},{4,3},{5,6},{6,5},{7,8},{8,7},{9,10},{10,9},{11,... | collective-permute-start | bytes 1351688 | tf_op jit(solution)/shard_map/ppermute | solution.py:518
  13.6 23.3 %all-to-all-start = ((bf16[16,32,128]{2,1,0:T(8,128)(2,1)}), bf16[16,32,128]{2,1,0:T(8,128)(2,1)S(1)}, u32[]{:S(2)}, u32[]{:S(2)}) async-start(bf16[16,32,128]{2,1,0:T(8,128)(2,1)} %get-tuple-element.24), calls=%async_computation | async-start | bytes 262144 | tf_op jit(solution)/shard_map/all_to_all | solution.py:556
  19.4 30.3 %collective-permute-start = (bf16[110,16,128]{2,1,0:T(8,128)(2,1)}, bf16[110,16,128]{2,1,0:T(8,128)(2,1)S(1)}, u32[]{:S(2)}, u32[]{:S(2)}) collective-permute-start(bf16[110,16,128]{2,1,0:T(8,128)(2,1)} %get-tuple-element.20), channel_id=1, source_target_pairs={{0,16},{16,0},{32,48},{48,32},{64,80},{80,64},{96,112},{112,96},{1... | collective-permute-start | bytes 1351688 | tf_op jit(solution)/shard_map/ppermute | solution.py:517
  21.3 28.4 %collective-permute-start.1 = (bf16[110,16,128]{2,1,0:T(8,128)(2,1)}, bf16[110,16,128]{2,1,0:T(8,128)(2,1)S(1)}, u32[]{:S(2)}, u32[]{:S(2)}) collective-permute-start(bf16[110,16,128]{2,1,0:T(8,128)(2,1)} %get-tuple-element.21), channel_id=1, source_target_pairs={{16,32},{32,16},{48,64},{64,48},{80,96},{96,80},{112,128},{128,112... | collective-permute-start | bytes 1351688 | tf_op jit(solution)/shard_map/ppermute | solution.py:518
  37.1 12.7 %collective-permute-start.4 = (bf16[76,16,128]{2,1,0:T(8,128)(2,1)S(1)}, bf16[76,16,128]{2,1,0:T(8,128)(2,1)S(1)}, u32[]{:S(2)}, u32[]{:S(2)}) collective-permute-start(bf16[76,16,128]{2,1,0:T(8,128)(2,1)S(1)} %get-tuple-element.25), channel_id=1, source_target_pairs={{0,16},{16,0},{32,48},{48,32},{64,80},{80,64},{96,112},{112,96},{1... | collective-permute-start | bytes 933896 | tf_op jit(solution)/shard_map/ppermute | solution.py:517
  39.0 11.8 %collective-permute-start.5 = (bf16[76,16,128]{2,1,0:T(8,128)(2,1)S(1)}, bf16[76,16,128]{2,1,0:T(8,128)(2,1)S(1)}, u32[]{:S(2)}, u32[]{:S(2)}) collective-permute-start(bf16[76,16,128]{2,1,0:T(8,128)(2,1)S(1)} %get-tuple-element.26), channel_id=1, source_target_pairs={{16,32},{32,16},{48,64},{64,48},{80,96},{96,80},{112,128},{128,112... | collective-permute-start | bytes 933896 | tf_op jit(solution)/shard_map/ppermute | solution.py:518

commit v6 on v5

--- a/solution.py
+++ b/solution.py
@@ -30,6 +30,7 @@
 CORN = [(q,) + unit for q in range(NQ) for unit in PACKED[CORNER[q]]]
 NCORN = len(CORN)
 SLOTS = 64
+FLOPS = 1_000_000
 LIMIT = (24, 24)
 FAR = (6, 3)
 NEAR = (5, 2)
@@ -347,6 +348,30 @@
         put(one, two)
 
 
+def place_beyond(msg, up, beyond, corner, k):
+    groups = (msg.shape[0] - NCORN) * 2 // 3
+    first = lanes([msg[NCORN + groups + g].astype(F32) for g in range(groups // 2)])
+    plane = first[12:13, :].astype(I32)
+    levels = one_hot(first[13:14, :].astype(I32), Z)
+    x, y = plane // N, plane % N
+
+    def faces(far):
+        i = x - jnp.where(up, 0, N - far)
+        return one_hot(jnp.where(i >= 0, i * N + y, -1), far * N)
+
+    parts = ((faces(FAR[0]), 0), (faces(FAR[1]), 6))
+    beyond[k] = place(parts, first.astype(BF16), levels)
+    sides = lanes([msg[NCORN + g].astype(F32) for g in range(groups)])
+    sx, row, levels = sided(groups, sides)
+
+    def edges(near):
+        i = sx - jnp.where(up, 0, N - near)
+        return one_hot(jnp.where(i >= 0, i * 8 + row, -1), 8 * near)
+
+    parts = ((edges(NEAR[0]), 0), (edges(NEAR[1]), 6))
+    corner[k] = place(parts, sides.astype(BF16), levels)
+
+
 def prepare(lists, ya, yb, v, s, mats, out_own, out_side, ev, es, eb, el, em):
     refs = (v, s, mats.at[0], mats.at[1], mats.at[2])
     ext = (ev, es, eb, el, em)
@@ -369,8 +394,12 @@
     sweep(stress_at, 4, N - 5, 8, 32, 8)
 
 
+def beside(ca, beyond, corner):
+    place_beyond(ca, lax.rem(lax.axis_index("gx"), 2) == 0, beyond, corner, 0)
+
+
 def advance(xa, xb, ca, cb, own, side, *refs):
-    vout, sout, ev, es, eb, el, em, beyond, corner = refs[5:]
+    vout, sout, ev, es, eb, el, em, beyond, corner = refs[7:]
     odd_x = lax.rem(lax.axis_index("gx"), 2)
     ext = (ev, es, eb, el, em)
 
@@ -417,58 +446,23 @@
                 add(c, XO + x, YO - 8, side[6 * t + c, rows, 0:Z])
                 add(c, XO + x, YO + N, side[6 * t + c, rows, Z : 2 * Z])
 
-    def place_beyond():
-        groups = (ca.shape[0] - NCORN) * 2 // 3
-        base = NCORN
-
-        def one(msg, up, k):
-            first = lanes([msg[base + groups + g].astype(F32) for g in range(groups // 2)])
-            plane = first[12:13, :].astype(I32)
-            levels = one_hot(first[13:14, :].astype(I32), Z)
-            x, y = plane // N, plane % N
-
-            def faces(far):
-                i = x if up else x - (N - far)
-                return one_hot(jnp.where(i >= 0, i * N + y, -1), far * N)
-
-            parts = ((faces(FAR[0]), 0), (faces(FAR[1]), 6))
-            beyond[k] = place(parts, first.astype(BF16), levels)
-            sides = lanes([msg[base + g].astype(F32) for g in range(groups)])
-            sx, row, levels = sided(groups, sides)
-
-            def edges(near):
-                i = sx if up else sx - (N - near)
-                return one_hot(jnp.where(i >= 0, i * 8 + row, -1), 8 * near)
-
-            parts = ((edges(NEAR[0]), 0), (edges(NEAR[1]), 6))
-            corner[k] = place(parts, sides.astype(BF16), levels)
-
-        @pl.when(odd_x == 0)
-        def _():
-            one(cb, False, 0)
-            one(ca, True, 1)
-
-        @pl.when(odd_x == 1)
-        def _():
-            one(ca, False, 0)
-            one(cb, True, 1)
-
     def add_beyond(t):
         far, near = FAR[t], NEAR[t]
         f0, n0 = (0, 0) if t == 0 else (6 * N * FAR[0], 6 * 8 * NEAR[0])
         for k in range(2):
+            slot = jnp.where(odd_x == 1, k, 1 - k)
             for c in range(6):
                 x0 = XO + N if k else XO - far
                 for i in range(far):
                     r = f0 + N * (c * far + i)
-                    add(c, x0 + i, YO, beyond[k, r : r + N, :])
+                    add(c, x0 + i, YO, beyond[slot, r : r + N, :])
                 x0 = XO + N if k else XO - near
                 for i in range(near):
                     r = n0 + 8 * (c * near + i)
-                    add(c, x0 + i, YO - 8, corner[k, r : r + 8, 0:Z])
-                    add(c, x0 + i, YO + N, corner[k, r : r + 8, Z : 2 * Z])
-
-    place_beyond()
+                    add(c, x0 + i, YO - 8, corner[slot, r : r + 8, 0:Z])
+                    add(c, x0 + i, YO + N, corner[slot, r : r + 8, Z : 2 * Z])
+
+    place_beyond(cb, odd_x == 1, beyond, corner, 1)
     sweep(velocity_at, -4, 1, 8, 32, 6)
     sweep(velocity_at, N - 2, N + 3, 8, 32, 6)
     strips(velocity_at, ((5, 24), (6, 24), (7, 16), (8, 16)))
@@ -498,9 +492,9 @@
 
 
 EXT = [((n, XE * YE, Z), F32) for n in (3, 6)] + [((XE * YE, Z), F32)] * 3
-SCRATCH = [
-    pltpu.VMEM((2, 6 * N * (FAR[0] + FAR[1]), Z), F32),
-    pltpu.VMEM((2, 6 * 8 * (NEAR[0] + NEAR[1]), 2 * Z), F32),
+BEYOND = [
+    ((2, 6 * N * (FAR[0] + FAR[1]), Z), F32),
+    ((2, 6 * 8 * (NEAR[0] + NEAR[1]), 2 * Z), F32),
 ]
 
 
@@ -566,14 +560,14 @@
         flops=10_000_000_000,
         mib=LIMIT[0],
     )
+    ext += call(beside, BEYOND, (ca,), flops=FLOPS, mib=16)
     vout, sout, *_ = call(
         advance,
-        [(v.shape, F32), (s.shape, F32)] + EXT,
+        [(v.shape, F32), (s.shape, F32)] + EXT + BEYOND,
         (xa, xb, ca, cb, own, side) + tuple(ext),
-        SCRATCH,
         keep=False,
         mib=LIMIT[1],
-        aliases={6 + i: 2 + i for i in range(5)},
+        aliases={6 + i: 2 + i for i in range(len(EXT + BEYOND))},
     )
     return vout.reshape(velocity.shape), sout.reshape(stresses.shape)
 

time: 59.7 us -> 58.6 us (0.982)
  waiting for transfers between devices: 1.12 us -> 0.07 us
    ppermute x3, waiting for transfers between devices: 1.11 us -> 0.06 us  [swap_both(): lax.ppermute(b, axis, swaps(count, 1))]
    pallas_call x5 -> x6, Pallas kernels: 18.2 us -> 18.2 us  [call(): pl.pallas_call(kernel, out_shape=[(pltpu.VMEM if keep else jax.ShapeDtype...]
  transfers between devices with their start and end apart: 7 -> 7, of which waited for: 1 -> 1; matrix products, arithmetic and copies ran while one was open for 0% -> 0% of each run, Pallas kernels for 10% -> 12%
where the time goes in v6:
time: 58.6 us; the launch traced here: 58.2 us
  starting transfers between devices  39.2 us (67%)
  Pallas kernels  18.2 us (31%)
  between operations  0.79 us (1%)
    ppermute x3, starting transfers between devices, swap_both(): lax.ppermute(b, axis, swaps(count, 1))  27.1 us
    pallas_call x6, Pallas kernels, call(): pl.pallas_call(kernel, out_shape=[(pltpu.VMEM if keep else jax.ShapeDtype...  18.2 us
    ppermute x3, starting transfers between devices, swap_both(): lax.ppermute(a, axis, swaps(count, 0))  7.31 us
    all_to_all x1, starting transfers between devices, local(): lists = lax.all_to_all(sent, 'gy', split_axis=0, concat_axis=0, tiled=True)  4.74 us
  transfers between devices with their start and end apart: 7, of which 1 were waited for; matrix products, arithmetic and copies ran while one was open for 0% of the time, Pallas kernels for 12%

profile of v6, /device:TPU:6, one launch (start us, length us, event | category | flops | bytes accessed | tf_op | source)
XLA Modules:
  0.0 58.2 jit_solution(16934042499194834977)
XLA Ops:
  0.6 0.0 copy-start
  0.6 0.0 copy-start.1
  0.7 4.0 %shard_map.113 = (bf16[110,16,128]{2,1,0:T(8,128)(2,1)}, bf16[110,16,128]{2,1,0:T(8,128)(2,1)}, bf16[16,32,128]{2,1,0:T(8,128)(2,1)}, f32[3,256,128]{2,1,0:T(8,128)S(1)}) custom-call(f32[3,256,128]{2,1,0:T(8,128)} %bitcast.14, f32[6,256,128]{2,1,0:T(8,128)} %bitcast.11, f32[256,128]{1,0:T(8,128)} %bitcast.17, f32[256,128]{1,0:T(8,128)} %bitcast.18, ...), custom_call_target="tpu_custom_call" | custom-call | flops 1000000 | bytes 1000000 | tf_op jit(solution)/shard_map/pallas_call | solution.py:521
  4.6 3.5 %collective-permute-start.2 = (bf16[110,16,128]{2,1,0:T(8,128)(2,1)}, bf16[110,16,128]{2,1,0:T(8,128)(2,1)S(1)}, u32[]{:S(2)}, u32[]{:S(2)}) collective-permute-start(bf16[110,16,128]{2,1,0:T(8,128)(2,1)} %get-tuple-element.24), channel_id=1, source_target_pairs={{0,1},{1,0},{2,3},{3,2},{4,5},{5,4},{6,7},{7,6},{8,9},{9,8},{10,11... | collective-permute-start | bytes 1351688 | tf_op jit(solution)/shard_map/ppermute | solution.py:511
  8.1 5.4 %collective-permute-start.3 = (bf16[110,16,128]{2,1,0:T(8,128)(2,1)}, bf16[110,16,128]{2,1,0:T(8,128)(2,1)S(1)}, u32[]{:S(2)}, u32[]{:S(2)}) collective-permute-start(bf16[110,16,128]{2,1,0:T(8,128)(2,1)} %get-tuple-element.25), channel_id=1, source_target_pairs={{1,2},{2,1},{3,4},{4,3},{5,6},{6,5},{7,8},{8,7},{9,10},{10,9},{11,... | collective-permute-start | bytes 1351688 | tf_op jit(solution)/shard_map/ppermute | solution.py:512
  13.6 4.7 %all-to-all-start = ((bf16[16,32,128]{2,1,0:T(8,128)(2,1)}), bf16[16,32,128]{2,1,0:T(8,128)(2,1)S(1)}, u32[]{:S(2)}, u32[]{:S(2)}) async-start(bf16[16,32,128]{2,1,0:T(8,128)(2,1)} %get-tuple-element.26), calls=%async_computation | async-start | bytes 262144 | tf_op jit(solution)/shard_map/all_to_all | solution.py:550
  18.3 0.0 copy-done
  18.3 0.0 copy-done.1
  18.3 1.1 %shard_map.114 = (bf16[110,16,128]{2,1,0:T(8,128)(2,1)}, bf16[110,16,128]{2,1,0:T(8,128)(2,1)}) custom-call(f32[3,256,128]{2,1,0:T(8,128)S(1)} %bitcast.15, f32[6,256,128]{2,1,0:T(8,128)S(1)} %bitcast.12, f32[3,256,128]{2,1,0:T(8,128)S(1)} %get-tuple-element.21.mats), custom_call_target="tpu_custom_call" | custom-call | flops 1000000 | bytes 1000000 | tf_op jit(solution)/shard_map/pallas_call | solution.py:521
  19.4 1.9 %collective-permute-start = (bf16[110,16,128]{2,1,0:T(8,128)(2,1)}, bf16[110,16,128]{2,1,0:T(8,128)(2,1)S(1)}, u32[]{:S(2)}, u32[]{:S(2)}) collective-permute-start(bf16[110,16,128]{2,1,0:T(8,128)(2,1)} %get-tuple-element.22), channel_id=1, source_target_pairs={{0,16},{16,0},{32,48},{48,32},{64,80},{80,64},{96,112},{112,96},{1... | collective-permute-start | bytes 1351688 | tf_op jit(solution)/shard_map/ppermute | solution.py:511
  21.3 15.5 %collective-permute-start.1 = (bf16[110,16,128]{2,1,0:T(8,128)(2,1)}, bf16[110,16,128]{2,1,0:T(8,128)(2,1)S(1)}, u32[]{:S(2)}, u32[]{:S(2)}) collective-permute-start(bf16[110,16,128]{2,1,0:T(8,128)(2,1)} %get-tuple-element.23), channel_id=1, source_target_pairs={{16,32},{32,16},{48,64},{64,48},{80,96},{96,80},{112,128},{128,112... | collective-permute-start | bytes 1351688 | tf_op jit(solution)/shard_map/ppermute | solution.py:512
  36.8 0.0 all-to-all-done.lists
  36.8 0.0 collective-permute-done.2.ya
  36.9 0.0 collective-permute-done.3.yb
  36.9 0.2 shard_map.115
  37.1 1.9 %collective-permute-start.4 = (bf16[76,16,128]{2,1,0:T(8,128)(2,1)S(1)}, bf16[76,16,128]{2,1,0:T(8,128)(2,1)S(1)}, u32[]{:S(2)}, u32[]{:S(2)}) collective-permute-start(bf16[76,16,128]{2,1,0:T(8,128)(2,1)S(1)} %get-tuple-element.27), channel_id=1, source_target_pairs={{0,16},{16,0},{32,48},{48,32},{64,80},{80,64},{96,112},{112,96},{1... | collective-permute-start | bytes 933896 | tf_op jit(solution)/shard_map/ppermute | solution.py:511
  39.0 6.2 %collective-permute-start.5 = (bf16[76,16,128]{2,1,0:T(8,128)(2,1)S(1)}, bf16[76,16,128]{2,1,0:T(8,128)(2,1)S(1)}, u32[]{:S(2)}, u32[]{:S(2)}) collective-permute-start(bf16[76,16,128]{2,1,0:T(8,128)(2,1)S(1)} %get-tuple-element.28), channel_id=1, source_target_pairs={{16,32},{32,16},{48,64},{64,48},{80,96},{96,80},{112,128},{128,112... | collective-permute-start | bytes 933896 | tf_op jit(solution)/shard_map/ppermute | solution.py:512
  45.2 4.5 %shard_map.116 = (f32[18,256,128]{2,1,0:T(8,128)S(1)}, f32[12,128,256]{2,1,0:T(8,128)S(1)}, f32[3,1480,128]{2,1,0:T(8,128)S(1)}, f32[6,1480,128]{2,1,0:T(8,128)S...) custom-call(bf16[16,32,128]{2,1,0:T(8,128)(2,1)S(1)} %all-to-all-done.lists, ...), custom_call_target="tpu_custom_call" | custom-call | flops 10000000000 | bytes 1000000 | tf_op jit(solution)/shard_map/pallas_call | solution.py:521
  49.7 0.0 collective-permute-done.4.ca
  49.7 1.0 %shard_map.117 = (f32[2,864,128]{2,1,0:T(8,128)S(1)}, f32[2,336,256]{2,1,0:T(8,128)S(1)}) custom-call(bf16[76,16,128]{2,1,0:T(8,128)(2,1)S(1)} %collective-permute-done.4.ca), custom_call_target="tpu_custom_call" | custom-call | flops 1000000 | bytes 1000000 | tf_op jit(solution)/shard_map/pallas_call | solution.py:521
  50.7 0.0 collective-permute-done.xa
  50.7 0.0 collective-permute-done.1.xb
  50.8 0.1 collective-permute-done.5.cb
  50.8 7.4 %shard_map.118 = (f32[3,256,128]{2,1,0:T(8,128)}, f32[6,256,128]{2,1,0:T(8,128)}, f32[3,1480,128]{2,1,0:T(8,128)S(1)}, f32[6,1480,128]{2,1,0:T(8,128)S(1)}, f32[...) custom-call(bf16[110,16,128]{2,1,0:T(8,128)(2,1)S(1)} %collective-pe, ...), custom_call_target="tpu_custom_call", output_to_operand_aliasing={{2}: (6, {}), {3}: (7, {}), {4}: (8, {}), {5}: (9, {}), {6}... | custom-call | flops 1000000 | bytes 1000000 | tf_op jit(solution)/shard_map/pallas_call | solution.py:521
Async XLA Ops:
  0.6 17.7 %copy-start = (f32[6,16,16,128]{3,2,1,0:T(8,128)S(1)}, f32[6,16,16,128]{3,2,1,0:T(8,128)}, u32[]{:S(2)}) copy-start(f32[6,16,16,128]{3,2,1,0:T(8,128)} %param.11) | copy-start | bytes 2359300
  0.6 17.7 %copy-start.1 = (f32[3,16,16,128]{3,2,1,0:T(8,128)S(1)}, f32[3,16,16,128]{3,2,1,0:T(8,128)}, u32[]{:S(2)}) copy-start(f32[3,16,16,128]{3,2,1,0:T(8,128)} %param.10) | copy-start | bytes 1179652
  4.6 32.2 %collective-permute-start.2 = (bf16[110,16,128]{2,1,0:T(8,128)(2,1)}, bf16[110,16,128]{2,1,0:T(8,128)(2,1)S(1)}, u32[]{:S(2)}, u32[]{:S(2)}) collective-permute-start(bf16[110,16,128]{2,1,0:T(8,128)(2,1)} %get-tuple-element.24), channel_id=1, source_target_pairs={{0,1},{1,0},{2,3},{3,2},{4,5},{5,4},{6,7},{7,6},{8,9},{9,8},{10,11... | collective-permute-start | bytes 1351688 | tf_op jit(solution)/shard_map/ppermute | solution.py:511
  8.1 28.7 %collective-permute-start.3 = (bf16[110,16,128]{2,1,0:T(8,128)(2,1)}, bf16[110,16,128]{2,1,0:T(8,128)(2,1)S(1)}, u32[]{:S(2)}, u32[]{:S(2)}) collective-permute-start(bf16[110,16,128]{2,1,0:T(8,128)(2,1)} %get-tuple-element.25), channel_id=1, source_target_pairs={{1,2},{2,1},{3,4},{4,3},{5,6},{6,5},{7,8},{8,7},{9,10},{10,9},{11,... | collective-permute-start | bytes 1351688 | tf_op jit(solution)/shard_map/ppermute | solution.py:512
  13.6 23.3 %all-to-all-start = ((bf16[16,32,128]{2,1,0:T(8,128)(2,1)}), bf16[16,32,128]{2,1,0:T(8,128)(2,1)S(1)}, u32[]{:S(2)}, u32[]{:S(2)}) async-start(bf16[16,32,128]{2,1,0:T(8,128)(2,1)} %get-tuple-element.26), calls=%async_computation | async-start | bytes 262144 | tf_op jit(solution)/shard_map/all_to_all | solution.py:550
  19.4 31.4 %collective-permute-start = (bf16[110,16,128]{2,1,0:T(8,128)(2,1)}, bf16[110,16,128]{2,1,0:T(8,128)(2,1)S(1)}, u32[]{:S(2)}, u32[]{:S(2)}) collective-permute-start(bf16[110,16,128]{2,1,0:T(8,128)(2,1)} %get-tuple-element.22), channel_id=1, source_target_pairs={{0,16},{16,0},{32,48},{48,32},{64,80},{80,64},{96,112},{112,96},{1... | collective-permute-start | bytes 1351688 | tf_op jit(solution)/shard_map/ppermute | solution.py:511
  21.3 29.5 %collective-permute-start.1 = (bf16[110,16,128]{2,1,0:T(8,128)(2,1)}, bf16[110,16,128]{2,1,0:T(8,128)(2,1)S(1)}, u32[]{:S(2)}, u32[]{:S(2)}) collective-permute-start(bf16[110,16,128]{2,1,0:T(8,128)(2,1)} %get-tuple-element.23), channel_id=1, source_target_pairs={{16,32},{32,16},{48,64},{64,48},{80,96},{96,80},{112,128},{128,112... | collective-permute-start | bytes 1351688 | tf_op jit(solution)/shard_map/ppermute | solution.py:512
  37.1 12.6 %collective-permute-start.4 = (bf16[76,16,128]{2,1,0:T(8,128)(2,1)S(1)}, bf16[76,16,128]{2,1,0:T(8,128)(2,1)S(1)}, u32[]{:S(2)}, u32[]{:S(2)}) collective-permute-start(bf16[76,16,128]{2,1,0:T(8,128)(2,1)S(1)} %get-tuple-element.27), channel_id=1, source_target_pairs={{0,16},{16,0},{32,48},{48,32},{64,80},{80,64},{96,112},{112,96},{1... | collective-permute-start | bytes 933896 | tf_op jit(solution)/shard_map/ppermute | solution.py:511
  39.0 11.8 %collective-permute-start.5 = (bf16[76,16,128]{2,1,0:T(8,128)(2,1)S(1)}, bf16[76,16,128]{2,1,0:T(8,128)(2,1)S(1)}, u32[]{:S(2)}, u32[]{:S(2)}) collective-permute-start(bf16[76,16,128]{2,1,0:T(8,128)(2,1)S(1)} %get-tuple-element.28), channel_id=1, source_target_pairs={{16,32},{32,16},{48,64},{64,48},{80,96},{96,80},{112,128},{128,112... | collective-permute-start | bytes 933896 | tf_op jit(solution)/shard_map/ppermute | solution.py:512
